TPU v7x, 128 devices: a whole 4x4x4 slice. The times are simulated.
128 devices in a mesh: bx: 16 (over z, x), by: 8 (over y, core).
Axes of the slice: x: 4, y: 4, z: 4, core: 2. Of those that a mesh axis runs over, the one named last changes fastest.
Arguments:
- layer_temps: float32 [40, 1024, 4096], P(None, 'by', 'bx'), may hold values from -12 to -2
- ice_thick: float32 [5, 1024, 4096], P(None, 'by', 'bx'), may hold values from 0.5 to 3
- snow_thick: float32 [5, 1024, 4096], P(None, 'by', 'bx'), may hold values from 0.05 to 0.5
- ice_area: float32 [5, 1024, 4096], P(None, 'by', 'bx'), may hold values from 0.12 to 0.2
- air_temp: float32 [1024, 4096], P('by', 'bx'), may hold values from -30 to -5
- ocean_heat: float32 [1024, 4096], P('by', 'bx'), may hold values from 0 to 300
- velocity: float32 [2, 1024, 4096], P(None, 'by', 'bx'), may hold values from -3 to 3
- stress: float32 [3, 1024, 4096], P(None, 'by', 'bx'), may hold values from -2 to 2
- wind_stress: float32 [2, 1024, 4096], P(None, 'by', 'bx'), may hold values from -5 to 5
- ocean_current: float32 [2, 1024, 4096], P(None, 'by', 'bx'), may hold values from -2 to 2
- ocean_mask: int32 [1024, 4096], P('by', 'bx'), may hold values 0 or 1
- ice_cols: int32 [8, 16, 6144], P('by', 'bx'), may hold values from -1 to 32767, as said below
Outputs:
- layer_temps_new: float32 [40, 1024, 4096], P(None, 'by', 'bx')
- ice_thick_new: float32 [5, 1024, 4096], P(None, 'by', 'bx')
- velocity_new: float32 [2, 1024, 4096], P(None, 'by', 'bx')
- stress_new: float32 [3, 1024, 4096], P(None, 'by', 'bx')
Inputs may be any that keep to these rules, and one draw needn't show every extreme that they name: `ice_cols`: each block's 6144 slots list its ice-covered cells first, each cell once, as e = row * 256 + column inside the block, and hold -1 in every later slot. All blocks together list exactly 2048 times the number of blocks cells, and some block lists 6144 cells.
All inputs are finite; a program needn't handle non-finite values. No bound on the sum of `ocean_mask` on one device may be relied on, other than what follows from the above.
Results may differ from a plain program's by a relative error of at most 0.0001.
Values sent between devices are 32-bit elements; how exact they have to be, the bound alone decides.
No kernel may reach another device: no remote copies, remote signals or barrier semaphores. Data moves between devices by JAX's collectives and lax.ppermute only.
A program may use at most 192 MiB of HBM per device.

v0:
```python
import jax
import jax.numpy as jnp
from jax import lax
from jax.sharding import PartitionSpec as P

ITERS = 4
SUB = 4


FREEZING = -1.8
THERMO_STEP = 0.1
AIR_EXCHANGE = 20.0
GROWTH_RATE = 0.0005
RELAX = 0.5
DRAG = 1.0
DENSITY = 0.9
HARDENING = 20.0


def with_halo(x, sides, width, wrap):
    for axis, dim in sides:
        peers, length = (lax.axis_size(axis), x.shape[dim])
        up = [(i, (i + 1) % peers) for i in range(peers if wrap else peers - 1)]
        down = [(j, i) for i, j in up]
        last = lax.slice_in_dim(x, length - width, length, axis=dim)
        first = lax.slice_in_dim(x, 0, width, axis=dim)
        before = lax.ppermute(last, axis, up)
        after = lax.ppermute(first, axis, down)
        x = jnp.concatenate([before, x, after], axis=dim)
    return x


def partner(x, axis, distance):
    return lax.ppermute(x, axis, [(i, i ^ 1 << distance) for i in range(lax.axis_size(axis))])


def solve_layers(diagonal, coupling, right_side):
    ratios = [coupling[0] / diagonal[0]]
    values = [right_side[0] / diagonal[0]]
    for layer_pos in range(1, len(diagonal)):
        denom = diagonal[layer_pos] - coupling[layer_pos - 1] * ratios[layer_pos - 1]
        if layer_pos < len(diagonal) - 1:
            ratios.append(coupling[layer_pos] / denom)
        values.append(
            (right_side[layer_pos] + coupling[layer_pos - 1] * values[layer_pos - 1]) / denom
        )
    result = [values[-1]]
    for layer_pos in range(len(diagonal) - 2, -1, -1):
        result.insert(0, values[layer_pos] + ratios[layer_pos] * result[0])
    return result


def conductivity(current, layers, snow):
    return [jnp.full_like(snow, 0.31)] + [
        2.03 + 0.47 / (1.0 + current[layer_pos] * current[layer_pos])
        for layer_pos in range(1, layers)
    ]


def column_physics(packed, categories, layers):
    width = packed.shape[1]
    stacked = categories * layers
    temps = packed[:stacked].reshape(categories, layers, width)
    thick = packed[stacked : stacked + categories]
    snow = packed[stacked + categories : stacked + 2 * categories]
    air = packed[stacked + 2 * categories]
    heat = packed[stacked + 2 * categories + 1]
    depth = [snow] + [thick / (layers - 1)] * (layers - 1)
    start = [temps[:, layer_pos] for layer_pos in range(layers)]
    current = start
    for repeat in range(ITERS):
        conduct = conductivity(current, layers, snow)
        capacity = [2.1 * depth[0] / THERMO_STEP] + [
            (2.1 + 72.0 / (1.0 + current[layer_pos] * current[layer_pos]))
            * depth[layer_pos]
            / THERMO_STEP
            for layer_pos in range(1, layers)
        ]
        inner = [
            2.0
            / (
                depth[layer_pos] / conduct[layer_pos]
                + depth[layer_pos + 1] / conduct[layer_pos + 1]
            )
            for layer_pos in range(layers - 1)
        ]
        top_link = 1.0 / (1.0 / AIR_EXCHANGE + 0.5 * depth[0] / conduct[0])
        base_link = 2.0 * conduct[-1] / depth[-1]
        links = [top_link] + inner + [base_link]
        diagonal = [
            capacity[layer_pos] + links[layer_pos] + links[layer_pos + 1]
            for layer_pos in range(layers)
        ]
        right_side = [capacity[layer_pos] * start[layer_pos] for layer_pos in range(layers)]
        right_side[0] = right_side[0] + top_link * air
        right_side[-1] = right_side[-1] + base_link * FREEZING
        current = solve_layers(diagonal, inner, right_side)
    final_link = 2.0 * conductivity(current, layers, snow)[-1] / depth[-1]
    new_thick = thick + GROWTH_RATE * (final_link * (FREEZING - current[-1]) - heat)
    new_temps = jnp.stack(current, axis=1).reshape(stacked, width)
    return jnp.concatenate([new_temps, new_thick], axis=0)


def strain_terms(east_ext, north_ext):
    east_dx = 0.5 * (east_ext[1:-1, 2:] - east_ext[1:-1, :-2])
    north_dy = 0.5 * (north_ext[2:, 1:-1] - north_ext[:-2, 1:-1])
    east_dy = 0.5 * (east_ext[2:, 1:-1] - east_ext[:-2, 1:-1])
    north_dx = 0.5 * (north_ext[1:-1, 2:] - north_ext[1:-1, :-2])
    return (east_dx + north_dy, east_dx - north_dy, east_dy + north_dx)


def relax_stress(stress_sum, stress_diff, stress_shear, strength, east_ext, north_ext):
    diverge, tension, shearing = strain_terms(east_ext, north_ext)
    deform = jnp.sqrt(diverge * diverge + 0.25 * (tension * tension + shearing * shearing) + 1.0)
    bulk = strength / deform
    shear_visc = 0.25 * bulk
    stress_sum = (stress_sum + RELAX * (bulk * diverge - strength)) / (1.0 + RELAX)
    stress_diff = (stress_diff + RELAX * shear_visc * tension) / (1.0 + RELAX)
    stress_shear = (stress_shear + RELAX * 0.5 * shear_visc * shearing) / (1.0 + RELAX)
    return (stress_sum, stress_diff, stress_shear)


def stress_force(normal_xx, normal_yy, shear_xy):
    force_east = 0.5 * (normal_xx[1:-1, 2:] - normal_xx[1:-1, :-2]) + 0.5 * (
        shear_xy[2:, 1:-1] - shear_xy[:-2, 1:-1]
    )
    force_north = 0.5 * (shear_xy[1:-1, 2:] - shear_xy[1:-1, :-2]) + 0.5 * (
        normal_yy[2:, 1:-1] - normal_yy[:-2, 1:-1]
    )
    return (force_east, force_north)


def momentum(
    east_vel,
    north_vel,
    force_east,
    force_north,
    mass,
    coriolis,
    wind_stress,
    ocean_current,
    ocean_cells,
):
    diagonal = mass + DRAG
    turning = coriolis * mass
    rhs_east = mass * east_vel + force_east + wind_stress[0] + DRAG * ocean_current[0]
    rhs_north = mass * north_vel + force_north + wind_stress[1] + DRAG * ocean_current[1]
    determinant = diagonal * diagonal + turning * turning
    east_new = (diagonal * rhs_east + turning * rhs_north) / determinant * ocean_cells
    north_new = (diagonal * rhs_north - turning * rhs_east) / determinant * ocean_cells
    return (east_new, north_new)


def place_fold(tall, folded, rows, width):
    on_top = lax.axis_index("by") == lax.axis_size("by") - 1
    north = jnp.where(on_top, folded, tall[:, rows + width :])
    return jnp.concatenate([tall[:, : rows + width], north], axis=1)


def extend_deep(fields, signs):
    wide = with_halo(fields, (("bx", 2),), 2, True)
    folded = wide[:, ::-1][:, :2][:, :, ::-1] * signs[:, None, None]
    for bit_pos in range(lax.axis_size("bx").bit_length() - 1):
        folded = partner(folded, "bx", bit_pos)
    tall = with_halo(wide, (("by", 1),), 2, False)
    return place_fold(tall, folded, fields.shape[1], 2)


def per_device(
    layer_temps,
    ice_thick,
    snow_thick,
    ice_area,
    air_temp,
    ocean_heat,
    velocity,
    stress,
    wind_stress,
    ocean_current,
    ocean_mask,
    ice_cols,
):
    categories, rows, columns = ice_thick.shape
    stacked = layer_temps.shape[0]
    layers = stacked // categories
    cells = rows * columns
    listed = ice_cols.reshape(-1)
    safe = jnp.maximum(listed, 0)
    target = jnp.where(listed >= 0, listed, cells)
    state_rows = jnp.concatenate(
        [
            layer_temps.reshape(stacked, cells),
            ice_thick.reshape(categories, cells),
            snow_thick.reshape(categories, cells),
            air_temp.reshape(1, cells),
            ocean_heat.reshape(1, cells),
        ],
        axis=0,
    )
    kept = stacked + categories
    updated = column_physics(jnp.take(state_rows, safe, axis=1), categories, layers)
    renewed = state_rows[:kept].at[:, target].set(updated, mode="drop")
    temps_new = renewed[:stacked].reshape(stacked, rows, columns)
    thick_new = renewed[stacked:].reshape(categories, rows, columns)
    ice = jnp.zeros((cells,), jnp.float32).at[target].set(1.0, mode="drop").reshape(rows, columns)
    load = jnp.sum(ice_area * thick_new, axis=0)
    area_total = jnp.sum(ice_area, axis=0)
    strength = ice * load * jnp.exp(-HARDENING * (1.0 - area_total))
    mass = DENSITY * ice * load
    global_row = lax.axis_index("by") * rows + jnp.arange(rows, dtype=jnp.int32)
    lat_rows = rows * lax.axis_size("by")
    latitude = global_row.astype(jnp.float32) + 0.5
    coriolis = (1.4 * jnp.sin(0.5 * jnp.pi * (2.0 * latitude / lat_rows - 1.0)))[:, None]
    ocean_cells = ocean_mask.astype(jnp.float32)
    east_vel, north_vel = (velocity[0], velocity[1])
    stress_sum, stress_diff, stress_shear = (stress[0], stress[1], stress[2])
    state_signs = jnp.array([-1.0, -1.0, 1.0, 1.0, 1.0], jnp.float32)
    hard_cycle = extend_deep(strength[None], jnp.ones((1,), jnp.float32))[0][1:-1, 1:-1]
    for subcycle in range(SUB):
        state = extend_deep(
            jnp.stack([east_vel, north_vel, stress_sum, stress_diff, stress_shear]), state_signs
        )
        cycle_sum, cycle_diff, cycle_shear = relax_stress(
            state[2, 1:-1, 1:-1],
            state[3, 1:-1, 1:-1],
            state[4, 1:-1, 1:-1],
            hard_cycle,
            state[0],
            state[1],
        )
        force_east, force_north = stress_force(
            0.5 * (cycle_sum + cycle_diff), 0.5 * (cycle_sum - cycle_diff), cycle_shear
        )
        stress_sum = cycle_sum[1:-1, 1:-1]
        stress_diff = cycle_diff[1:-1, 1:-1]
        stress_shear = cycle_shear[1:-1, 1:-1]
        east_vel, north_vel = momentum(
            east_vel,
            north_vel,
            force_east,
            force_north,
            mass,
            coriolis,
            wind_stress,
            ocean_current,
            ocean_cells,
        )
    return (
        temps_new,
        thick_new,
        jnp.stack([east_vel, north_vel]),
        jnp.stack([stress_sum, stress_diff, stress_shear]),
    )


def solution(mesh):
    in_specs = (
        P(None, "by", "bx"),
        P(None, "by", "bx"),
        P(None, "by", "bx"),
        P(None, "by", "bx"),
        P("by", "bx"),
        P("by", "bx"),
        P(None, "by", "bx"),
        P(None, "by", "bx"),
        P(None, "by", "bx"),
        P(None, "by", "bx"),
        P("by", "bx"),
        P("by", "bx", None),
    )
    out_specs = (P(None, "by", "bx"), P(None, "by", "bx"), P(None, "by", "bx"), P(None, "by", "bx"))
    return jax.shard_map(
        per_device, mesh=mesh, in_specs=in_specs, out_specs=out_specs, check_vma=False
    )
```

profile of v0, /device:TPU:14, one launch (start us, length us, event | category | flops | bytes accessed | tf_op | source)
XLA Modules:
  0.0 354.0 jit_solution(5221036455361404506)
XLA Ops:
  2.3 7.9 %copy.108 = f32[5,8,128,256]{3,1,2,0:T(8,128)} copy(f32[5,8,128,256]{3,2,1,0:T(8,128)} %bitcast.748) | data formatting | bytes 10485760
  11.4 27.2 %concatenate.40 = f32[52,32768]{1,0:T(8,128)} concatenate(f32[40,32768]{1,0:T(8,128)} %bitcast.744, f32[5,32768]{1,0:T(8,128)S(1)} %bitcast.746, f32[5,32768]{1,0:T(8,128)S(1)} %bitcast.749, f32[1,32768]{1,0:T(1,128)S(1)} %bitcast.757, f32[1,32768]{1,0:T(1,128)S(1)} %bitcast.758), dimensions={0} | concatenate | bytes 13631488 | tf_op jit(solution)/shard_map/concatenate | solution.py:190
  38.6 12.0 %copy.77 = f32[52,32768]{0,1:T(8,128)} copy(f32[52,32768]{1,0:T(8,128)} %concatenate.40) | data formatting | bytes 13631488 | tf_op jit(solution)/shard_map/concatenate | solution.py:190
  50.6 26.8 %gather_fusion = f32[6144,52]{1,0:T(8,128)} fusion(f32[52,32768]{0,1:T(8,128)} %copy.77, s32[6144]{0:T(1024)S(1)} %broadcast_clamp_fusion), kind=kCustom, calls=%fused_computation | custom fusion | bytes 2580480 | tf_op jit(solution)/shard_map/jit(_take)/gather | solution.py:201
  77.5 2.6 copy.78
  80.3 5.5 %pad_maximum_fusion = f32[45,32768]{1,0:T(8,128)} fusion(f32[5,32768]{1,0:T(8,128)S(1)} %bitcast.747, f32[40,32768]{1,0:T(8,128)} %bitcast.745), kind=kLoop, calls=%fused_computation.3 | loop fusion | flops 1474560 | bytes 11796480 | tf_op jit(solution)/shard_map/concatenate | solution.py:190
  100.5 2.1 copy.96
  102.6 11.6 %copy.95 = f32[45,32768]{0,1:T(8,128)} copy(f32[45,32768]{1,0:T(8,128)} %pad_maximum_fusion) | data formatting | bytes 11796480 | tf_op jit(solution)/shard_map/concatenate | solution.py:190
  114.2 27.1 %scatter_fusion = f32[45,32768]{0,1:T(8,128)} fusion(f32[45,32768]{0,1:T(8,128)} %copy.95, s32[6144]{0:T(1024)S(1)} %bitcast.764, f32[6144,45]{1,0:T(8,128)S(1)} %copy.96), kind=kCustom, calls=%fused_computation.1 | custom fusion | bytes 3342336 | tf_op jit(solution)/shard_map/scatter | solution.py:202
  141.3 12.8 %slice.597 = f32[5,32768]{0,1:T(8,128)} slice(f32[45,32768]{0,1:T(8,128)} %scatter_fusion), slice={[40:45], [0:32768]} | slice | bytes 1310720 | tf_op jit(solution)/shard_map/slice | solution.py:204
  154.1 10.1 %copy.99 = f32[5,128,256]{2,1,0:T(8,128)S(1)} copy(f32[5,128,256]{0,2,1:T(8,128)} %bitcast.743) | data formatting | bytes 1310720
  164.3 23.0 %scatter_custom_fusion.1 = f32[32768]{0:T(1024)S(1)} fusion(s32[6144]{0:T(1024)S(1)} %bitcast.765, f32[6144]{0:T(1024)S(1)} %broadcast.228, f32[]{:T(128)} %constant.129.clone.1), kind=kCustom, calls=%fused_computation.536 | custom fusion | bytes 131076 | tf_op jit(solution)/shard_map/scatter | solution.py:205
  189.9 4.0 %collective-permute-start = (f32[5,128,2]{2,1,0:T(8,128)S(1)}, f32[5,128,2]{2,1,0:T(8,128)S(1)}, u32[]{:S(2)}, u32[]{:S(2)}) collective-permute-start(f32[5,128,2]{2,1,0:T(8,128)S(1)} %get-tuple-element.175), channel_id=1, source_target_pairs={{0,8},{8,16},{16,24},{24,32},{32,40},{40,48},{48,56},{56,64},{64,7... | collective-permute-start | bytes 15368 | tf_op jit(solution)/shard_map/ppermute | solution.py:27
  193.9 1.9 collective-permute-done.9
  196.3 4.1 %collective-permute-done.11 = f32[1,2,260]{2,1,0:T(2,128)S(1)} collective-permute-done((f32[1,2,260]{2,1,0:T(2,128)S(1)}, f32[1,2,260]{2,1,0:T(2,128)S(1)}, u32[]{:S(2)}, u32[]{:S(2)}) %collective-permute-start.11) | collective-permute-done | bytes 2112 | tf_op jit(solution)/shard_map/ppermute | solution.py:34
  200.4 3.3 collective-permute-start.12
  207.5 1.9 collective-permute-start.15
  209.4 4.6 %collective-permute-start.14 = (f32[1,2,260]{2,1,0:T(2,128)S(1)}, f32[1,2,260]{2,1,0:T(2,128)S(1)}, u32[]{:S(2)}, u32[]{:S(2)}) collective-permute-start(f32[1,2,260]{2,1,0:T(2,128)S(1)} %collective-permute-done.13), channel_id=1, source_target_pairs={{0,64},{8,72},{16,80},{24,88},{32,96},{40,104},{48,112},{56,120},{... | collective-permute-start | bytes 6248 | tf_op jit(solution)/shard_map/ppermute | solution.py:34
  217.0 3.6 %collective-permute-start.2 = (f32[5,2,260]{2,1,0:T(2,128)S(1)}, f32[5,2,260]{2,1,0:T(2,128)S(1)}, u32[]{:S(2)}, u32[]{:S(2)}) collective-permute-start(f32[5,2,260]{2,1,0:T(2,128)S(1)} %get-tuple-element.152), channel_id=1, source_target_pairs={{0,1},{1,2},{2,3},{3,4},{4,5},{5,6},{6,7},{8,9},{9,10},{10,11},{11... | collective-permute-start | bytes 31208 | tf_op jit(solution)/shard_map/ppermute | solution.py:27
  220.6 2.0 collective-permute-start.7
  223.7 2.8 collective-permute-done.5
  228.5 3.6 %collective-permute-done.6 = f32[5,2,260]{2,1,0:T(2,128)S(1)} collective-permute-done((f32[5,2,260]{2,1,0:T(2,128)S(1)}, f32[5,2,260]{2,1,0:T(2,128)S(1)}, u32[]{:S(2)}, u32[]{:S(2)}) %collective-permute-start.6) | collective-permute-done | bytes 10432 | tf_op jit(solution)/shard_map/ppermute | solution.py:34
  234.6 4.0 %collective-permute-start.16 = (f32[5,128,2]{2,1,0:T(8,128)S(1)}, f32[5,128,2]{2,1,0:T(8,128)S(1)}, u32[]{:S(2)}, u32[]{:S(2)}) collective-permute-start(f32[5,128,2]{2,1,0:T(8,128)S(1)} %get-tuple-element.173), channel_id=1, source_target_pairs={{0,8},{8,16},{16,24},{24,32},{32,40},{40,48},{48,56},{56,64},{64,7... | collective-permute-start | bytes 15368 | tf_op jit(solution)/shard_map/ppermute | solution.py:27
  238.6 5.3 %collective-permute-done.16 = f32[5,128,2]{2,1,0:T(8,128)S(1)} collective-permute-done((f32[5,128,2]{2,1,0:T(8,128)S(1)}, f32[5,128,2]{2,1,0:T(8,128)S(1)}, u32[]{:S(2)}, u32[]{:S(2)}) %collective-permute-start.16) | collective-permute-done | bytes 5152 | tf_op jit(solution)/shard_map/ppermute | solution.py:27
  243.8 4.3 %collective-permute-done.17 = f32[5,128,2]{2,1,0:T(8,128)S(1)} collective-permute-done((f32[5,128,2]{2,1,0:T(8,128)S(1)}, f32[5,128,2]{2,1,0:T(8,128)S(1)}, u32[]{:S(2)}, u32[]{:S(2)}) %collective-permute-start.17) | collective-permute-done | bytes 5152 | tf_op jit(solution)/shard_map/ppermute | solution.py:28
  248.8 3.7 %collective-permute-done.19 = f32[5,2,260]{2,1,0:T(2,128)S(1)} collective-permute-done((f32[5,2,260]{2,1,0:T(2,128)S(1)}, f32[5,2,260]{2,1,0:T(2,128)S(1)}, u32[]{:S(2)}, u32[]{:S(2)}) %collective-permute-start.19) | collective-permute-done | bytes 10432 | tf_op jit(solution)/shard_map/ppermute | solution.py:34
  253.1 4.7 %collective-permute-done.20 = f32[5,2,260]{2,1,0:T(2,128)S(1)} collective-permute-done((f32[5,2,260]{2,1,0:T(2,128)S(1)}, f32[5,2,260]{2,1,0:T(2,128)S(1)}, u32[]{:S(2)}, u32[]{:S(2)}) %collective-permute-start.20) | collective-permute-done | bytes 10432 | tf_op jit(solution)/shard_map/ppermute | solution.py:34
  261.5 3.2 collective-permute-start.22
  264.7 2.1 collective-permute-start.18
  266.9 2.9 collective-permute-done.18
  272.0 2.0 collective-permute-start.25
  274.0 6.7 %collective-permute-done.24 = f32[5,128,2]{2,1,0:T(8,128)S(1)} collective-permute-done((f32[5,128,2]{2,1,0:T(8,128)S(1)}, f32[5,128,2]{2,1,0:T(8,128)S(1)}, u32[]{:S(2)}, u32[]{:S(2)}) %collective-permute-start.24) | collective-permute-done | bytes 5152 | tf_op jit(solution)/shard_map/ppermute | solution.py:27
  280.7 2.2 collective-permute-done.25
  283.6 3.7 %collective-permute-done.27 = f32[5,2,260]{2,1,0:T(2,128)S(1)} collective-permute-done((f32[5,2,260]{2,1,0:T(2,128)S(1)}, f32[5,2,260]{2,1,0:T(2,128)S(1)}, u32[]{:S(2)}, u32[]{:S(2)}) %collective-permute-start.27) | collective-permute-done | bytes 10432 | tf_op jit(solution)/shard_map/ppermute | solution.py:34
  287.3 5.2 %collective-permute-done.28 = f32[5,2,260]{2,1,0:T(2,128)S(1)} collective-permute-done((f32[5,2,260]{2,1,0:T(2,128)S(1)}, f32[5,2,260]{2,1,0:T(2,128)S(1)}, u32[]{:S(2)}, u32[]{:S(2)}) %collective-permute-start.28) | collective-permute-done | bytes 10432 | tf_op jit(solution)/shard_map/ppermute | solution.py:34
  296.3 2.4 collective-permute-start.30
  298.7 2.1 collective-permute-start.26
  301.5 2.2 collective-permute-done.26
  306.0 2.0 collective-permute-start.33
  308.0 6.7 %collective-permute-done.32 = f32[5,128,2]{2,1,0:T(8,128)S(1)} collective-permute-done((f32[5,128,2]{2,1,0:T(8,128)S(1)}, f32[5,128,2]{2,1,0:T(8,128)S(1)}, u32[]{:S(2)}, u32[]{:S(2)}) %collective-permute-start.32) | collective-permute-done | bytes 5152 | tf_op jit(solution)/shard_map/ppermute | solution.py:27
  314.7 2.2 collective-permute-done.33
  317.6 3.7 %collective-permute-done.35 = f32[5,2,260]{2,1,0:T(2,128)S(1)} collective-permute-done((f32[5,2,260]{2,1,0:T(2,128)S(1)}, f32[5,2,260]{2,1,0:T(2,128)S(1)}, u32[]{:S(2)}, u32[]{:S(2)}) %collective-permute-start.35) | collective-permute-done | bytes 10432 | tf_op jit(solution)/shard_map/ppermute | solution.py:34
  321.4 5.1 %collective-permute-done.36 = f32[5,2,260]{2,1,0:T(2,128)S(1)} collective-permute-done((f32[5,2,260]{2,1,0:T(2,128)S(1)}, f32[5,2,260]{2,1,0:T(2,128)S(1)}, u32[]{:S(2)}, u32[]{:S(2)}) %collective-permute-start.36) | collective-permute-done | bytes 10432 | tf_op jit(solution)/shard_map/ppermute | solution.py:34
  327.6 2.1 collective-permute-start.39
  330.2 2.9 collective-permute-start.38
  333.2 12.1 %copy.98 = f32[40,128,256]{2,1,0:T(8,128)} copy(f32[40,128,256]{0,2,1:T(8,128)} %bitcast.742) | data formatting | bytes 10485760
  345.3 2.1 collective-permute-start.34
  347.4 2.9 collective-permute-done.34
  (176 shorter events, 52.9 us)
Async XLA Ops:
  2.3 7.9 %copy-start.5 = (f32[5,128,256]{2,1,0:T(8,128)S(1)}, f32[5,128,256]{2,1,0:T(8,128)}, u32[]{:S(2)}) copy-start(f32[5,128,256]{2,1,0:T(8,128)} %param.14) | copy-start | bytes 1966084
  2.3 8.3 %copy-start.6 = (f32[5,128,256]{2,1,0:T(8,128)S(1)}, f32[5,128,256]{2,1,0:T(8,128)}, u32[]{:S(2)}) copy-start(f32[5,128,256]{2,1,0:T(8,128)} %param.15) | copy-start | bytes 1966084
  154.1 33.2 %copy-start.7 = (f32[5,128,256]{2,1,0:T(8,128)S(1)}, f32[5,128,256]{2,1,0:T(8,128)}, u32[]{:S(2)}) copy-start(f32[5,128,256]{2,1,0:T(8,128)} %param.16) | copy-start | bytes 1966084
  154.1 35.6 %copy-start.4 = (f32[2,128,256]{2,1,0:T(8,128)S(1)}, f32[2,128,256]{2,1,0:T(8,128)}, u32[]{:S(2)}) copy-start(f32[2,128,256]{2,1,0:T(8,128)} %param.19) | copy-start | bytes 786436
  164.2 40.5 %copy-start.3 = (f32[5,128,256]{2,1,0:T(8,128)}, f32[5,128,256]{2,1,0:T(8,128)S(1)}, u32[]{:S(2)}) copy-start(f32[5,128,256]{2,1,0:T(8,128)S(1)} %copy.99) | copy-start | bytes 1966084
  164.3 25.4 %copy-start.8 = (f32[3,128,256]{2,1,0:T(8,128)S(1)}, f32[3,128,256]{2,1,0:T(8,128)}, u32[]{:S(2)}) copy-start(f32[3,128,256]{2,1,0:T(8,128)} %param.20) | copy-start | bytes 1179652
  187.4 17.8 %copy-start.11 = (f32[5]{0:T(128)S(1)}, f32[5]{0:T(128)}, u32[]{:S(2)}) copy-start(f32[5]{0:T(128)} %constant.144.clone) | copy-start | bytes 64
  187.6 6.3 %collective-permute-start.8 = (f32[1,128,2]{2,1,0:T(8,128)S(1)}, f32[1,128,2]{2,1,0:T(8,128)S(1)}, u32[]{:S(2)}, u32[]{:S(2)}) collective-permute-start(f32[1,128,2]{2,1,0:T(8,128)S(1)} %get-tuple-element.180), channel_id=1, source_target_pairs={{0,8},{8,16},{16,24},{24,32},{32,40},{40,48},{48,56},{56,64},{64,7... | collective-permute-start | bytes 3080 | tf_op jit(solution)/shard_map/ppermute | solution.py:27
  189.5 6.4 %collective-permute-start.9 = (f32[1,128,2]{2,1,0:T(8,128)S(1)}, f32[1,128,2]{2,1,0:T(8,128)S(1)}, u32[]{:S(2)}, u32[]{:S(2)}) collective-permute-start(f32[1,128,2]{2,1,0:T(8,128)S(1)} %get-tuple-element.181), channel_id=1, source_target_pairs={{8,0},{16,8},{24,16},{32,24},{40,32},{48,40},{56,48},{64,56},{72,6... | collective-permute-start | bytes 3080 | tf_op jit(solution)/shard_map/ppermute | solution.py:28
  189.9 13.8 %collective-permute-start = (f32[5,128,2]{2,1,0:T(8,128)S(1)}, f32[5,128,2]{2,1,0:T(8,128)S(1)}, u32[]{:S(2)}, u32[]{:S(2)}) collective-permute-start(f32[5,128,2]{2,1,0:T(8,128)S(1)} %get-tuple-element.175), channel_id=1, source_target_pairs={{0,8},{8,16},{16,24},{24,32},{32,40},{40,48},{48,56},{56,64},{64,7... | collective-permute-start | bytes 15368 | tf_op jit(solution)/shard_map/ppermute | solution.py:27
  193.9 10.8 %collective-permute-start.1 = (f32[5,128,2]{2,1,0:T(8,128)S(1)}, f32[5,128,2]{2,1,0:T(8,128)S(1)}, u32[]{:S(2)}, u32[]{:S(2)}) collective-permute-start(f32[5,128,2]{2,1,0:T(8,128)S(1)} %get-tuple-element.176), channel_id=1, source_target_pairs={{8,0},{16,8},{24,16},{32,24},{40,32},{48,40},{56,48},{64,56},{72,6... | collective-permute-start | bytes 15368 | tf_op jit(solution)/shard_map/ppermute | solution.py:28
  196.3 4.1 %collective-permute-start.11 = (f32[1,2,260]{2,1,0:T(2,128)S(1)}, f32[1,2,260]{2,1,0:T(2,128)S(1)}, u32[]{:S(2)}, u32[]{:S(2)}) collective-permute-start(f32[1,2,260]{2,1,0:T(2,128)S(1)} %slice.1333), channel_id=1, source_target_pairs={{0,8},{8,0},{16,24},{24,16},{32,40},{40,32},{48,56},{56,48},{64,72... | collective-permute-start | bytes 6248 | tf_op jit(solution)/shard_map/ppermute | solution.py:34
  200.4 5.3 %collective-permute-start.12 = (f32[1,2,260]{2,1,0:T(2,128)S(1)}, f32[1,2,260]{2,1,0:T(2,128)S(1)}, u32[]{:S(2)}, u32[]{:S(2)}) collective-permute-start(f32[1,2,260]{2,1,0:T(2,128)S(1)} %collective-permute-done.11), channel_id=1, source_target_pairs={{0,16},{8,24},{16,0},{24,8},{32,48},{40,56},{48,32},{56,40},{64,80... | collective-permute-start | bytes 6248 | tf_op jit(solution)/shard_map/ppermute | solution.py:34
  205.2 8.7 %collective-permute-start.3 = (f32[5,2,260]{2,1,0:T(2,128)S(1)}, f32[5,2,260]{2,1,0:T(2,128)S(1)}, u32[]{:S(2)}, u32[]{:S(2)}) collective-permute-start(f32[5,2,260]{2,1,0:T(2,128)S(1)} %broadcast_multiply_fusion.4), channel_id=1, source_target_pairs={{0,8},{8,0},{16,24},{24,16},{32,40},{40,32},{48,56},{56,48},{64,72... | collective-permute-start | bytes 31208 | tf_op jit(solution)/shard_map/ppermute | solution.py:34
  205.7 3.7 %collective-permute-start.13 = (f32[1,2,260]{2,1,0:T(2,128)S(1)}, f32[1,2,260]{2,1,0:T(2,128)S(1)}, u32[]{:S(2)}, u32[]{:S(2)}) collective-permute-start(f32[1,2,260]{2,1,0:T(2,128)S(1)} %collective-permute-done.12), channel_id=1, source_target_pairs={{0,32},{8,40},{16,48},{24,56},{32,0},{40,8},{48,16},{56,24},{64,96... | collective-permute-start | bytes 6248 | tf_op jit(solution)/shard_map/ppermute | solution.py:34
  207.5 13.2 %collective-permute-start.15 = (f32[1,2,260]{2,1,0:T(2,128)S(1)}, f32[1,2,260]{2,1,0:T(2,128)S(1)}, u32[]{:S(2)}, u32[]{:S(2)}) collective-permute-start(f32[1,2,260]{2,1,0:T(2,128)S(1)} %get-tuple-element.177), channel_id=1, source_target_pairs={{1,0},{2,1},{3,2},{4,3},{5,4},{6,5},{7,6},{9,8},{10,9},{11,10},{12... | collective-permute-start | bytes 6248 | tf_op jit(solution)/shard_map/ppermute | solution.py:28
  209.4 14.3 %collective-permute-start.14 = (f32[1,2,260]{2,1,0:T(2,128)S(1)}, f32[1,2,260]{2,1,0:T(2,128)S(1)}, u32[]{:S(2)}, u32[]{:S(2)}) collective-permute-start(f32[1,2,260]{2,1,0:T(2,128)S(1)} %collective-permute-done.13), channel_id=1, source_target_pairs={{0,64},{8,72},{16,80},{24,88},{32,96},{40,104},{48,112},{56,120},{... | collective-permute-start | bytes 6248 | tf_op jit(solution)/shard_map/ppermute | solution.py:34
  214.0 8.7 %collective-permute-start.4 = (f32[5,2,260]{2,1,0:T(2,128)S(1)}, f32[5,2,260]{2,1,0:T(2,128)S(1)}, u32[]{:S(2)}, u32[]{:S(2)}) collective-permute-start(f32[5,2,260]{2,1,0:T(2,128)S(1)} %collective-permute-done.3), channel_id=1, source_target_pairs={{0,16},{8,24},{16,0},{24,8},{32,48},{40,56},{48,32},{56,40},{64,80... | collective-permute-start | bytes 31208 | tf_op jit(solution)/shard_map/ppermute | solution.py:34
  215.1 13.2 %collective-permute-start.10 = (f32[1,2,260]{2,1,0:T(2,128)S(1)}, f32[1,2,260]{2,1,0:T(2,128)S(1)}, u32[]{:S(2)}, u32[]{:S(2)}) collective-permute-start(f32[1,2,260]{2,1,0:T(2,128)S(1)} %get-tuple-element.178), channel_id=1, source_target_pairs={{0,1},{1,2},{2,3},{3,4},{4,5},{5,6},{6,7},{8,9},{9,10},{10,11},{11... | collective-permute-start | bytes 6248 | tf_op jit(solution)/shard_map/ppermute | solution.py:27
  217.0 15.0 %collective-permute-start.2 = (f32[5,2,260]{2,1,0:T(2,128)S(1)}, f32[5,2,260]{2,1,0:T(2,128)S(1)}, u32[]{:S(2)}, u32[]{:S(2)}) collective-permute-start(f32[5,2,260]{2,1,0:T(2,128)S(1)} %get-tuple-element.152), channel_id=1, source_target_pairs={{0,1},{1,2},{2,3},{3,4},{4,5},{5,6},{6,7},{8,9},{9,10},{10,11},{11... | collective-permute-start | bytes 31208 | tf_op jit(solution)/shard_map/ppermute | solution.py:27
  220.6 7.8 %collective-permute-start.7 = (f32[5,2,260]{2,1,0:T(2,128)S(1)}, f32[5,2,260]{2,1,0:T(2,128)S(1)}, u32[]{:S(2)}, u32[]{:S(2)}) collective-permute-start(f32[5,2,260]{2,1,0:T(2,128)S(1)} %get-tuple-element.151), channel_id=1, source_target_pairs={{1,0},{2,1},{3,2},{4,3},{5,4},{6,5},{7,6},{9,8},{10,9},{11,10},{12... | collective-permute-start | bytes 31208 | tf_op jit(solution)/shard_map/ppermute | solution.py:28
  222.6 3.8 %collective-permute-start.5 = (f32[5,2,260]{2,1,0:T(2,128)S(1)}, f32[5,2,260]{2,1,0:T(2,128)S(1)}, u32[]{:S(2)}, u32[]{:S(2)}) collective-permute-start(f32[5,2,260]{2,1,0:T(2,128)S(1)} %collective-permute-done.4), channel_id=1, source_target_pairs={{0,32},{8,40},{16,48},{24,56},{32,0},{40,8},{48,16},{56,24},{64,96... | collective-permute-start | bytes 31208 | tf_op jit(solution)/shard_map/ppermute | solution.py:34
  226.4 5.6 %collective-permute-start.6 = (f32[5,2,260]{2,1,0:T(2,128)S(1)}, f32[5,2,260]{2,1,0:T(2,128)S(1)}, u32[]{:S(2)}, u32[]{:S(2)}) collective-permute-start(f32[5,2,260]{2,1,0:T(2,128)S(1)} %collective-permute-done.5), channel_id=1, source_target_pairs={{0,64},{8,72},{16,80},{24,88},{32,96},{40,104},{48,112},{56,120},{... | collective-permute-start | bytes 31208 | tf_op jit(solution)/shard_map/ppermute | solution.py:34
  232.6 1.1 copy-start.2
  234.6 9.3 %collective-permute-start.16 = (f32[5,128,2]{2,1,0:T(8,128)S(1)}, f32[5,128,2]{2,1,0:T(8,128)S(1)}, u32[]{:S(2)}, u32[]{:S(2)}) collective-permute-start(f32[5,128,2]{2,1,0:T(8,128)S(1)} %get-tuple-element.173), channel_id=1, source_target_pairs={{0,8},{8,16},{16,24},{24,32},{32,40},{40,48},{48,56},{56,64},{64,7... | collective-permute-start | bytes 15368 | tf_op jit(solution)/shard_map/ppermute | solution.py:27
  238.6 9.6 %collective-permute-start.17 = (f32[5,128,2]{2,1,0:T(8,128)S(1)}, f32[5,128,2]{2,1,0:T(8,128)S(1)}, u32[]{:S(2)}, u32[]{:S(2)}) collective-permute-start(f32[5,128,2]{2,1,0:T(8,128)S(1)} %get-tuple-element.174), channel_id=1, source_target_pairs={{8,0},{16,8},{24,16},{32,24},{40,32},{48,40},{56,48},{64,56},{72,6... | collective-permute-start | bytes 15368 | tf_op jit(solution)/shard_map/ppermute | solution.py:28
  248.7 3.8 %collective-permute-start.19 = (f32[5,2,260]{2,1,0:T(2,128)S(1)}, f32[5,2,260]{2,1,0:T(2,128)S(1)}, u32[]{:S(2)}, u32[]{:S(2)}) collective-permute-start(f32[5,2,260]{2,1,0:T(2,128)S(1)} %broadcast_multiply_fusion.3), channel_id=1, source_target_pairs={{0,8},{8,0},{16,24},{24,16},{32,40},{40,32},{48,56},{56,48},{64,72... | collective-permute-start | bytes 31208 | tf_op jit(solution)/shard_map/ppermute | solution.py:34
  252.5 5.2 %collective-permute-start.20 = (f32[5,2,260]{2,1,0:T(2,128)S(1)}, f32[5,2,260]{2,1,0:T(2,128)S(1)}, u32[]{:S(2)}, u32[]{:S(2)}) collective-permute-start(f32[5,2,260]{2,1,0:T(2,128)S(1)} %collective-permute-done.19), channel_id=1, source_target_pairs={{0,16},{8,24},{16,0},{24,8},{32,48},{40,56},{48,32},{56,40},{64,80... | collective-permute-start | bytes 31208 | tf_op jit(solution)/shard_map/ppermute | solution.py:34
  257.8 3.7 %collective-permute-start.21 = (f32[5,2,260]{2,1,0:T(2,128)S(1)}, f32[5,2,260]{2,1,0:T(2,128)S(1)}, u32[]{:S(2)}, u32[]{:S(2)}) collective-permute-start(f32[5,2,260]{2,1,0:T(2,128)S(1)} %collective-permute-done.20), channel_id=1, source_target_pairs={{0,32},{8,40},{16,48},{24,56},{32,0},{40,8},{48,16},{56,24},{64,96... | collective-permute-start | bytes 31208 | tf_op jit(solution)/shard_map/ppermute | solution.py:34
  257.8 9.1 %collective-permute-start.23 = (f32[5,2,260]{2,1,0:T(2,128)S(1)}, f32[5,2,260]{2,1,0:T(2,128)S(1)}, u32[]{:S(2)}, u32[]{:S(2)}) collective-permute-start(f32[5,2,260]{2,1,0:T(2,128)S(1)} %get-tuple-element.149), channel_id=1, source_target_pairs={{1,0},{2,1},{3,2},{4,3},{5,4},{6,5},{7,6},{9,8},{10,9},{11,10},{12... | collective-permute-start | bytes 31208 | tf_op jit(solution)/shard_map/ppermute | solution.py:28
  261.5 5.4 %collective-permute-start.22 = (f32[5,2,260]{2,1,0:T(2,128)S(1)}, f32[5,2,260]{2,1,0:T(2,128)S(1)}, u32[]{:S(2)}, u32[]{:S(2)}) collective-permute-start(f32[5,2,260]{2,1,0:T(2,128)S(1)} %collective-permute-done.21), channel_id=1, source_target_pairs={{0,64},{8,72},{16,80},{24,88},{32,96},{40,104},{48,112},{56,120},{... | collective-permute-start | bytes 31208 | tf_op jit(solution)/shard_map/ppermute | solution.py:34
  264.7 5.0 %collective-permute-start.18 = (f32[5,2,260]{2,1,0:T(2,128)S(1)}, f32[5,2,260]{2,1,0:T(2,128)S(1)}, u32[]{:S(2)}, u32[]{:S(2)}) collective-permute-start(f32[5,2,260]{2,1,0:T(2,128)S(1)} %get-tuple-element.150), channel_id=1, source_target_pairs={{0,1},{1,2},{2,3},{3,4},{4,5},{5,6},{6,7},{8,9},{9,10},{10,11},{11... | collective-permute-start | bytes 31208 | tf_op jit(solution)/shard_map/ppermute | solution.py:27
  271.9 8.8 %collective-permute-start.24 = (f32[5,128,2]{2,1,0:T(8,128)S(1)}, f32[5,128,2]{2,1,0:T(8,128)S(1)}, u32[]{:S(2)}, u32[]{:S(2)}) collective-permute-start(f32[5,128,2]{2,1,0:T(8,128)S(1)} %get-tuple-element.171), channel_id=1, source_target_pairs={{0,8},{8,16},{16,24},{24,32},{32,40},{40,48},{48,56},{56,64},{64,7... | collective-permute-start | bytes 15368 | tf_op jit(solution)/shard_map/ppermute | solution.py:27
  272.0 10.9 %collective-permute-start.25 = (f32[5,128,2]{2,1,0:T(8,128)S(1)}, f32[5,128,2]{2,1,0:T(8,128)S(1)}, u32[]{:S(2)}, u32[]{:S(2)}) collective-permute-start(f32[5,128,2]{2,1,0:T(8,128)S(1)} %get-tuple-element.172), channel_id=1, source_target_pairs={{8,0},{16,8},{24,16},{32,24},{40,32},{48,40},{56,48},{64,56},{72,6... | collective-permute-start | bytes 15368 | tf_op jit(solution)/shard_map/ppermute | solution.py:28
  283.5 3.8 %collective-permute-start.27 = (f32[5,2,260]{2,1,0:T(2,128)S(1)}, f32[5,2,260]{2,1,0:T(2,128)S(1)}, u32[]{:S(2)}, u32[]{:S(2)}) collective-permute-start(f32[5,2,260]{2,1,0:T(2,128)S(1)} %broadcast_multiply_fusion.2), channel_id=1, source_target_pairs={{0,8},{8,0},{16,24},{24,16},{32,40},{40,32},{48,56},{56,48},{64,72... | collective-permute-start | bytes 31208 | tf_op jit(solution)/shard_map/ppermute | solution.py:34
  287.3 5.2 %collective-permute-start.28 = (f32[5,2,260]{2,1,0:T(2,128)S(1)}, f32[5,2,260]{2,1,0:T(2,128)S(1)}, u32[]{:S(2)}, u32[]{:S(2)}) collective-permute-start(f32[5,2,260]{2,1,0:T(2,128)S(1)} %collective-permute-done.27), channel_id=1, source_target_pairs={{0,16},{8,24},{16,0},{24,8},{32,48},{40,56},{48,32},{56,40},{64,80... | collective-permute-start | bytes 31208 | tf_op jit(solution)/shard_map/ppermute | solution.py:34
  292.5 3.7 %collective-permute-start.29 = (f32[5,2,260]{2,1,0:T(2,128)S(1)}, f32[5,2,260]{2,1,0:T(2,128)S(1)}, u32[]{:S(2)}, u32[]{:S(2)}) collective-permute-start(f32[5,2,260]{2,1,0:T(2,128)S(1)} %collective-permute-done.28), channel_id=1, source_target_pairs={{0,32},{8,40},{16,48},{24,56},{32,0},{40,8},{48,16},{56,24},{64,96... | collective-permute-start | bytes 31208 | tf_op jit(solution)/shard_map/ppermute | solution.py:34
  293.6 7.2 %collective-permute-start.31 = (f32[5,2,260]{2,1,0:T(2,128)S(1)}, f32[5,2,260]{2,1,0:T(2,128)S(1)}, u32[]{:S(2)}, u32[]{:S(2)}) collective-permute-start(f32[5,2,260]{2,1,0:T(2,128)S(1)} %get-tuple-element.147), channel_id=1, source_target_pairs={{1,0},{2,1},{3,2},{4,3},{5,4},{6,5},{7,6},{9,8},{10,9},{11,10},{12... | collective-permute-start | bytes 31208 | tf_op jit(solution)/shard_map/ppermute | solution.py:28
  296.3 5.2 %collective-permute-start.30 = (f32[5,2,260]{2,1,0:T(2,128)S(1)}, f32[5,2,260]{2,1,0:T(2,128)S(1)}, u32[]{:S(2)}, u32[]{:S(2)}) collective-permute-start(f32[5,2,260]{2,1,0:T(2,128)S(1)} %collective-permute-done.29), channel_id=1, source_target_pairs={{0,64},{8,72},{16,80},{24,88},{32,96},{40,104},{48,112},{56,120},{... | collective-permute-start | bytes 31208 | tf_op jit(solution)/shard_map/ppermute | solution.py:34
  298.7 5.0 %collective-permute-start.26 = (f32[5,2,260]{2,1,0:T(2,128)S(1)}, f32[5,2,260]{2,1,0:T(2,128)S(1)}, u32[]{:S(2)}, u32[]{:S(2)}) collective-permute-start(f32[5,2,260]{2,1,0:T(2,128)S(1)} %get-tuple-element.148), channel_id=1, source_target_pairs={{0,1},{1,2},{2,3},{3,4},{4,5},{5,6},{6,7},{8,9},{9,10},{10,11},{11... | collective-permute-start | bytes 31208 | tf_op jit(solution)/shard_map/ppermute | solution.py:27
  305.9 8.8 %collective-permute-start.32 = (f32[5,128,2]{2,1,0:T(8,128)S(1)}, f32[5,128,2]{2,1,0:T(8,128)S(1)}, u32[]{:S(2)}, u32[]{:S(2)}) collective-permute-start(f32[5,128,2]{2,1,0:T(8,128)S(1)} %get-tuple-element.169), channel_id=1, source_target_pairs={{0,8},{8,16},{16,24},{24,32},{32,40},{40,48},{48,56},{56,64},{64,7... | collective-permute-start | bytes 15368 | tf_op jit(solution)/shard_map/ppermute | solution.py:27
  306.0 10.9 %collective-permute-start.33 = (f32[5,128,2]{2,1,0:T(8,128)S(1)}, f32[5,128,2]{2,1,0:T(8,128)S(1)}, u32[]{:S(2)}, u32[]{:S(2)}) collective-permute-start(f32[5,128,2]{2,1,0:T(8,128)S(1)} %get-tuple-element.170), channel_id=1, source_target_pairs={{8,0},{16,8},{24,16},{32,24},{40,32},{48,40},{56,48},{64,56},{72,6... | collective-permute-start | bytes 15368 | tf_op jit(solution)/shard_map/ppermute | solution.py:28
  317.5 3.8 %collective-permute-start.35 = (f32[5,2,260]{2,1,0:T(2,128)S(1)}, f32[5,2,260]{2,1,0:T(2,128)S(1)}, u32[]{:S(2)}, u32[]{:S(2)}) collective-permute-start(f32[5,2,260]{2,1,0:T(2,128)S(1)} %broadcast_multiply_fusion.1), channel_id=1, source_target_pairs={{0,8},{8,0},{16,24},{24,16},{32,40},{40,32},{48,56},{56,48},{64,72... | collective-permute-start | bytes 31208 | tf_op jit(solution)/shard_map/ppermute | solution.py:34
  321.3 5.2 %collective-permute-start.36 = (f32[5,2,260]{2,1,0:T(2,128)S(1)}, f32[5,2,260]{2,1,0:T(2,128)S(1)}, u32[]{:S(2)}, u32[]{:S(2)}) collective-permute-start(f32[5,2,260]{2,1,0:T(2,128)S(1)} %collective-permute-done.35), channel_id=1, source_target_pairs={{0,16},{8,24},{16,0},{24,8},{32,48},{40,56},{48,32},{56,40},{64,80... | collective-permute-start | bytes 31208 | tf_op jit(solution)/shard_map/ppermute | solution.py:34
  326.5 3.7 %collective-permute-start.37 = (f32[5,2,260]{2,1,0:T(2,128)S(1)}, f32[5,2,260]{2,1,0:T(2,128)S(1)}, u32[]{:S(2)}, u32[]{:S(2)}) collective-permute-start(f32[5,2,260]{2,1,0:T(2,128)S(1)} %collective-permute-done.36), channel_id=1, source_target_pairs={{0,32},{8,40},{16,48},{24,56},{32,0},{40,8},{48,16},{56,24},{64,96... | collective-permute-start | bytes 31208 | tf_op jit(solution)/shard_map/ppermute | solution.py:34
  327.6 19.8 %collective-permute-start.39 = (f32[5,2,260]{2,1,0:T(2,128)S(1)}, f32[5,2,260]{2,1,0:T(2,128)S(1)}, u32[]{:S(2)}, u32[]{:S(2)}) collective-permute-start(f32[5,2,260]{2,1,0:T(2,128)S(1)} %get-tuple-element.145), channel_id=1, source_target_pairs={{1,0},{2,1},{3,2},{4,3},{5,4},{6,5},{7,6},{9,8},{10,9},{11,10},{12... | collective-permute-start | bytes 31208 | tf_op jit(solution)/shard_map/ppermute | solution.py:28
  330.2 17.2 %collective-permute-start.38 = (f32[5,2,260]{2,1,0:T(2,128)S(1)}, f32[5,2,260]{2,1,0:T(2,128)S(1)}, u32[]{:S(2)}, u32[]{:S(2)}) collective-permute-start(f32[5,2,260]{2,1,0:T(2,128)S(1)} %collective-permute-done.37), channel_id=1, source_target_pairs={{0,64},{8,72},{16,80},{24,88},{32,96},{40,104},{48,112},{56,120},{... | collective-permute-start | bytes 31208 | tf_op jit(solution)/shard_map/ppermute | solution.py:34
  345.3 5.0 %collective-permute-start.34 = (f32[5,2,260]{2,1,0:T(2,128)S(1)}, f32[5,2,260]{2,1,0:T(2,128)S(1)}, u32[]{:S(2)}, u32[]{:S(2)}) collective-permute-start(f32[5,2,260]{2,1,0:T(2,128)S(1)} %get-tuple-element.146), channel_id=1, source_target_pairs={{0,1},{1,2},{2,3},{3,4},{4,5},{5,6},{6,7},{8,9},{9,10},{10,11},{11... | collective-permute-start | bytes 31208 | tf_op jit(solution)/shard_map/ppermute | solution.py:27
  (4 other events, 3.9 us)
where the time goes:
time: 360 us; the launch traced here: 354 us
  local copies, waits for them, and re-layouts  184 us (51%)
  waiting for transfers between devices  78.6 us (22%)
  starting transfers between devices  61.6 us (17%)
  other arithmetic  27.7 us (8%)
    concatenate x3, local copies, waits for them, and re-layouts, per_device(): jnp.concatenate([layer_temps.reshape(stacked, cells), ice_thick.reshape(c...  50.8 us
    ppermute x20, waiting for transfers between devices, partner(): lax.ppermute(x, axis, [(i, i ^ 1 << distance) for i in range(lax.axis_siz...  40.4 us
    unnamed x44, local copies, waits for them, and re-layouts  34 us
    gather x2, local copies, waits for them, and re-layouts, per_device(): jnp.take(state_rows, safe, axis=1)  29.4 us
    scatter x1, local copies, waits for them, and re-layouts, per_device(): renewed = state_rows[:kept].at[:, target].set(updated, mode='drop')  27.1 us
    ppermute x10, waiting for transfers between devices, with_halo(): before = lax.ppermute(last, axis, up)  26.6 us
    ppermute x20, starting transfers between devices, partner(): lax.ppermute(x, axis, [(i, i ^ 1 << distance) for i in range(lax.axis_siz...  25.7 us
    scatter x1, local copies, waits for them, and re-layouts, per_device(): jnp.zeros((cells,), jnp.float32).at[target].set(1.0, mode='drop')  23 us
  transfers between devices with their start and end apart: 40, of which 24 were waited for; matrix products, arithmetic and copies ran while one was open for 4% of the time, Pallas kernels for 0%

commit v1 on v0

v1 whole, which is shorter than its diff:
```python
import jax
import jax.numpy as jnp
from jax import lax
from jax.experimental import pallas as pl
from jax.experimental.pallas import tpu as pltpu
from jax.sharding import PartitionSpec as P

ITERS = 4
SUB = 4
CATS = 5
LAYERS = 8
ROWS = 128
COLS = 256
CHUNK = 8
DEEP = 8
FIELDS = 10
WIDE = COLS + 128
TALL = ROWS + 4 * DEEP
BAND = 24

FREEZING = -1.8
K_BASE = 2.03
K_GAIN = 0.47
K_SNOW = 0.31
ROOT = K_BASE / K_GAIN


def inverse(x):
    return 1.0 / x


def column(temps, thick, snow, air):
    depth = thick * (1.0 / (LAYERS - 1))
    square = depth * depth
    slope = square * (360.0 / K_GAIN)
    floor = square * (10.5 / K_GAIN)
    inv_depth = inverse(depth)
    snow_res = snow * inv_depth * (K_GAIN / K_SNOW)
    top_link = depth * (0.5 / K_GAIN) * inverse(snow * (0.5 / K_SNOW) + 0.05)
    snow_cap = snow * depth * (10.5 / K_GAIN)
    top_sum = snow_cap + top_link
    top_right = snow_cap * temps[0] + top_link * air
    current = list(temps)
    last = LAYERS - 1
    for repeat in range(ITERS):
        soft = [None] + [inverse(current[i] * current[i] + 1.0) for i in range(1, LAYERS)]
        conduct = [None] + [soft[i] + ROOT for i in range(1, LAYERS)]
        res = [snow_res] + [inverse(conduct[i]) for i in range(1, LAYERS)]
        cap = [None] + [slope * soft[i] + floor for i in range(1, LAYERS)]
        link = [res[i] + res[i + 1] for i in range(last)]
        ratio = [None] * LAYERS
        value = [None] * LAYERS
        down, down_flux = None, None
        for i in range(0, 4):
            total = top_sum if i == 0 else cap[i] + down
            right = top_right if i == 0 else cap[i] * temps[i] + down_flux
            ratio[i] = inverse(total * link[i] + 1.0)
            down = total * ratio[i]
            down_flux = right * ratio[i]
            value[i] = link[i] * down_flux
        up = conduct[last]
        up_flux = up * FREEZING
        for i in range(last, 4, -1):
            total = cap[i] + up
            right = cap[i] * temps[i] + up_flux
            ratio[i] = inverse(total * link[i - 1] + 1.0)
            up = total * ratio[i]
            up_flux = right * ratio[i]
            value[i] = link[i - 1] * up_flux
        renewed = [None] * LAYERS
        renewed[4] = (cap[4] * temps[4] + (down_flux + up_flux)) * inverse(cap[4] + (down + up))
        for i in range(3, -1, -1):
            if i > 0 or repeat == ITERS - 1:
                renewed[i] = value[i] + ratio[i] * renewed[i + 1]
        for i in range(5, LAYERS):
            renewed[i] = value[i] + ratio[i] * renewed[i - 1]
        current = renewed
    base = inverse(current[last] * current[last] + 1.0) + ROOT
    growth = (2.0 * K_GAIN * 0.0005) * (base * inv_depth) * (FREEZING - current[last])
    return current, growth


def draw_mask(list_ref, mask_ref):
    step = 512
    total = jnp.zeros((ROWS, COLS), jnp.float32)
    for start in range(0, list_ref.shape[1], step):
        cells = list_ref[:, start : start + step]
        row = lax.shift_right_arithmetic(cells, 8)
        col = jnp.where(cells >= 0, lax.bitwise_and(cells, 255), -1)
        rows = lax.broadcasted_iota(jnp.int32, (ROWS, step), 0) == row
        cols = lax.broadcasted_iota(jnp.int32, (COLS, step), 0) == col
        total = total + lax.dot_general(
            rows.astype(jnp.float32).astype(jnp.bfloat16),
            cols.astype(jnp.float32).astype(jnp.bfloat16),
            (((1,), (1,)), ((), ())),
            preferred_element_type=jnp.float32,
        )
    mask_ref[...] = total


def thermo_kernel(
    list_ref, temps_ref, thick_ref, snow_ref, area_ref, air_ref, heat_ref,
    vel_ref, stress_ref, wind_ref, ocean_ref, cells_ref,
    temps_out, thick_out, forcing_out, left_out, right_out, mask_ref,
):
    step = pl.program_id(0)

    @pl.when(step == 0)
    def _():
        draw_mask(list_ref, mask_ref)

    ice = mask_ref[pl.ds(pl.multiple_of(step * CHUNK, CHUNK), CHUNK), :]
    listed = ice > 0.5
    load = jnp.zeros((CHUNK, COLS), jnp.float32)
    area_total = jnp.zeros((CHUNK, COLS), jnp.float32)
    air = air_ref[...]
    heat = heat_ref[...]
    for cat in range(CATS):
        temps = [temps_ref[cat * LAYERS + i] for i in range(LAYERS)]
        thick = thick_ref[cat]
        current, growth = column(temps, thick, snow_ref[cat], air)
        for i in range(LAYERS):
            temps_out[cat * LAYERS + i] = jnp.where(listed, current[i], temps[i])
        thick_new = jnp.where(listed, thick + (growth - 0.0005 * heat), thick)
        thick_out[cat] = thick_new
        area = area_ref[cat]
        load = load + area * thick_new
        area_total = area_total + area
    load = ice * load
    strength = load * jnp.exp(-20.0 * (1.0 - area_total))
    fields = [vel_ref[0], vel_ref[1], stress_ref[0], stress_ref[1], stress_ref[2]]
    forcing = [
        wind_ref[0] + ocean_ref[0],
        wind_ref[1] + ocean_ref[1],
        cells_ref[...].astype(jnp.float32),
        strength,
        0.9 * load,
    ]
    for i, x in enumerate(forcing):
        forcing_out[i] = x
    lane = lax.broadcasted_iota(jnp.int32, (CHUNK, 128), 1)
    group = lax.shift_right_logical(lane, 3)
    left = jnp.zeros((CHUNK, 128), jnp.float32)
    right = jnp.zeros((CHUNK, 128), jnp.float32)
    for i, x in enumerate(fields + forcing):
        first = x[:, :128]
        final = x[:, COLS - 128 :]
        if i:
            first = pltpu.roll(first, 8 * i, axis=1)
        final = pltpu.roll(final, (8 * i + 8) % 128, axis=1)
        left = jnp.where(group == i, first, left)
        right = jnp.where(group == i, final, right)
    left_out[...] = left
    right_out[...] = right


def halo_tile(west, east, field, rows):
    lane = lax.broadcasted_iota(jnp.int32, (rows, 128), 1)
    east_side = pltpu.roll(east, (128 - 8 * field) % 128, axis=1) if field else east
    west_side = pltpu.roll(west, (120 - 8 * field) % 128, axis=1)
    zero = jnp.zeros((rows, 128), jnp.float32)
    return jnp.where(lane < DEEP, east_side, jnp.where(lane >= 128 - DEEP, west_side, zero))


def rows_kernel(spot_ref, vel_ref, stress_ref, forcing_ref, west_ref, east_ref, even_out, odd_out):
    even = lax.rem(spot_ref[0], 2) == 0
    for side, start in ((0, 0), (1, ROWS - DEEP)):
        out = odd_out if side == 0 else even_out
        other = even_out if side == 0 else odd_out
        west = west_ref[start : start + DEEP, :]
        east = east_ref[start : start + DEEP, :]
        for i in range(FIELDS):
            ref, at = (vel_ref, i) if i < 2 else (stress_ref, i - 2) if i < 5 else (forcing_ref, i - 5)
            inner = ref[at, start : start + DEEP, :]
            tile = halo_tile(west, east, i, DEEP)

            @pl.when(even)
            def _():
                out[i, :, :COLS] = inner
                out[i, :, COLS:] = tile

            @pl.when(jnp.logical_not(even))
            def _():
                other[i, :, :COLS] = inner
                other[i, :, COLS:] = tile


def flip(x):
    lane = 127 - lax.broadcasted_iota(jnp.int32, (DEEP, 128), 1)
    turned = jnp.take_along_axis(x, lane, axis=1)
    return jnp.concatenate([turned[i : i + 1] for i in range(DEEP - 1, -1, -1)], axis=0)


def motion_kernel(
    spot_ref, vel_ref, stress_ref, forcing_ref, west_ref, east_ref, even_ref, odd_ref,
    vel_out, stress_out, state_ref,
):
    spot = spot_ref[0]
    even = lax.rem(spot, 2) == 0
    top = spot == spot_ref[1] - 1
    low = slice(DEEP, 2 * DEEP)
    mid = slice(2 * DEEP, 2 * DEEP + ROWS)
    high = slice(2 * DEEP + ROWS, 3 * DEEP + ROWS)
    for i in range(FIELDS):
        ref, at = (vel_ref, i) if i < 2 else (stress_ref, i - 2) if i < 5 else (forcing_ref, i - 5)
        state_ref[i, mid, :COLS] = ref[at]
        state_ref[i, mid, COLS:] = halo_tile(west_ref[...], east_ref[...], i, ROWS)
        state_ref[i, :DEEP, :] = jnp.zeros((DEEP, WIDE), jnp.float32)
        state_ref[i, TALL - DEEP :, :] = jnp.zeros((DEEP, WIDE), jnp.float32)

        @pl.when(even)
        def _():
            state_ref[i, high, :] = even_ref[i]
            state_ref[i, low, :] = odd_ref[i]

        @pl.when(jnp.logical_not(even))
        def _():
            state_ref[i, low, :] = even_ref[i]

            @pl.when(top)
            def _():
                sign = -1.0 if i in (0, 1, 5, 6) else 1.0
                for tile, source in ((0, 1), (1, 0), (2, 2)):
                    state_ref[i, high, tile * 128 : tile * 128 + 128] = sign * flip(
                        odd_ref[i, :, source * 128 : source * 128 + 128]
                    )

            @pl.when(jnp.logical_not(top))
            def _():
                state_ref[i, high, :] = odd_ref[i]

    bands = (TALL - 2 * DEEP) // BAND

    def prepare(band, carry):
        start = pl.multiple_of(DEEP + band * BAND, 8)
        at = pl.ds(start, BAND)
        row = lax.broadcasted_iota(jnp.int32, (BAND, 128), 0) + (start - 2 * DEEP) + spot * ROWS
        whole = spot_ref[1] * ROWS
        row = jnp.where(row >= whole, 2 * whole - 1 - row, row)
        latitude = row.astype(jnp.float32) + 0.5
        turn = 1.4 * jnp.sin(0.5 * jnp.pi * (2.0 * latitude / whole.astype(jnp.float32) - 1.0))
        turn = jnp.concatenate([turn] * 3, axis=1)
        mass = state_ref[9, at, :]
        diagonal = mass + 1.0
        turning = turn * mass
        scale = state_ref[7, at, :] / (diagonal * diagonal + turning * turning)
        state_ref[7, at, :] = diagonal * scale
        state_ref[10, at, :] = turning * scale
        return carry

    lax.fori_loop(0, bands, prepare, 0)

    def shift_x(x):
        return pltpu.roll(x, WIDE - 1, axis=1) - pltpu.roll(x, 1, axis=1)

    def tall(field, start):
        return state_ref[field, pl.ds(pl.multiple_of(start - 8, 8), BAND + 16), :]

    def shift_y(x):
        return x[9 : 9 + BAND] - x[7 : 7 + BAND]

    def stresses(band, carry):
        start = pl.multiple_of(DEEP + band * BAND, 8)
        at = pl.ds(start, BAND)
        east = tall(0, start)
        north = tall(1, start)
        east_dx = shift_x(east[8 : 8 + BAND])
        north_dx = shift_x(north[8 : 8 + BAND])
        east_dy = shift_y(east)
        north_dy = shift_y(north)
        diverge = 0.5 * (east_dx + north_dy)
        tension = 0.5 * (east_dx - north_dy)
        shearing = 0.5 * (east_dy + north_dx)
        deform = diverge * diverge + 0.25 * (tension * tension + shearing * shearing) + 1.0
        strength = state_ref[8, at, :]
        bulk = strength * lax.rsqrt(deform)
        state_ref[2, at, :] = state_ref[2, at, :] * (2.0 / 3.0) + (bulk * diverge - strength) * (1.0 / 3.0)
        state_ref[3, at, :] = state_ref[3, at, :] * (2.0 / 3.0) + bulk * tension * (1.0 / 12.0)
        state_ref[4, at, :] = state_ref[4, at, :] * (2.0 / 3.0) + bulk * shearing * (1.0 / 24.0)
        return carry

    def momentum(band, carry):
        start = pl.multiple_of(DEEP + band * BAND, 8)
        at = pl.ds(start, BAND)
        total = tall(2, start)
        differ = tall(3, start)
        shear = tall(4, start)
        normal_dx = shift_x(0.5 * (total[8 : 8 + BAND] + differ[8 : 8 + BAND]))
        shear_dx = shift_x(shear[8 : 8 + BAND])
        shear_dy = shift_y(shear)
        normal_dy = shift_y(0.5 * (total - differ))
        mass = state_ref[9, at, :]
        right_east = mass * state_ref[0, at, :] + 0.5 * (normal_dx + shear_dy) + state_ref[5, at, :]
        right_north = mass * state_ref[1, at, :] + 0.5 * (shear_dx + normal_dy) + state_ref[6, at, :]
        straight = state_ref[7, at, :]
        turned = state_ref[10, at, :]
        state_ref[0, at, :] = straight * right_east + turned * right_north
        state_ref[1, at, :] = straight * right_north - turned * right_east
        return carry

    def subcycle(turn, carry):
        lax.fori_loop(0, bands, stresses, 0)
        lax.fori_loop(0, bands, momentum, 0)
        return carry

    lax.fori_loop(0, SUB, subcycle, 0)
    for i in range(2):
        vel_out[i] = state_ref[i, mid, :COLS]
    for i in range(3):
        stress_out[i] = state_ref[2 + i, mid, :COLS]


def per_device(
    layer_temps, ice_thick, snow_thick, ice_area, air_temp, ocean_heat,
    velocity, stress, wind_stress, ocean_current, ocean_mask, ice_cols,
):
    stacked = CATS * LAYERS
    f32 = jnp.float32

    def rows3(n):
        return pl.BlockSpec((n, CHUNK, COLS), lambda i: (0, i, 0))

    rows2 = pl.BlockSpec((CHUNK, COLS), lambda i: (i, 0))
    edge = pl.BlockSpec((CHUNK, 128), lambda i: (i, 0))
    listed = ice_cols.reshape(1, -1)
    temps_new, thick_new, forcing, left, right = pl.pallas_call(
        thermo_kernel,
        name="thermo",
        grid=(ROWS // CHUNK,),
        in_specs=[
            pl.BlockSpec(listed.shape, lambda i: (0, 0)),
            rows3(stacked), rows3(CATS), rows3(CATS), rows3(CATS), rows2, rows2,
            rows3(2), rows3(3), rows3(2), rows3(2), rows2,
        ],
        out_specs=[rows3(stacked), rows3(CATS), rows3(5), edge, edge],
        out_shape=[
            jax.ShapeDtypeStruct((stacked, ROWS, COLS), f32),
            jax.ShapeDtypeStruct((CATS, ROWS, COLS), f32),
            jax.ShapeDtypeStruct((5, ROWS, COLS), f32),
            jax.ShapeDtypeStruct((ROWS, 128), f32),
            jax.ShapeDtypeStruct((ROWS, 128), f32),
        ],
        scratch_shapes=[pltpu.VMEM((ROWS, COLS), f32)],
    )(
        listed, layer_temps, ice_thick, snow_thick, ice_area, air_temp, ocean_heat,
        velocity, stress, wind_stress, ocean_current, ocean_mask,
    )
    n_bx = lax.axis_size("bx")
    n_by = lax.axis_size("by")
    west = lax.ppermute(right, "bx", [(q, (q + 1) % n_bx) for q in range(n_bx)])
    east = lax.ppermute(left, "bx", [((q + 1) % n_bx, q) for q in range(n_bx)])

    spot = jnp.stack([lax.axis_index("by"), jnp.int32(n_by)]).astype(jnp.int32)
    smem = pl.BlockSpec(memory_space=pltpu.SMEM)
    vmem = pl.BlockSpec(memory_space=pltpu.VMEM)
    band = jax.ShapeDtypeStruct((FIELDS, DEEP, WIDE), f32)
    even_rows, odd_rows = pl.pallas_call(
        rows_kernel,
        name="edge_rows",
        in_specs=[smem] + [vmem] * 5,
        out_specs=[vmem, vmem],
        out_shape=[band, band],
    )(spot, velocity, stress, forcing, west, east)

    def at(p, q):
        return q * n_by + p

    even_pairs, odd_pairs = [], []
    for q in range(n_bx):
        for p in range(0, n_by, 2):
            even_pairs += [(at(p, q), at(p + 1, q)), (at(p + 1, q), at(p, q))]
        for p in range(1, n_by - 1, 2):
            odd_pairs += [(at(p, q), at(p + 1, q)), (at(p + 1, q), at(p, q))]
        odd_pairs.append((at(n_by - 1, q), at(n_by - 1, n_bx - 1 - q)))
    even_halo = lax.ppermute(even_rows, ("bx", "by"), even_pairs)
    odd_halo = lax.ppermute(odd_rows, ("bx", "by"), odd_pairs)

    velocity_new, stress_new = pl.pallas_call(
        motion_kernel,
        name="motion",
        in_specs=[smem] + [vmem] * 7,
        out_specs=[vmem, vmem],
        out_shape=[
            jax.ShapeDtypeStruct((2, ROWS, COLS), f32),
            jax.ShapeDtypeStruct((3, ROWS, COLS), f32),
        ],
        scratch_shapes=[pltpu.VMEM((FIELDS + 1, TALL, WIDE), f32)],
    )(spot, velocity, stress, forcing, west, east, even_halo, odd_halo)
    return temps_new, thick_new, velocity_new, stress_new


def solution(mesh):
    grid3 = P(None, "by", "bx")
    grid2 = P("by", "bx")
    in_specs = (
        grid3, grid3, grid3, grid3, grid2, grid2, grid3, grid3, grid3, grid3, grid2,
        P("by", "bx", None),
    )
    return jax.shard_map(
        per_device, mesh=mesh, in_specs=in_specs, out_specs=(grid3,) * 4, check_vma=False
    )
```

time: 360 us -> 56.5 us (0.16)
  the two profiles are of different devices: /device:TPU:14 before, /device:TPU:25 now
where the time goes in v1:
time: 56.5 us; the launch traced here: 55.9 us
  Pallas kernels  35 us (62%)
  starting transfers between devices  14.6 us (26%)
  waiting for transfers between devices  3.62 us (6%)
  local copies, waits for them, and re-layouts  1.3 us (2%)
  between operations  0.67 us (1%)
  other arithmetic  0.61 us (1%)
    pallas_call x1, Pallas kernels, per_device(): pl.pallas_call(thermo_kernel, name='thermo', grid=(ROWS // CHUNK,), in_sp...  20.7 us
    pallas_call x1, Pallas kernels, per_device(): pl.pallas_call(motion_kernel, name='motion', in_specs=[smem] + [vmem] * 7...  10.9 us
    ppermute x1, starting transfers between devices, per_device(): odd_halo = lax.ppermute(odd_rows, ('bx', 'by'), odd_pairs)  7.01 us
    ppermute x1, starting transfers between devices, per_device(): east = lax.ppermute(left, 'bx', [((q + 1) % n_bx, q) for q in range(n_bx)])  4.82 us
    pallas_call x1, Pallas kernels, per_device(): pl.pallas_call(rows_kernel, name='edge_rows', in_specs=[smem] + [vmem] *...  3.44 us
    ppermute x1, waiting for transfers between devices, per_device(): odd_halo = lax.ppermute(odd_rows, ('bx', 'by'), odd_pairs)  2.44 us
    ppermute x1, starting transfers between devices, per_device(): even_halo = lax.ppermute(even_rows, ('bx', 'by'), even_pairs)  1.53 us
    unnamed x8, local copies, waits for them, and re-layouts  1.3 us
  transfers between devices with their start and end apart: 4, of which 2 were waited for; matrix products, arithmetic and copies ran while one was open for 1% of the time, Pallas kernels for 0%

profile of v1, /device:TPU:25, one launch (start us, length us, event | category | flops | bytes accessed | tf_op | source)
XLA Modules:
  0.0 55.9 jit_solution(8722775764286853892)
XLA Ops:
  0.6 20.7 %thermo.1 = (f32[40,128,256]{2,1,0:T(8,128)}, f32[5,128,256]{2,1,0:T(8,128)}, f32[5,128,256]{2,1,0:T(8,128)}, f32[128,128]{1,0:T(8,128)}, f32[128,128]{1,0:T(8,128)}) custom-call(s32[1,6144]{1,0:T(1,128)} %bitcast.2, f32[40,128,256]{2,1,0:T(8,128)} %temps_ref.1, f32[5,128,256]{2,1,0:T(8,128)} %thick_ref.1, f32[5,128,256]{2,1,0:T(8,128)} %snow_ref.1, ...), custom_call_target="tpu_custom_call" | custom-call | tf_op jit(solution)/shard_map/thermo/pallas_call | solution.py:326
  21.4 1.3 %collective-permute-start = (f32[128,128]{1,0:T(8,128)}, f32[128,128]{1,0:T(8,128)S(1)}, u32[]{:S(2)}, u32[]{:S(2)}) collective-permute-start(f32[128,128]{1,0:T(8,128)} %get-tuple-element.16), channel_id=1, source_target_pairs={{0,8},{8,16},{16,24},{24,32},{32,40},{40,48},{48,56},{56,64},{64,7... | collective-permute-start | bytes 196616 | tf_op jit(solution)/shard_map/ppermute | solution.py:350
  22.6 4.8 %collective-permute-start.1 = (f32[128,128]{1,0:T(8,128)}, f32[128,128]{1,0:T(8,128)S(1)}, u32[]{:S(2)}, u32[]{:S(2)}) collective-permute-start(f32[128,128]{1,0:T(8,128)} %get-tuple-element.17), channel_id=1, source_target_pairs={{8,0},{16,8},{24,16},{32,24},{40,32},{48,40},{56,48},{64,56},{72,6... | collective-permute-start | bytes 196616 | tf_op jit(solution)/shard_map/ppermute | solution.py:351
  27.5 0.6 %pad_add_fusion.spot_ref = s32[2]{0:T(128)} fusion(s32[1]{0:T(128)} %constant.1.clone.1, s32[1]{0:T(128)} %bitcast.1), kind=kLoop, calls=%fused_computation | loop fusion | flops 2 | bytes 16 | tf_op jit(solution)/shard_map/stack | solution.py:353
  28.1 1.2 %collective-permute-done.west_ref = f32[128,128]{1,0:T(8,128)S(1)} collective-permute-done((f32[128,128]{1,0:T(8,128)}, f32[128,128]{1,0:T(8,128)S(1)}, u32[]{:S(2)}, u32[]{:S(2)}) %collective-permute-start) | collective-permute-done | bytes 65568 | tf_op jit(solution)/shard_map/ppermute | solution.py:350
  29.3 0.0 copy-start
  29.3 0.0 collective-permute-done.1.east_ref
  29.3 0.0 copy-start.1
  29.3 0.6 %copy-done = f32[128,128]{1,0:T(8,128)} copy-done((f32[128,128]{1,0:T(8,128)}, f32[128,128]{1,0:T(8,128)S(1)}, u32[]{:S(2)}) %copy-start) | copy-done | bytes 65560
  29.9 0.0 copy-done.1
  29.9 3.4 %edge_rows.1 = (f32[10,8,384]{2,1,0:T(8,128)}, f32[10,8,384]{2,1,0:T(8,128)}) custom-call(s32[2]{0:T(128)} %pad_add_fusion.spot_ref, f32[2,128,256]{2,1,0:T(8,128)} %vel_ref.5, f32[3,128,256]{2,1,0:T(8,128)} %stress_ref.5, f32[5,128,256]{2,1,0:T(8,128)} %get-tuple-element.15.forcing_ref, f32[128,128]{1,0:T(8,128)} %copy-done, f32[128,128]{1,0:T(8,128)} %copy-done.1), custom_call_target="tpu_custom_call" | custom-call | tf_op jit(solution)/shard_map/edge_rows/pallas_call | solution.py:357
  33.3 1.5 %collective-permute-start.2 = (f32[10,8,384]{2,1,0:T(8,128)}, f32[10,8,384]{2,1,0:T(8,128)S(1)}, u32[]{:S(2)}, u32[]{:S(2)}) collective-permute-start(f32[10,8,384]{2,1,0:T(8,128)} %get-tuple-element.18), channel_id=1, source_target_pairs={{0,1},{1,0},{2,3},{3,2},{4,5},{5,4},{6,7},{7,6},{8,9},{9,8},{10,11... | collective-permute-start | bytes 368648 | tf_op jit(solution)/shard_map/ppermute | solution.py:375
  34.9 7.0 %collective-permute-start.3 = (f32[10,8,384]{2,1,0:T(8,128)}, f32[10,8,384]{2,1,0:T(8,128)S(1)}, u32[]{:S(2)}, u32[]{:S(2)}) collective-permute-start(f32[10,8,384]{2,1,0:T(8,128)} %get-tuple-element.19), channel_id=1, source_target_pairs={{1,2},{2,1},{3,4},{4,3},{5,6},{6,5},{7,127},{9,10},{10,9},{11,12},... | collective-permute-start | bytes 368648 | tf_op jit(solution)/shard_map/ppermute | solution.py:376
  41.9 0.0 collective-permute-done.2.even_ref
  41.9 0.0 copy-start.2
  41.9 2.4 %collective-permute-done.3.odd_ref = f32[10,8,384]{2,1,0:T(8,128)S(1)} collective-permute-done((f32[10,8,384]{2,1,0:T(8,128)}, f32[10,8,384]{2,1,0:T(8,128)S(1)}, u32[]{:S(2)}, u32[]{:S(2)}) %collective-permute-start.3) | collective-permute-done | bytes 122912 | tf_op jit(solution)/shard_map/ppermute | solution.py:376
  44.4 0.0 copy-done.2
  44.4 0.0 copy-start.3
  44.4 0.6 %copy-done.3 = f32[10,8,384]{2,1,0:T(8,128)} copy-done((f32[10,8,384]{2,1,0:T(8,128)}, f32[10,8,384]{2,1,0:T(8,128)S(1)}, u32[]{:S(2)}) %copy-start.3) | copy-done | bytes 122904
  45.0 10.9 %motion.1 = (f32[2,128,256]{2,1,0:T(8,128)}, f32[3,128,256]{2,1,0:T(8,128)}) custom-call(s32[2]{0:T(128)} %pad_add_fusion.spot_ref, f32[2,128,256]{2,1,0:T(8,128)} %vel_ref.5, f32[3,128,256]{2,1,0:T(8,128)} %stress_ref.5, f32[5,128,256]{2,1,0:T(8,128)} %get-tuple-element.15.forcing_ref, f32[128,128]{1,0:T(8,128)} %copy-done, f32[128,128]{1,0:T(8,128)} %copy-done.1, ...), custom_call_target="tpu_custom_call" | custom-call | tf_op jit(solution)/shard_map/motion/pallas_call | solution.py:378
Async XLA Ops:
  21.4 7.9 %collective-permute-start = (f32[128,128]{1,0:T(8,128)}, f32[128,128]{1,0:T(8,128)S(1)}, u32[]{:S(2)}, u32[]{:S(2)}) collective-permute-start(f32[128,128]{1,0:T(8,128)} %get-tuple-element.16), channel_id=1, source_target_pairs={{0,8},{8,16},{16,24},{24,32},{32,40},{40,48},{48,56},{56,64},{64,7... | collective-permute-start | bytes 196616 | tf_op jit(solution)/shard_map/ppermute | solution.py:350
  22.6 6.6 %collective-permute-start.1 = (f32[128,128]{1,0:T(8,128)}, f32[128,128]{1,0:T(8,128)S(1)}, u32[]{:S(2)}, u32[]{:S(2)}) collective-permute-start(f32[128,128]{1,0:T(8,128)} %get-tuple-element.17), channel_id=1, source_target_pairs={{8,0},{16,8},{24,16},{32,24},{40,32},{48,40},{56,48},{64,56},{72,6... | collective-permute-start | bytes 196616 | tf_op jit(solution)/shard_map/ppermute | solution.py:351
  29.3 0.6 %copy-start = (f32[128,128]{1,0:T(8,128)}, f32[128,128]{1,0:T(8,128)S(1)}, u32[]{:S(2)}) copy-start(f32[128,128]{1,0:T(8,128)S(1)} %collective-permute-done.west_ref) | copy-start | bytes 196612
  29.3 0.6 %copy-start.1 = (f32[128,128]{1,0:T(8,128)}, f32[128,128]{1,0:T(8,128)S(1)}, u32[]{:S(2)}) copy-start(f32[128,128]{1,0:T(8,128)S(1)} %collective-permute-done.1.east_ref) | copy-start | bytes 196612
  33.3 8.6 %collective-permute-start.2 = (f32[10,8,384]{2,1,0:T(8,128)}, f32[10,8,384]{2,1,0:T(8,128)S(1)}, u32[]{:S(2)}, u32[]{:S(2)}) collective-permute-start(f32[10,8,384]{2,1,0:T(8,128)} %get-tuple-element.18), channel_id=1, source_target_pairs={{0,1},{1,0},{2,3},{3,2},{4,5},{5,4},{6,7},{7,6},{8,9},{9,8},{10,11... | collective-permute-start | bytes 368648 | tf_op jit(solution)/shard_map/ppermute | solution.py:375
  34.9 9.5 %collective-permute-start.3 = (f32[10,8,384]{2,1,0:T(8,128)}, f32[10,8,384]{2,1,0:T(8,128)S(1)}, u32[]{:S(2)}, u32[]{:S(2)}) collective-permute-start(f32[10,8,384]{2,1,0:T(8,128)} %get-tuple-element.19), channel_id=1, source_target_pairs={{1,2},{2,1},{3,4},{4,3},{5,6},{6,5},{7,127},{9,10},{10,9},{11,12},... | collective-permute-start | bytes 368648 | tf_op jit(solution)/shard_map/ppermute | solution.py:376
  41.9 2.5 %copy-start.2 = (f32[10,8,384]{2,1,0:T(8,128)}, f32[10,8,384]{2,1,0:T(8,128)S(1)}, u32[]{:S(2)}) copy-start(f32[10,8,384]{2,1,0:T(8,128)S(1)} %collective-permute-done.2.even_ref) | copy-start | bytes 368644
  44.4 0.7 %copy-start.3 = (f32[10,8,384]{2,1,0:T(8,128)}, f32[10,8,384]{2,1,0:T(8,128)S(1)}, u32[]{:S(2)}) copy-start(f32[10,8,384]{2,1,0:T(8,128)S(1)} %collective-permute-done.3.odd_ref) | copy-start | bytes 368644

commit v2 on v1

v2 whole, which is shorter than its diff:
```python
import jax
import jax.numpy as jnp
from jax import lax
from jax.experimental import pallas as pl
from jax.experimental.pallas import tpu as pltpu
from jax.sharding import PartitionSpec as P

ITERS = 4
SUB = 4
CATS = 5
LAYERS = 8
ROWS = 128
COLS = 256
DEEP = 8
FIELDS = 10
TALL = ROWS + 4 * DEEP
BAND = 24
LANES = 128
TILES = 32
FLAT = TILES * 8
STACKED = CATS * LAYERS
KEPT = STACKED + CATS
GROUPS = 8

FREEZING = -1.8
K_BASE = 2.03
K_GAIN = 0.47
K_SNOW = 0.31
ROOT = K_BASE / K_GAIN


def inverse(x):
    return 1.0 / x


def column(temps, thick, snow, air):
    depth = thick * (1.0 / (LAYERS - 1))
    square = depth * depth
    slope = square * (360.0 / K_GAIN)
    floor = square * (10.5 / K_GAIN)
    inv_depth = inverse(depth)
    snow_res = snow * inv_depth * (K_GAIN / K_SNOW)
    top_link = depth * (0.5 / K_GAIN) * inverse(snow * (0.5 / K_SNOW) + 0.05)
    snow_cap = snow * depth * (10.5 / K_GAIN)
    top_sum = snow_cap + top_link
    top_right = snow_cap * temps[0] + top_link * air
    current = list(temps)
    last = LAYERS - 1
    for repeat in range(ITERS):
        soft = [None] + [inverse(current[i] * current[i] + 1.0) for i in range(1, LAYERS)]
        conduct = [None] + [soft[i] + ROOT for i in range(1, LAYERS)]
        res = [snow_res] + [inverse(conduct[i]) for i in range(1, LAYERS)]
        cap = [None] + [slope * soft[i] + floor for i in range(1, LAYERS)]
        link = [res[i] + res[i + 1] for i in range(last)]
        ratio = [None] * LAYERS
        value = [None] * LAYERS
        down, down_flux = None, None
        for i in range(0, 4):
            total = top_sum if i == 0 else cap[i] + down
            right = top_right if i == 0 else cap[i] * temps[i] + down_flux
            ratio[i] = inverse(total * link[i] + 1.0)
            down = total * ratio[i]
            down_flux = right * ratio[i]
            value[i] = link[i] * down_flux
        up = conduct[last]
        up_flux = up * FREEZING
        for i in range(last, 4, -1):
            total = cap[i] + up
            right = cap[i] * temps[i] + up_flux
            ratio[i] = inverse(total * link[i - 1] + 1.0)
            up = total * ratio[i]
            up_flux = right * ratio[i]
            value[i] = link[i - 1] * up_flux
        renewed = [None] * LAYERS
        renewed[4] = (cap[4] * temps[4] + (down_flux + up_flux)) * inverse(cap[4] + (down + up))
        for i in range(3, -1, -1):
            if i > 0 or repeat == ITERS - 1:
                renewed[i] = value[i] + ratio[i] * renewed[i + 1]
        for i in range(5, LAYERS):
            renewed[i] = value[i] + ratio[i] * renewed[i - 1]
        current = renewed
    base = inverse(current[last] * current[last] + 1.0) + ROOT
    growth = (2.0 * K_GAIN * 0.0005) * (base * inv_depth) * (FREEZING - current[last])
    return current, growth


def draw_mask(list_ref):
    step = 512
    total = jnp.zeros((FLAT, LANES), jnp.float32)
    row_iota = lax.broadcasted_iota(jnp.int32, (FLAT, step), 0).astype(jnp.float32).astype(jnp.bfloat16)
    lane_iota = lax.broadcasted_iota(jnp.int32, (LANES, step), 0).astype(jnp.float32).astype(jnp.bfloat16)
    one = jnp.bfloat16(1.0)
    zero = jnp.bfloat16(0.0)
    for start in range(0, list_ref.shape[1], step):
        cells = list_ref[:, start : start + step]
        row = lax.shift_right_arithmetic(cells, 8) + (lax.bitwise_and(cells, 128))
        row = jnp.where(cells >= 0, row, -1).astype(jnp.float32).astype(jnp.bfloat16)
        lane = lax.bitwise_and(cells, 127).astype(jnp.float32).astype(jnp.bfloat16)
        total = total + lax.dot_general(
            jnp.where(row_iota == row, one, zero),
            jnp.where(lane_iota == lane, one, zero),
            (((1,), (1,)), ((), ())),
            preferred_element_type=jnp.float32,
        )
    return total


def index_cells(list_ref, mask_ref, base_ref, count_ref, inverse_ref, table_ref):
    mask = draw_mask(list_ref)
    mask_ref[...] = mask
    small = mask.astype(jnp.bfloat16)
    before = lax.broadcasted_iota(jnp.int32, (LANES, LANES), 0) < lax.broadcasted_iota(jnp.int32, (LANES, LANES), 1)
    before = before.astype(jnp.float32).astype(jnp.bfloat16)
    prefix = jnp.dot(small, before, preferred_element_type=jnp.float32).astype(jnp.int32)
    count = jnp.dot(small, jnp.ones((LANES, LANES), jnp.bfloat16), preferred_element_type=jnp.float32).astype(jnp.int32)
    count_ref[...] = count
    lane = lax.broadcasted_iota(jnp.int32, (8, LANES), 1)
    running = jnp.zeros((8, LANES), jnp.int32)
    bases = jnp.zeros((8, LANES), jnp.int32)
    ends = jnp.zeros((8, LANES), jnp.int32)
    for t in range(TILES):
        base_ref[8 * t : 8 * t + 8, :] = running
        bases = jnp.where(lane == t, running, bases)
        running = running + count[8 * t : 8 * t + 8]
        ends = jnp.where(lane == t, running, ends)
    wide_lane = lax.broadcasted_iota(jnp.int32, (FLAT, LANES), 1)
    moved = jnp.where(mask > 0.5, (wide_lane - prefix) * 256 + wide_lane, 0)
    for bit in range(7):
        probe = 256 << bit
        near = pltpu.roll(moved, LANES - (1 << bit), axis=1)
        moved = jnp.where(
            lax.bitwise_and(near, probe) != 0,
            near,
            jnp.where(lax.bitwise_and(moved, probe) != 0, 0, moved),
        )
    inverse_ref[...] = lax.bitwise_and(moved, 127)
    place = prefix + base_ref[...]
    base_min = jnp.min(bases, axis=0, keepdims=True)
    end_max = jnp.max(ends, axis=0, keepdims=True)
    used = lax.broadcasted_iota(jnp.int32, (TILES, LANES), 1) < TILES
    level = lax.broadcasted_iota(jnp.int32, (TILES, LANES), 0) * LANES
    first = jnp.sum(jnp.where(jnp.logical_and(used, end_max <= level), 1.0, 0.0), axis=1, keepdims=True)
    final = jnp.sum(jnp.where(jnp.logical_and(used, base_min < level + LANES), 1.0, 0.0), axis=1, keepdims=True)
    spread = lax.broadcasted_iota(jnp.int32, (TILES, LANES), 1)
    table_ref[:TILES, :] = jnp.where(spread == 0, first, final).astype(jnp.int32)
    top = lax.broadcasted_iota(jnp.int32, (8, LANES), 0)
    table_ref[TILES:, :] = jnp.where(top == 0, base_min, end_max)
    return place


def thermo_kernel(
    list_ref, temps_hbm, thick_hbm, snow_hbm, area_hbm, air_hbm, heat_hbm,
    vel_hbm, stress_hbm, wind_hbm, ocean_hbm, cells_hbm,
    temps_out, thick_out, forcing_out, left_out, right_out,
    kept_ref, snow_ref, area_ref, single_ref, moving_ref, drive_ref, cells_ref, forcing_ref,
    mask_ref, base_ref, count_ref, inverse_ref, place_ref, table_ref, gathered_ref, result_ref,
    plan_ref, in_sem, out_sem, table_sem,
):
    halves = ((0, slice(0, LANES), slice(0, ROWS)), (1, slice(LANES, COLS), slice(ROWS, FLAT)))
    copies = []
    order = 0
    for source, target in (
        (temps_hbm, kept_ref.at[:STACKED]),
        (thick_hbm, kept_ref.at[STACKED:]),
        (snow_hbm, snow_ref),
        (air_hbm, single_ref.at[0]),
        (heat_hbm, single_ref.at[1]),
        (area_hbm, area_ref),
        (vel_hbm, moving_ref.at[0:2]),
        (stress_hbm, moving_ref.at[2:5]),
        (wind_hbm, drive_ref.at[0:2]),
        (ocean_hbm, drive_ref.at[2:4]),
        (cells_hbm, cells_ref),
    ):
        for half, span, rows in halves:
            if len(source.shape) == 3:
                copy = pltpu.make_async_copy(source.at[:, :, span], target.at[:, rows, :], in_sem.at[order])
            else:
                copy = pltpu.make_async_copy(source.at[:, span], target.at[rows, :], in_sem.at[order])
            copy.start()
            copies.append(copy)
            order += 1

    place_ref[...] = index_cells(list_ref, mask_ref, base_ref, count_ref, inverse_ref, table_ref)
    plan = pltpu.make_async_copy(table_ref, plan_ref, table_sem)
    plan.start()
    for copy in copies:
        copy.wait()
    plan.wait()
    lane = lax.broadcasted_iota(jnp.int32, (8, LANES), 1)

    def solve(level, carry):
        begin = plan_ref[level, 0]
        end = plan_ref[level, 1]

        def gather(turn, inner):
            picks = []
            for offset in range(4):
                tile = jnp.minimum(begin + turn * 4 + offset, TILES - 1)
                at = pl.ds(pl.multiple_of(tile * 8, 8), 8)
                rank = lane + level * LANES - base_ref[at, :]
                inside = jnp.logical_and(rank >= 0, rank < count_ref[at, :])
                rank = jnp.where(inside, rank, 0)
                spot = jnp.take_along_axis(inverse_ref[at, :], rank, axis=1)
                picks.append((at, inside, spot))
            planes = [(kept_ref, p) for p in range(KEPT)]
            planes += [(snow_ref, p) for p in range(CATS)] + [(single_ref, 0), (single_ref, 1)]
            for number, (ref, p) in enumerate(planes):
                value = gathered_ref[number]
                for at, inside, spot in picks:
                    value = jnp.where(inside, jnp.take_along_axis(ref[p, at, :], spot, axis=1), value)
                gathered_ref[number] = value
            return inner

        lax.fori_loop(0, lax.div(end - begin + 3, 4), gather, 0)
        air = gathered_ref[KEPT + CATS]
        heat = gathered_ref[KEPT + CATS + 1]
        for cat in range(CATS):
            temps = [gathered_ref[cat * LAYERS + i] for i in range(LAYERS)]
            thick = gathered_ref[STACKED + cat]
            current, growth = column(temps, thick, gathered_ref[KEPT + cat], air)
            for i in range(LAYERS):
                result_ref[level, cat * LAYERS + i] = current[i]
            result_ref[level, STACKED + cat] = thick + (growth - 0.0005 * heat)
        return carry

    levels = lax.div(plan_ref[TILES + 1, TILES - 1] + (LANES - 1), LANES)
    lax.fori_loop(0, levels, solve, 0)

    def spread(tile, carry):
        at = pl.ds(pl.multiple_of(tile * 8, 8), 8)
        first = lax.div(plan_ref[TILES, tile], LANES)
        final = lax.div(plan_ref[TILES + 1, tile] + (LANES - 1), LANES)
        place = place_ref[at, :]
        ice = mask_ref[at, :]
        level = jnp.where(ice > 0.5, lax.shift_right_logical(place, 7), -1)
        spot = lax.bitwise_and(place, LANES - 1)

        def fill(turn, inner):
            low = jnp.minimum(first + 2 * turn, TILES - 1)
            high = jnp.minimum(low + 1, TILES - 1)
            in_low = level == low
            in_high = level == high
            for p in range(KEPT):
                from_low = jnp.take_along_axis(result_ref[low, p], spot, axis=1)
                from_high = jnp.take_along_axis(result_ref[high, p], spot, axis=1)
                kept_ref[p, at, :] = jnp.where(in_low, from_low, jnp.where(in_high, from_high, kept_ref[p, at, :]))
            return inner

        lax.fori_loop(0, lax.div(final - first + 1, 2), fill, 0)
        load = jnp.zeros((8, LANES), jnp.float32)
        area_total = jnp.zeros((8, LANES), jnp.float32)
        for cat in range(CATS):
            area = area_ref[cat, at, :]
            load = load + area * kept_ref[STACKED + cat, at, :]
            area_total = area_total + area
        load = ice * load
        forcing_ref[0, at, :] = drive_ref[0, at, :] + drive_ref[2, at, :]
        forcing_ref[1, at, :] = drive_ref[1, at, :] + drive_ref[3, at, :]
        forcing_ref[2, at, :] = cells_ref[at, :].astype(jnp.float32)
        forcing_ref[3, at, :] = load * jnp.exp(-20.0 * (1.0 - area_total))
        forcing_ref[4, at, :] = 0.9 * load
        return carry

    def send_out(group):
        pieces = []
        per_half = GROUPS // 2
        height = ROWS // per_half
        half, inner = group // per_half, group % per_half
        span = slice(half * LANES, half * LANES + LANES)
        there = slice(inner * height, inner * height + height)
        here = slice(group * height, group * height + height)
        pieces.append(pltpu.make_async_copy(
            kept_ref.at[:STACKED, here, :], temps_out.at[:, there, span], out_sem.at[group, 0]))
        pieces.append(pltpu.make_async_copy(
            kept_ref.at[STACKED:, here, :], thick_out.at[:, there, span], out_sem.at[group, 1]))
        pieces.append(pltpu.make_async_copy(
            forcing_ref.at[:, here, :], forcing_out.at[:, there, span], out_sem.at[group, 2]))
        return pieces

    sent = []
    per_group = TILES // GROUPS
    for group in range(GROUPS):
        lax.fori_loop(group * per_group, group * per_group + per_group, spread, 0)
        for copy in send_out(group):
            copy.start()
            sent.append(copy)

    def pack(tile, carry):
        group = lax.shift_right_logical(lane, 3)
        for out_ref, half, push in ((left_out, 0, 0), (right_out, 1, 8)):
            at = pl.ds(pl.multiple_of(tile * 8 + half * ROWS, 8), 8)
            packed = jnp.zeros((8, LANES), jnp.float32)
            for i in range(FIELDS):
                x = moving_ref[i, at, :] if i < 5 else forcing_ref[i - 5, at, :]
                turn = (8 * i + push) % LANES
                if turn:
                    x = pltpu.roll(x, turn, axis=1)
                packed = jnp.where(group == i, x, packed)
            out_ref[pl.ds(pl.multiple_of(tile * 8, 8), 8), :] = packed
        return carry

    lax.fori_loop(0, ROWS // 8, pack, 0)
    for copy in sent:
        copy.wait()


def halo_tile(west, east, field, rows):
    lane = lax.broadcasted_iota(jnp.int32, (rows, LANES), 1)
    east_side = pltpu.roll(east, (LANES - 8 * field) % LANES, axis=1) if field else east
    west_side = pltpu.roll(west, (120 - 8 * field) % LANES, axis=1)
    zero = jnp.zeros((rows, LANES), jnp.float32)
    return jnp.where(lane < DEEP, east_side, jnp.where(lane >= LANES - DEEP, west_side, zero))


def rows_kernel(
    spot_ref, vel_low, stress_low, forcing_low, west_low, east_low,
    vel_high, stress_high, forcing_high, west_high, east_high, even_out, odd_out,
):
    even = lax.rem(spot_ref[0], 2) == 0

    def fill(to_low, to_high):
        for out, vel_ref, stress_ref, forcing_ref, west_ref, east_ref in (
            (to_low, vel_low, stress_low, forcing_low, west_low, east_low),
            (to_high, vel_high, stress_high, forcing_high, west_high, east_high),
        ):
            for i in range(FIELDS):
                ref, at = (vel_ref, i) if i < 2 else (stress_ref, i - 2) if i < 5 else (forcing_ref, i - 5)
                out[i, 0] = ref[at, :, :LANES]
                out[i, 1] = ref[at, :, LANES:]
                out[i, 2] = halo_tile(west_ref[...], east_ref[...], i, DEEP)

    @pl.when(even)
    def _():
        fill(odd_out, even_out)

    @pl.when(jnp.logical_not(even))
    def _():
        fill(even_out, odd_out)


def flip(x):
    lane = (LANES - 1) - lax.broadcasted_iota(jnp.int32, (DEEP, LANES), 1)
    turned = jnp.take_along_axis(x, lane, axis=1)
    return jnp.concatenate([turned[i : i + 1] for i in range(DEEP - 1, -1, -1)], axis=0)


def motion_kernel(
    spot_ref, vel_hbm, stress_hbm, forcing_hbm, west_ref, east_ref, even_ref, odd_ref,
    vel_out, stress_out, state_ref, in_sem, out_sem,
):
    spot = spot_ref[0]
    even = lax.rem(spot, 2) == 0
    top = spot == spot_ref[1] - 1
    low = slice(DEEP, 2 * DEEP)
    mid = slice(2 * DEEP, 2 * DEEP + ROWS)
    high = slice(2 * DEEP + ROWS, 3 * DEEP + ROWS)
    copies = []
    for tile in range(2):
        span = slice(tile * LANES, tile * LANES + LANES)
        for number, (source, target) in enumerate((
            (vel_hbm, state_ref.at[0:2, tile, mid, :]),
            (stress_hbm, state_ref.at[2:5, tile, mid, :]),
            (forcing_hbm, state_ref.at[5:10, tile, mid, :]),
        )):
            copy = pltpu.make_async_copy(source.at[:, :, span], target, in_sem.at[tile, number])
            copy.start()
            copies.append(copy)
    blank = jnp.zeros((DEEP, LANES), jnp.float32)
    for i in range(FIELDS):
        for tile in range(3):
            state_ref[i, tile, :DEEP, :] = blank
            state_ref[i, tile, TALL - DEEP :, :] = blank
        state_ref[i, 2, mid, :] = halo_tile(west_ref[...], east_ref[...], i, ROWS)

    @pl.when(even)
    def _():
        for i in range(FIELDS):
            for tile in range(3):
                state_ref[i, tile, high, :] = even_ref[i, tile]
                state_ref[i, tile, low, :] = odd_ref[i, tile]

    @pl.when(jnp.logical_not(even))
    def _():
        for i in range(FIELDS):
            for tile in range(3):
                state_ref[i, tile, low, :] = even_ref[i, tile]
                state_ref[i, tile, high, :] = odd_ref[i, tile]

    @pl.when(top)
    def _():
        for i in range(FIELDS):
            for tile, source in ((0, 1), (1, 0), (2, 2)):
                turned = flip(odd_ref[i, source])
                state_ref[i, tile, high, :] = -turned if i in (0, 1, 5, 6) else turned

    for copy in copies:
        copy.wait()
    bands = (TALL - 2 * DEEP) // BAND
    lane = lax.broadcasted_iota(jnp.int32, (BAND, LANES), 1)
    is_first = lane == 0
    is_final = lane == LANES - 1

    def prepare(band, carry):
        start = pl.multiple_of(DEEP + band * BAND, 8)
        at = pl.ds(start, BAND)
        row = lax.broadcasted_iota(jnp.int32, (BAND, LANES), 0) + (start - 2 * DEEP) + spot * ROWS
        whole = spot_ref[1] * ROWS
        row = jnp.where(row >= whole, 2 * whole - 1 - row, row)
        latitude = row.astype(jnp.float32) + 0.5
        turn = 1.4 * jnp.sin(0.5 * jnp.pi * (2.0 * latitude / whole.astype(jnp.float32) - 1.0))
        for tile in range(3):
            mass = state_ref[9, tile, at, :]
            diagonal = mass + 1.0
            turning = turn * mass
            scale = state_ref[7, tile, at, :] / (diagonal * diagonal + turning * turning)
            state_ref[7, tile, at, :] = diagonal * scale
            state_ref[10, tile, at, :] = turning * scale
        return carry

    lax.fori_loop(0, bands, prepare, 0)

    def shift_x(parts):
        ahead = [pltpu.roll(x, LANES - 1, axis=1) for x in parts]
        behind = [pltpu.roll(x, 1, axis=1) for x in parts]
        return [
            jnp.where(is_final, ahead[(k + 1) % 3], ahead[k]) - jnp.where(is_first, behind[(k + 2) % 3], behind[k])
            for k in range(3)
        ]

    def shift_y(field, tile, start):
        return state_ref[field, tile, pl.ds(start + 1, BAND), :] - state_ref[field, tile, pl.ds(start - 1, BAND), :]

    def stresses(band, carry):
        start = pl.multiple_of(DEEP + band * BAND, 8)
        at = pl.ds(start, BAND)
        east_dx = shift_x([state_ref[0, k, at, :] for k in range(3)])
        north_dx = shift_x([state_ref[1, k, at, :] for k in range(3)])
        for k in range(3):
            north_dy = shift_y(1, k, start)
            diverge = 0.5 * (east_dx[k] + north_dy)
            tension = 0.5 * (east_dx[k] - north_dy)
            shearing = 0.5 * (shift_y(0, k, start) + north_dx[k])
            deform = diverge * diverge + 0.25 * (tension * tension + shearing * shearing) + 1.0
            strength = state_ref[8, k, at, :] * (1.0 / 3.0)
            bulk = strength * lax.rsqrt(deform)
            viscous = bulk * 0.25
            state_ref[2, k, at, :] = state_ref[2, k, at, :] * (2.0 / 3.0) + (bulk * diverge - strength)
            state_ref[3, k, at, :] = state_ref[3, k, at, :] * (2.0 / 3.0) + viscous * tension
            state_ref[4, k, at, :] = state_ref[4, k, at, :] * (2.0 / 3.0) + viscous * (0.5 * shearing)
        return carry

    def momentum(band, carry):
        start = pl.multiple_of(DEEP + band * BAND, 8)
        at = pl.ds(start, BAND)
        up = pl.ds(start + 1, BAND)
        down = pl.ds(start - 1, BAND)
        normal_dx = shift_x([state_ref[2, k, at, :] + state_ref[3, k, at, :] for k in range(3)])
        shear_dx = shift_x([state_ref[4, k, at, :] for k in range(3)])
        for k in range(3):
            shear_dy = shift_y(4, k, start)
            normal_dy = (state_ref[2, k, up, :] - state_ref[3, k, up, :]) - (
                state_ref[2, k, down, :] - state_ref[3, k, down, :]
            )
            mass = state_ref[9, k, at, :]
            right_east = mass * state_ref[0, k, at, :] + (0.25 * normal_dx[k] + 0.5 * shear_dy) + state_ref[5, k, at, :]
            right_north = mass * state_ref[1, k, at, :] + (0.5 * shear_dx[k] + 0.25 * normal_dy) + state_ref[6, k, at, :]
            straight = state_ref[7, k, at, :]
            turned = state_ref[10, k, at, :]
            state_ref[0, k, at, :] = straight * right_east + turned * right_north
            state_ref[1, k, at, :] = straight * right_north - turned * right_east
        return carry

    def subcycle(turn, carry):
        lax.fori_loop(0, bands, stresses, 0)
        lax.fori_loop(0, bands, momentum, 0)
        return carry

    lax.fori_loop(0, SUB, subcycle, 0)
    sent = []
    for tile in range(2):
        span = slice(tile * LANES, tile * LANES + LANES)
        for number, (source, target) in enumerate((
            (state_ref.at[0:2, tile, mid, :], vel_out),
            (state_ref.at[2:5, tile, mid, :], stress_out),
        )):
            copy = pltpu.make_async_copy(source, target.at[:, :, span], out_sem.at[tile, number])
            copy.start()
            sent.append(copy)
    for copy in sent:
        copy.wait()


def per_device(
    layer_temps, ice_thick, snow_thick, ice_area, air_temp, ocean_heat,
    velocity, stress, wind_stress, ocean_current, ocean_mask, ice_cols,
):
    f32 = jnp.float32
    i32 = jnp.int32
    smem = pl.BlockSpec(memory_space=pltpu.SMEM)
    vmem = pl.BlockSpec(memory_space=pltpu.VMEM)
    here = pl.BlockSpec(memory_space=pl.ANY)
    listed = ice_cols.reshape(1, -1)

    def flat(n, kind=f32):
        return pltpu.VMEM((n, FLAT, LANES), kind)

    one = pltpu.VMEM((FLAT, LANES), i32)
    temps_new, thick_new, forcing, left, right = pl.pallas_call(
        thermo_kernel,
        name="thermo",
        in_specs=[vmem] + [here] * 11,
        out_specs=[here, here, here, vmem, vmem],
        out_shape=[
            jax.ShapeDtypeStruct((STACKED, ROWS, COLS), f32),
            jax.ShapeDtypeStruct((CATS, ROWS, COLS), f32),
            jax.ShapeDtypeStruct((5, ROWS, COLS), f32),
            jax.ShapeDtypeStruct((ROWS, LANES), f32),
            jax.ShapeDtypeStruct((ROWS, LANES), f32),
        ],
        scratch_shapes=[
            flat(KEPT), flat(CATS), flat(CATS), flat(2), flat(5), flat(4), one, flat(5),
            pltpu.VMEM((FLAT, LANES), f32), one, one, one, one,
            pltpu.VMEM((TILES + 8, LANES), i32),
            pltpu.VMEM((KEPT + CATS + 2, 8, LANES), f32),
            pltpu.VMEM((TILES, KEPT, 8, LANES), f32),
            pltpu.SMEM((TILES + 8, LANES), i32),
            pltpu.SemaphoreType.DMA((22,)),
            pltpu.SemaphoreType.DMA((GROUPS, 3)),
            pltpu.SemaphoreType.DMA,
        ],
    )(
        listed, layer_temps, ice_thick, snow_thick, ice_area, air_temp, ocean_heat,
        velocity, stress, wind_stress, ocean_current, ocean_mask,
    )
    n_bx = lax.axis_size("bx")
    n_by = lax.axis_size("by")
    west = lax.ppermute(right, "bx", [(q, (q + 1) % n_bx) for q in range(n_bx)])
    east = lax.ppermute(left, "bx", [((q + 1) % n_bx, q) for q in range(n_bx)])

    spot = jnp.stack([lax.axis_index("by"), jnp.int32(n_by)]).astype(i32)
    band = jax.ShapeDtypeStruct((FIELDS, 3, DEEP, LANES), f32)

    def slab(n, block):
        return pl.BlockSpec((n, DEEP, COLS), lambda i: (0, block, 0))

    def edge(block):
        return pl.BlockSpec((DEEP, LANES), lambda i: (block, 0))

    final = ROWS // DEEP - 1
    halo = pl.BlockSpec((FIELDS, 3, DEEP, LANES), lambda i: (0, 0, 0, 0))
    even_rows, odd_rows = pl.pallas_call(
        rows_kernel,
        name="edge_rows",
        grid=(1,),
        in_specs=[smem]
        + [slab(2, 0), slab(3, 0), slab(5, 0), edge(0), edge(0)]
        + [slab(2, final), slab(3, final), slab(5, final), edge(final), edge(final)],
        out_specs=[halo, halo],
        out_shape=[band, band],
    )(spot, velocity, stress, forcing, west, east, velocity, stress, forcing, west, east)

    def at(p, q):
        return q * n_by + p

    even_pairs, odd_pairs = [], []
    for q in range(n_bx):
        for p in range(0, n_by, 2):
            even_pairs += [(at(p, q), at(p + 1, q)), (at(p + 1, q), at(p, q))]
        for p in range(1, n_by - 1, 2):
            odd_pairs += [(at(p, q), at(p + 1, q)), (at(p + 1, q), at(p, q))]
        odd_pairs.append((at(n_by - 1, q), at(n_by - 1, n_bx - 1 - q)))
    even_halo = lax.ppermute(even_rows, ("bx", "by"), even_pairs)
    odd_halo = lax.ppermute(odd_rows, ("bx", "by"), odd_pairs)

    velocity_new, stress_new = pl.pallas_call(
        motion_kernel,
        name="motion",
        in_specs=[smem] + [here] * 3 + [vmem] * 4,
        out_specs=[here, here],
        out_shape=[
            jax.ShapeDtypeStruct((2, ROWS, COLS), f32),
            jax.ShapeDtypeStruct((3, ROWS, COLS), f32),
        ],
        scratch_shapes=[
            pltpu.VMEM((FIELDS + 1, 3, TALL, LANES), f32),
            pltpu.SemaphoreType.DMA((2, 3)),
            pltpu.SemaphoreType.DMA((2, 2)),
        ],
    )(spot, velocity, stress, forcing, west, east, even_halo, odd_halo)
    return temps_new, thick_new, velocity_new, stress_new


def solution(mesh):
    grid3 = P(None, "by", "bx")
    grid2 = P("by", "bx")
    in_specs = (
        grid3, grid3, grid3, grid3, grid2, grid2, grid3, grid3, grid3, grid3, grid2,
        P("by", "bx", None),
    )
    return jax.shard_map(
        per_device, mesh=mesh, in_specs=in_specs, out_specs=(grid3,) * 4, check_vma=False
    )
```

time: 56.5 us -> 55.1 us (0.975)
  Pallas kernels: 35 us -> 32.7 us
  starting transfers between devices: 14.6 us -> 15.9 us
    pallas_call x3, Pallas kernels: 35 us -> 32.7 us  [the longest x1 21 us: per_device(): pl.pallas_call(thermo_kernel, name='thermo', in_specs=[vmem] + [here] * 1...]
    ppermute x1, starting transfers between devices: 1.28 us -> 3.22 us  [per_device(): west = lax.ppermute(right, 'bx', [(q, (q + 1) % n_bx) for q in range(n_bx)])]
    ppermute x1, starting transfers between devices: 4.82 us -> 4.12 us  [per_device(): east = lax.ppermute(left, 'bx', [((q + 1) % n_bx, q) for q in range(n_bx)])]
where the time goes in v2:
time: 55.1 us; the launch traced here: 54.8 us
  Pallas kernels  32.7 us (59%)
  starting transfers between devices  15.9 us (29%)
  waiting for transfers between devices  3.62 us (7%)
  local copies, waits for them, and re-layouts  1.3 us (2%)
  between operations  0.67 us (1%)
  other arithmetic  0.61 us (1%)
    pallas_call x1, Pallas kernels, per_device(): pl.pallas_call(thermo_kernel, name='thermo', in_specs=[vmem] + [here] * 1...  21 us
    pallas_call x1, Pallas kernels, per_device(): pl.pallas_call(motion_kernel, name='motion', in_specs=[smem] + [here] * 3...  10 us
    ppermute x1, starting transfers between devices, per_device(): odd_halo = lax.ppermute(odd_rows, ('bx', 'by'), odd_pairs)  7.01 us
    ppermute x1, starting transfers between devices, per_device(): east = lax.ppermute(left, 'bx', [((q + 1) % n_bx, q) for q in range(n_bx)])  4.12 us
    ppermute x1, starting transfers between devices, per_device(): west = lax.ppermute(right, 'bx', [(q, (q + 1) % n_bx) for q in range(n_bx)])  3.22 us
    ppermute x1, waiting for transfers between devices, per_device(): odd_halo = lax.ppermute(odd_rows, ('bx', 'by'), odd_pairs)  2.44 us
    pallas_call x1, Pallas kernels, per_device(): pl.pallas_call(rows_kernel, name='edge_rows', grid=(1,), in_specs=[smem]...  1.68 us
    ppermute x1, starting transfers between devices, per_device(): even_halo = lax.ppermute(even_rows, ('bx', 'by'), even_pairs)  1.54 us
  transfers between devices with their start and end apart: 4, of which 2 were waited for; matrix products, arithmetic and copies ran while one was open for 1% of the time, Pallas kernels for 0%

profile of v2, /device:TPU:25, one launch (start us, length us, event | category | flops | bytes accessed | tf_op | source)
XLA Modules:
  0.0 54.8 jit_solution(4389551803558596486)
XLA Ops:
  0.6 21.0 %thermo.1 = (f32[40,128,256]{2,1,0:T(8,128)}, f32[5,128,256]{2,1,0:T(8,128)}, f32[5,128,256]{2,1,0:T(8,128)}, f32[128,128]{1,0:T(8,128)}, f32[128,128]{1,0:T(8,128)}) custom-call(s32[1,6144]{1,0:T(1,128)} %bitcast.2, f32[40,128,256]{2,1,0:T(8,128)} %temps_hbm.1, f32[5,128,256]{2,1,0:T(8,128)} %thick_hbm.1, f32[5,128,256]{2,1,0:T(8,128)} %snow_hbm.1, ...), custom_call_target="tpu_custom_call" | custom-call | tf_op jit(solution)/shard_map/thermo/pallas_call | solution.py:509
  21.7 3.2 %collective-permute-start = (f32[128,128]{1,0:T(8,128)}, f32[128,128]{1,0:T(8,128)S(1)}, u32[]{:S(2)}, u32[]{:S(2)}) collective-permute-start(f32[128,128]{1,0:T(8,128)} %get-tuple-element.16), channel_id=1, source_target_pairs={{0,8},{8,16},{16,24},{24,32},{32,40},{40,48},{48,56},{56,64},{64,7... | collective-permute-start | bytes 196616 | tf_op jit(solution)/shard_map/ppermute | solution.py:538
  24.9 4.1 %collective-permute-start.1 = (f32[128,128]{1,0:T(8,128)}, f32[128,128]{1,0:T(8,128)S(1)}, u32[]{:S(2)}, u32[]{:S(2)}) collective-permute-start(f32[128,128]{1,0:T(8,128)} %get-tuple-element.17), channel_id=1, source_target_pairs={{8,0},{16,8},{24,16},{32,24},{40,32},{48,40},{56,48},{64,56},{72,6... | collective-permute-start | bytes 196616 | tf_op jit(solution)/shard_map/ppermute | solution.py:539
  29.0 0.6 %pad_add_fusion.spot_ref = s32[2]{0:T(128)} fusion(s32[1]{0:T(128)} %constant.1.clone.1, s32[1]{0:T(128)} %bitcast.1), kind=kLoop, calls=%fused_computation | loop fusion | flops 2 | bytes 16 | tf_op jit(solution)/shard_map/stack | solution.py:541
  29.6 1.2 %collective-permute-done.west_low.west_high.west_ref = f32[128,128]{1,0:T(8,128)S(1)} collective-permute-done((f32[128,128]{1,0:T(8,128)}, f32[128,128]{1,0:T(8,128)S(1)}, u32[]{:S(2)}, u32[]{:S(2)}) %collective-permute-start) | collective-permute-done | bytes 65568 | tf_op jit(solution)/shard_map/ppermute | solution.py:538
  30.8 0.0 copy-start
  30.8 0.0 collective-permute-done.1.east_low.east_high.east_ref
  30.8 0.0 copy-start.1
  30.8 0.6 %copy-done = f32[128,128]{1,0:T(8,128)} copy-done((f32[128,128]{1,0:T(8,128)}, f32[128,128]{1,0:T(8,128)S(1)}, u32[]{:S(2)}) %copy-start) | copy-done | bytes 65560
  31.4 0.0 copy-done.1
  31.5 1.7 %edge_rows.1 = (f32[10,3,8,128]{3,2,1,0:T(8,128)}, f32[10,3,8,128]{3,2,1,0:T(8,128)}) custom-call(s32[2]{0:T(128)} %pad_add_fusion.spot_ref, f32[2,128,256]{2,1,0:T(8,128)} %vel_hbm.3, f32[3,128,256]{2,1,0:T(8,128)} %stress_hbm.3, f32[5,128,256]{2,1,0:T(8,128)} %get-tuple-element.15.forcing_low.forcing_high.forcing_hbm, f32[128,128]{1,0:T(8,128)} %copy-done, ...), custom_call_target="tpu_custom_call" | custom-call | tf_op jit(solution)/shard_map/edge_rows/pallas_call | solution.py:552
  33.1 1.5 %collective-permute-start.2 = (f32[10,3,8,128]{3,2,1,0:T(8,128)}, f32[10,3,8,128]{3,2,1,0:T(8,128)S(1)}, u32[]{:S(2)}, u32[]{:S(2)}) collective-permute-start(f32[10,3,8,128]{3,2,1,0:T(8,128)} %get-tuple-element.18), channel_id=1, source_target_pairs={{0,1},{1,0},{2,3},{3,2},{4,5},{5,4},{6,7},{7,6},{8,9},{9,8},{10,11... | collective-permute-start | bytes 368648 | tf_op jit(solution)/shard_map/ppermute | solution.py:573
  34.7 7.0 %collective-permute-start.3 = (f32[10,3,8,128]{3,2,1,0:T(8,128)}, f32[10,3,8,128]{3,2,1,0:T(8,128)S(1)}, u32[]{:S(2)}, u32[]{:S(2)}) collective-permute-start(f32[10,3,8,128]{3,2,1,0:T(8,128)} %get-tuple-element.19), channel_id=1, source_target_pairs={{1,2},{2,1},{3,4},{4,3},{5,6},{6,5},{7,127},{9,10},{10,9},{11,12},... | collective-permute-start | bytes 368648 | tf_op jit(solution)/shard_map/ppermute | solution.py:574
  41.7 0.0 collective-permute-done.2.even_ref
  41.7 0.0 copy-start.2
  41.7 2.4 %collective-permute-done.3.odd_ref = f32[10,3,8,128]{3,2,1,0:T(8,128)S(1)} collective-permute-done((f32[10,3,8,128]{3,2,1,0:T(8,128)}, f32[10,3,8,128]{3,2,1,0:T(8,128)S(1)}, u32[]{:S(2)}, u32[]{:S(2)}) %collective-permute-start.3) | collective-permute-done | bytes 122912 | tf_op jit(solution)/shard_map/ppermute | solution.py:574
  44.2 0.0 copy-done.2
  44.2 0.0 copy-start.3
  44.2 0.6 %copy-done.3 = f32[10,3,8,128]{3,2,1,0:T(8,128)} copy-done((f32[10,3,8,128]{3,2,1,0:T(8,128)}, f32[10,3,8,128]{3,2,1,0:T(8,128)S(1)}, u32[]{:S(2)}) %copy-start.3) | copy-done | bytes 122904
  44.8 10.0 %motion.1 = (f32[2,128,256]{2,1,0:T(8,128)}, f32[3,128,256]{2,1,0:T(8,128)}) custom-call(s32[2]{0:T(128)} %pad_add_fusion.spot_ref, f32[2,128,256]{2,1,0:T(8,128)} %vel_hbm.3, f32[3,128,256]{2,1,0:T(8,128)} %stress_hbm.3, f32[5,128,256]{2,1,0:T(8,128)} %get-tuple-element.15.forcing_low.forcing_high.forcing_hbm, f32[128,128]{1,0:T(8,128)} %copy-done, ...), custom_call_target="tpu_custom_call" | custom-call | tf_op jit(solution)/shard_map/motion/pallas_call | solution.py:576
Async XLA Ops:
  21.7 9.1 %collective-permute-start = (f32[128,128]{1,0:T(8,128)}, f32[128,128]{1,0:T(8,128)S(1)}, u32[]{:S(2)}, u32[]{:S(2)}) collective-permute-start(f32[128,128]{1,0:T(8,128)} %get-tuple-element.16), channel_id=1, source_target_pairs={{0,8},{8,16},{16,24},{24,32},{32,40},{40,48},{48,56},{56,64},{64,7... | collective-permute-start | bytes 196616 | tf_op jit(solution)/shard_map/ppermute | solution.py:538
  24.9 5.9 %collective-permute-start.1 = (f32[128,128]{1,0:T(8,128)}, f32[128,128]{1,0:T(8,128)S(1)}, u32[]{:S(2)}, u32[]{:S(2)}) collective-permute-start(f32[128,128]{1,0:T(8,128)} %get-tuple-element.17), channel_id=1, source_target_pairs={{8,0},{16,8},{24,16},{32,24},{40,32},{48,40},{56,48},{64,56},{72,6... | collective-permute-start | bytes 196616 | tf_op jit(solution)/shard_map/ppermute | solution.py:539
  30.8 0.6 %copy-start = (f32[128,128]{1,0:T(8,128)}, f32[128,128]{1,0:T(8,128)S(1)}, u32[]{:S(2)}) copy-start(f32[128,128]{1,0:T(8,128)S(1)} %collective-permute-done.west_low.west_high.west_ref) | copy-start | bytes 196612
  30.8 0.6 %copy-start.1 = (f32[128,128]{1,0:T(8,128)}, f32[128,128]{1,0:T(8,128)S(1)}, u32[]{:S(2)}) copy-start(f32[128,128]{1,0:T(8,128)S(1)} %collective-permute-done.1.east_low.east_high.east_ref) | copy-start | bytes 196612
  33.1 8.6 %collective-permute-start.2 = (f32[10,3,8,128]{3,2,1,0:T(8,128)}, f32[10,3,8,128]{3,2,1,0:T(8,128)S(1)}, u32[]{:S(2)}, u32[]{:S(2)}) collective-permute-start(f32[10,3,8,128]{3,2,1,0:T(8,128)} %get-tuple-element.18), channel_id=1, source_target_pairs={{0,1},{1,0},{2,3},{3,2},{4,5},{5,4},{6,7},{7,6},{8,9},{9,8},{10,11... | collective-permute-start | bytes 368648 | tf_op jit(solution)/shard_map/ppermute | solution.py:573
  34.7 9.5 %collective-permute-start.3 = (f32[10,3,8,128]{3,2,1,0:T(8,128)}, f32[10,3,8,128]{3,2,1,0:T(8,128)S(1)}, u32[]{:S(2)}, u32[]{:S(2)}) collective-permute-start(f32[10,3,8,128]{3,2,1,0:T(8,128)} %get-tuple-element.19), channel_id=1, source_target_pairs={{1,2},{2,1},{3,4},{4,3},{5,6},{6,5},{7,127},{9,10},{10,9},{11,12},... | collective-permute-start | bytes 368648 | tf_op jit(solution)/shard_map/ppermute | solution.py:574
  41.7 2.5 %copy-start.2 = (f32[10,3,8,128]{3,2,1,0:T(8,128)}, f32[10,3,8,128]{3,2,1,0:T(8,128)S(1)}, u32[]{:S(2)}) copy-start(f32[10,3,8,128]{3,2,1,0:T(8,128)S(1)} %collective-permute-done.2.even_ref) | copy-start | bytes 368644
  44.2 0.7 %copy-start.3 = (f32[10,3,8,128]{3,2,1,0:T(8,128)}, f32[10,3,8,128]{3,2,1,0:T(8,128)S(1)}, u32[]{:S(2)}) copy-start(f32[10,3,8,128]{3,2,1,0:T(8,128)S(1)} %collective-permute-done.3.odd_ref) | copy-start | bytes 368644

commit v3 on v2

--- a/solution.py
+++ b/solution.py
@@ -14,13 +14,17 @@
 DEEP = 8
 FIELDS = 10
 TALL = ROWS + 4 * DEEP
-BAND = 24
+BAND = 144
 LANES = 128
 TILES = 32
 FLAT = TILES * 8
 STACKED = CATS * LAYERS
 KEPT = STACKED + CATS
-GROUPS = 8
+TEAM = 4
+PAIR = 2
+TURNS = TILES // (TEAM * PAIR)
+HEIGHT = FLAT // TURNS
+BLOCK = 13
 
 FREEZING = -1.8
 K_BASE = 2.03
@@ -105,7 +109,7 @@
     return total
 
 
-def index_cells(list_ref, mask_ref, base_ref, count_ref, inverse_ref, table_ref):
+def index_cells(list_ref, mask_ref, base_ref, count_ref, inverse_ref, place_ref, spot_ref):
     mask = draw_mask(list_ref)
     mask_ref[...] = mask
     small = mask.astype(jnp.bfloat16)
@@ -114,15 +118,14 @@
     prefix = jnp.dot(small, before, preferred_element_type=jnp.float32).astype(jnp.int32)
     count = jnp.dot(small, jnp.ones((LANES, LANES), jnp.bfloat16), preferred_element_type=jnp.float32).astype(jnp.int32)
     count_ref[...] = count
-    lane = lax.broadcasted_iota(jnp.int32, (8, LANES), 1)
-    running = jnp.zeros((8, LANES), jnp.int32)
-    bases = jnp.zeros((8, LANES), jnp.int32)
-    ends = jnp.zeros((8, LANES), jnp.int32)
+    most = jnp.zeros((8, LANES), jnp.int32)
+    running = most
     for t in range(TILES):
+        if t % TEAM == 0:
+            running = jnp.zeros((8, LANES), jnp.int32)
         base_ref[8 * t : 8 * t + 8, :] = running
-        bases = jnp.where(lane == t, running, bases)
         running = running + count[8 * t : 8 * t + 8]
-        ends = jnp.where(lane == t, running, ends)
+        most = jnp.maximum(most, running)
     wide_lane = lax.broadcasted_iota(jnp.int32, (FLAT, LANES), 1)
     moved = jnp.where(mask > 0.5, (wide_lane - prefix) * 256 + wide_lane, 0)
     for bit in range(7):
@@ -133,126 +136,121 @@
             near,
             jnp.where(lax.bitwise_and(moved, probe) != 0, 0, moved),
         )
-    inverse_ref[...] = lax.bitwise_and(moved, 127)
-    place = prefix + base_ref[...]
-    base_min = jnp.min(bases, axis=0, keepdims=True)
-    end_max = jnp.max(ends, axis=0, keepdims=True)
-    used = lax.broadcasted_iota(jnp.int32, (TILES, LANES), 1) < TILES
-    level = lax.broadcasted_iota(jnp.int32, (TILES, LANES), 0) * LANES
-    first = jnp.sum(jnp.where(jnp.logical_and(used, end_max <= level), 1.0, 0.0), axis=1, keepdims=True)
-    final = jnp.sum(jnp.where(jnp.logical_and(used, base_min < level + LANES), 1.0, 0.0), axis=1, keepdims=True)
-    spread = lax.broadcasted_iota(jnp.int32, (TILES, LANES), 1)
-    table_ref[:TILES, :] = jnp.where(spread == 0, first, final).astype(jnp.int32)
-    top = lax.broadcasted_iota(jnp.int32, (8, LANES), 0)
-    table_ref[TILES:, :] = jnp.where(top == 0, base_min, end_max)
-    return place
+    inverse = lax.bitwise_and(moved, LANES - 1)
+    inverse_ref[...] = inverse
+    base = base_ref[...]
+    place_ref[...] = jnp.where(mask > 0.5, prefix + base, -1)
+    lane = lax.broadcasted_iota(jnp.int32, (8, LANES), 1)
+    for t in range(TILES):
+        here = slice(8 * t, 8 * t + 8)
+        rank = lane - base_ref[here, :]
+        inside = jnp.logical_and(rank >= 0, rank < count[here])
+        spot = jnp.take_along_axis(inverse[here], jnp.where(inside, rank, 0), axis=1)
+        spot_ref[here, :] = jnp.where(inside, spot, -1)
+    return jnp.max(most)
+
+
+def gather_team(picks, kept_ref, snow_ref, single_ref, gathered_ref):
+    planes = [(kept_ref, p) for p in range(KEPT)]
+    planes += [(snow_ref, p) for p in range(CATS)] + [(single_ref, 0), (single_ref, 1)]
+    for start in range(0, len(planes), BLOCK):
+        block = planes[start : start + BLOCK]
+        values = [None] * len(block)
+        for at, spot in picks:
+            inside = spot >= 0
+            spot = jnp.maximum(spot, 0)
+            for k, (ref, p) in enumerate(block):
+                value = jnp.take_along_axis(ref[p, at, :], spot, axis=1)
+                values[k] = value if values[k] is None else jnp.where(inside, value, values[k])
+        for k, value in enumerate(values):
+            gathered_ref[start + k] = value
+
+
+def solve_team(gathered_ref, result_ref):
+    air = gathered_ref[KEPT + CATS]
+    heat = gathered_ref[KEPT + CATS + 1]
+    for cat in range(CATS):
+        temps = [gathered_ref[cat * LAYERS + i] for i in range(LAYERS)]
+        thick = gathered_ref[STACKED + cat]
+        current, growth = column(temps, thick, gathered_ref[KEPT + cat], air)
+        for i in range(LAYERS):
+            result_ref[cat * LAYERS + i] = current[i]
+        result_ref[STACKED + cat] = thick + (growth - 0.0005 * heat)
+
+
+def spread_team(tiles, level, place_ref, source_ref, result_ref, fresh_ref):
+    for at in tiles:
+        place = place_ref[at, :] - level * LANES
+        inside = jnp.logical_and(place >= 0, place < LANES)
+        spot = jnp.where(inside, place, 0)
+        for p in range(KEPT):
+            value = jnp.take_along_axis(result_ref[p], spot, axis=1)
+            fresh_ref[p, at, :] = jnp.where(inside, value, source_ref[p, at, :])
 
 
 def thermo_kernel(
     list_ref, temps_hbm, thick_hbm, snow_hbm, area_hbm, air_hbm, heat_hbm,
     vel_hbm, stress_hbm, wind_hbm, ocean_hbm, cells_hbm,
     temps_out, thick_out, forcing_out, left_out, right_out,
-    kept_ref, snow_ref, area_ref, single_ref, moving_ref, drive_ref, cells_ref, forcing_ref,
-    mask_ref, base_ref, count_ref, inverse_ref, place_ref, table_ref, gathered_ref, result_ref,
-    plan_ref, in_sem, out_sem, table_sem,
+    kept_ref, fresh_ref, snow_ref, area_ref, single_ref, moving_ref, drive_ref, cells_ref, forcing_ref,
+    mask_ref, base_ref, count_ref, inverse_ref, place_ref, spot_ref,
+    gathered_a, gathered_b, result_a, result_b, in_sem, out_sem,
 ):
-    halves = ((0, slice(0, LANES), slice(0, ROWS)), (1, slice(LANES, COLS), slice(ROWS, FLAT)))
-    copies = []
-    order = 0
-    for source, target in (
-        (temps_hbm, kept_ref.at[:STACKED]),
-        (thick_hbm, kept_ref.at[STACKED:]),
-        (snow_hbm, snow_ref),
-        (air_hbm, single_ref.at[0]),
-        (heat_hbm, single_ref.at[1]),
-        (area_hbm, area_ref),
-        (vel_hbm, moving_ref.at[0:2]),
-        (stress_hbm, moving_ref.at[2:5]),
-        (wind_hbm, drive_ref.at[0:2]),
-        (ocean_hbm, drive_ref.at[2:4]),
-        (cells_hbm, cells_ref),
-    ):
-        for half, span, rows in halves:
+    def fetch(turn):
+        half, inner = turn // (TURNS // 2), turn % (TURNS // 2)
+        span = slice(half * LANES, half * LANES + LANES)
+        there = slice(inner * HEIGHT, inner * HEIGHT + HEIGHT)
+        rows = slice(turn * HEIGHT, turn * HEIGHT + HEIGHT)
+        copies = []
+        for source, target in (
+            (temps_hbm, kept_ref.at[:STACKED]),
+            (thick_hbm, kept_ref.at[STACKED:]),
+            (snow_hbm, snow_ref),
+            (air_hbm, single_ref.at[0]),
+            (heat_hbm, single_ref.at[1]),
+            (area_hbm, area_ref),
+            (wind_hbm, drive_ref.at[0:2]),
+            (ocean_hbm, drive_ref.at[2:4]),
+            (cells_hbm, cells_ref),
+            (vel_hbm, moving_ref.at[0:2]),
+            (stress_hbm, moving_ref.at[2:5]),
+        ):
+            sem = in_sem.at[turn, len(copies)]
             if len(source.shape) == 3:
-                copy = pltpu.make_async_copy(source.at[:, :, span], target.at[:, rows, :], in_sem.at[order])
+                copies.append(pltpu.make_async_copy(source.at[:, there, span], target.at[:, rows, :], sem))
             else:
-                copy = pltpu.make_async_copy(source.at[:, span], target.at[rows, :], in_sem.at[order])
+                copies.append(pltpu.make_async_copy(source.at[there, span], target.at[rows, :], sem))
+        return copies
+
+    def send(turn):
+        half, inner = turn // (TURNS // 2), turn % (TURNS // 2)
+        span = slice(half * LANES, half * LANES + LANES)
+        there = slice(inner * HEIGHT, inner * HEIGHT + HEIGHT)
+        rows = slice(turn * HEIGHT, turn * HEIGHT + HEIGHT)
+        return [
+            pltpu.make_async_copy(fresh_ref.at[:STACKED, rows, :], temps_out.at[:, there, span], out_sem.at[turn, 0]),
+            pltpu.make_async_copy(fresh_ref.at[STACKED:, rows, :], thick_out.at[:, there, span], out_sem.at[turn, 1]),
+            pltpu.make_async_copy(forcing_ref.at[:, rows, :], forcing_out.at[:, there, span], out_sem.at[turn, 2]),
+        ]
+
+    fetched = [fetch(turn) for turn in range(TURNS)]
+    for copies in fetched:
+        for copy in copies:
             copy.start()
-            copies.append(copy)
-            order += 1
-
-    place_ref[...] = index_cells(list_ref, mask_ref, base_ref, count_ref, inverse_ref, table_ref)
-    plan = pltpu.make_async_copy(table_ref, plan_ref, table_sem)
-    plan.start()
-    for copy in copies:
-        copy.wait()
-    plan.wait()
+    most = index_cells(list_ref, mask_ref, base_ref, count_ref, inverse_ref, place_ref, spot_ref)
     lane = lax.broadcasted_iota(jnp.int32, (8, LANES), 1)
-
-    def solve(level, carry):
-        begin = plan_ref[level, 0]
-        end = plan_ref[level, 1]
-
-        def gather(turn, inner):
-            picks = []
-            for offset in range(4):
-                tile = jnp.minimum(begin + turn * 4 + offset, TILES - 1)
-                at = pl.ds(pl.multiple_of(tile * 8, 8), 8)
-                rank = lane + level * LANES - base_ref[at, :]
-                inside = jnp.logical_and(rank >= 0, rank < count_ref[at, :])
-                rank = jnp.where(inside, rank, 0)
-                spot = jnp.take_along_axis(inverse_ref[at, :], rank, axis=1)
-                picks.append((at, inside, spot))
-            planes = [(kept_ref, p) for p in range(KEPT)]
-            planes += [(snow_ref, p) for p in range(CATS)] + [(single_ref, 0), (single_ref, 1)]
-            for number, (ref, p) in enumerate(planes):
-                value = gathered_ref[number]
-                for at, inside, spot in picks:
-                    value = jnp.where(inside, jnp.take_along_axis(ref[p, at, :], spot, axis=1), value)
-                gathered_ref[number] = value
-            return inner
-
-        lax.fori_loop(0, lax.div(end - begin + 3, 4), gather, 0)
-        air = gathered_ref[KEPT + CATS]
-        heat = gathered_ref[KEPT + CATS + 1]
-        for cat in range(CATS):
-            temps = [gathered_ref[cat * LAYERS + i] for i in range(LAYERS)]
-            thick = gathered_ref[STACKED + cat]
-            current, growth = column(temps, thick, gathered_ref[KEPT + cat], air)
-            for i in range(LAYERS):
-                result_ref[level, cat * LAYERS + i] = current[i]
-            result_ref[level, STACKED + cat] = thick + (growth - 0.0005 * heat)
-        return carry
-
-    levels = lax.div(plan_ref[TILES + 1, TILES - 1] + (LANES - 1), LANES)
-    lax.fori_loop(0, levels, solve, 0)
-
-    def spread(tile, carry):
-        at = pl.ds(pl.multiple_of(tile * 8, 8), 8)
-        first = lax.div(plan_ref[TILES, tile], LANES)
-        final = lax.div(plan_ref[TILES + 1, tile] + (LANES - 1), LANES)
-        place = place_ref[at, :]
+    buffers = ((gathered_a, result_a), (gathered_b, result_b))
+
+    def tiles_of(team):
+        return [pl.ds(pl.multiple_of((team * TEAM + u) * 8, 8), 8) for u in range(TEAM)]
+
+    def force(at):
         ice = mask_ref[at, :]
-        level = jnp.where(ice > 0.5, lax.shift_right_logical(place, 7), -1)
-        spot = lax.bitwise_and(place, LANES - 1)
-
-        def fill(turn, inner):
-            low = jnp.minimum(first + 2 * turn, TILES - 1)
-            high = jnp.minimum(low + 1, TILES - 1)
-            in_low = level == low
-            in_high = level == high
-            for p in range(KEPT):
-                from_low = jnp.take_along_axis(result_ref[low, p], spot, axis=1)
-                from_high = jnp.take_along_axis(result_ref[high, p], spot, axis=1)
-                kept_ref[p, at, :] = jnp.where(in_low, from_low, jnp.where(in_high, from_high, kept_ref[p, at, :]))
-            return inner
-
-        lax.fori_loop(0, lax.div(final - first + 1, 2), fill, 0)
-        load = jnp.zeros((8, LANES), jnp.float32)
-        area_total = jnp.zeros((8, LANES), jnp.float32)
+        load = jnp.zeros(ice.shape, jnp.float32)
+        area_total = jnp.zeros(ice.shape, jnp.float32)
         for cat in range(CATS):
             area = area_ref[cat, at, :]
-            load = load + area * kept_ref[STACKED + cat, at, :]
+            load = load + area * fresh_ref[STACKED + cat, at, :]
             area_total = area_total + area
         load = ice * load
         forcing_ref[0, at, :] = drive_ref[0, at, :] + drive_ref[2, at, :]
@@ -260,31 +258,53 @@
         forcing_ref[2, at, :] = cells_ref[at, :].astype(jnp.float32)
         forcing_ref[3, at, :] = load * jnp.exp(-20.0 * (1.0 - area_total))
         forcing_ref[4, at, :] = 0.9 * load
-        return carry
-
-    def send_out(group):
-        pieces = []
-        per_half = GROUPS // 2
-        height = ROWS // per_half
-        half, inner = group // per_half, group % per_half
-        span = slice(half * LANES, half * LANES + LANES)
-        there = slice(inner * height, inner * height + height)
-        here = slice(group * height, group * height + height)
-        pieces.append(pltpu.make_async_copy(
-            kept_ref.at[:STACKED, here, :], temps_out.at[:, there, span], out_sem.at[group, 0]))
-        pieces.append(pltpu.make_async_copy(
-            kept_ref.at[STACKED:, here, :], thick_out.at[:, there, span], out_sem.at[group, 1]))
-        pieces.append(pltpu.make_async_copy(
-            forcing_ref.at[:, here, :], forcing_out.at[:, there, span], out_sem.at[group, 2]))
-        return pieces
+
+    def extra(team):
+        def one(level, carry):
+            tiles = tiles_of(team)
+            picks = []
+            for at in tiles:
+                rank = lane + level * LANES - base_ref[at, :]
+                inside = jnp.logical_and(rank >= 0, rank < count_ref[at, :])
+                spot = jnp.take_along_axis(inverse_ref[at, :], jnp.where(inside, rank, 0), axis=1)
+                picks.append((at, jnp.where(inside, spot, -1)))
+            gather_team(picks, kept_ref, snow_ref, single_ref, gathered_a)
+            solve_team(gathered_a, result_a)
+            spread_team(tiles, level, place_ref, fresh_ref, result_a, fresh_ref)
+            return carry
+
+        return one
 
     sent = []
-    per_group = TILES // GROUPS
-    for group in range(GROUPS):
-        lax.fori_loop(group * per_group, group * per_group + per_group, spread, 0)
-        for copy in send_out(group):
+    for turn in range(TURNS):
+        for copy in fetched[turn]:
+            copy.wait()
+        teams = [turn * PAIR + k for k in range(PAIR)]
+        for k, team in enumerate(teams):
+            gather_team([(at, spot_ref[at, :]) for at in tiles_of(team)], kept_ref, snow_ref, single_ref, buffers[k % 2][0])
+        for k, team in enumerate(teams):
+            solve_team(*buffers[k % 2])
+        for k, team in enumerate(teams):
+            spread_team(tiles_of(team), 0, place_ref, kept_ref, buffers[k % 2][1], fresh_ref)
+
+        force(slice(turn * HEIGHT, turn * HEIGHT + HEIGHT))
+        for copy in send(turn):
             copy.start()
             sent.append(copy)
+
+    @pl.when(most > LANES)
+    def _():
+        for copy in sent:
+            copy.wait()
+
+        def again(team, carry):
+            return lax.fori_loop(1, TEAM, extra(team), carry)
+
+        lax.fori_loop(0, TILES // TEAM, again, 0)
+        for turn in range(TURNS):
+            force(slice(turn * HEIGHT, turn * HEIGHT + HEIGHT))
+        for copy in sent:
+            copy.start()
 
     def pack(tile, carry):
         group = lax.shift_right_logical(lane, 3)
@@ -300,7 +320,7 @@
             out_ref[pl.ds(pl.multiple_of(tile * 8, 8), 8), :] = packed
         return carry
 
-    lax.fori_loop(0, ROWS // 8, pack, 0)
+    lax.fori_loop(0, ROWS // 8, pack, 0, unroll=True)
     for copy in sent:
         copy.wait()
 
@@ -519,15 +539,14 @@
             jax.ShapeDtypeStruct((ROWS, LANES), f32),
         ],
         scratch_shapes=[
-            flat(KEPT), flat(CATS), flat(CATS), flat(2), flat(5), flat(4), one, flat(5),
-            pltpu.VMEM((FLAT, LANES), f32), one, one, one, one,
-            pltpu.VMEM((TILES + 8, LANES), i32),
+            flat(KEPT), flat(KEPT), flat(CATS), flat(CATS), flat(2), flat(5), flat(4), one, flat(5),
+            pltpu.VMEM((FLAT, LANES), f32), one, one, one, one, one,
             pltpu.VMEM((KEPT + CATS + 2, 8, LANES), f32),
-            pltpu.VMEM((TILES, KEPT, 8, LANES), f32),
-            pltpu.SMEM((TILES + 8, LANES), i32),
-            pltpu.SemaphoreType.DMA((22,)),
-            pltpu.SemaphoreType.DMA((GROUPS, 3)),
-            pltpu.SemaphoreType.DMA,
+            pltpu.VMEM((KEPT + CATS + 2, 8, LANES), f32),
+            pltpu.VMEM((KEPT, 8, LANES), f32),
+            pltpu.VMEM((KEPT, 8, LANES), f32),
+            pltpu.SemaphoreType.DMA((TURNS, 11)),
+            pltpu.SemaphoreType.DMA((TURNS, 3)),
         ],
     )(
         listed, layer_temps, ice_thick, snow_thick, ice_area, air_temp, ocean_heat,

time: 55.1 us -> 41.6 us (0.75)
  Pallas kernels: 32.7 us -> 20.5 us
  starting transfers between devices: 15.9 us -> 14.6 us
    pallas_call x1, Pallas kernels: 21 us -> 11.5 us  [per_device(): pl.pallas_call(thermo_kernel, name='thermo', in_specs=[vmem] + [here] * 1...]
    pallas_call x1, Pallas kernels: 10 us -> 7.28 us  [per_device(): pl.pallas_call(motion_kernel, name='motion', in_specs=[smem] + [here] * 3...]
    ppermute x1, starting transfers between devices: 3.22 us -> 1.28 us  [per_device(): west = lax.ppermute(right, 'bx', [(q, (q + 1) % n_bx) for q in range(n_bx)])]
    ppermute x1, starting transfers between devices: 4.12 us -> 4.82 us  [per_device(): east = lax.ppermute(left, 'bx', [((q + 1) % n_bx, q) for q in range(n_bx)])]
where the time goes in v3:
time: 41.6 us; the launch traced here: 41.3 us
  Pallas kernels  20.5 us (49%)
  starting transfers between devices  14.6 us (35%)
  waiting for transfers between devices  3.62 us (9%)
  local copies, waits for them, and re-layouts  1.3 us (3%)
  between operations  0.67 us (2%)
  other arithmetic  0.61 us (1%)
    pallas_call x1, Pallas kernels, per_device(): pl.pallas_call(thermo_kernel, name='thermo', in_specs=[vmem] + [here] * 1...  11.5 us
    pallas_call x1, Pallas kernels, per_device(): pl.pallas_call(motion_kernel, name='motion', in_specs=[smem] + [here] * 3...  7.28 us
    ppermute x1, starting transfers between devices, per_device(): odd_halo = lax.ppermute(odd_rows, ('bx', 'by'), odd_pairs)  7.01 us
    ppermute x1, starting transfers between devices, per_device(): east = lax.ppermute(left, 'bx', [((q + 1) % n_bx, q) for q in range(n_bx)])  4.82 us
    ppermute x1, waiting for transfers between devices, per_device(): odd_halo = lax.ppermute(odd_rows, ('bx', 'by'), odd_pairs)  2.44 us
    pallas_call x1, Pallas kernels, per_device(): pl.pallas_call(rows_kernel, name='edge_rows', grid=(1,), in_specs=[smem]...  1.68 us
    ppermute x1, starting transfers between devices, per_device(): even_halo = lax.ppermute(even_rows, ('bx', 'by'), even_pairs)  1.54 us
    unnamed x8, local copies, waits for them, and re-layouts  1.3 us
  transfers between devices with their start and end apart: 4, of which 2 were waited for; matrix products, arithmetic and copies ran while one was open for 1% of the time, Pallas kernels for 0%

profile of v3, /device:TPU:25, one launch (start us, length us, event | category | flops | bytes accessed | tf_op | source)
XLA Modules:
  0.0 41.3 jit_solution(18176427047587627736)
XLA Ops:
  0.6 11.5 %thermo.1 = (f32[40,128,256]{2,1,0:T(8,128)}, f32[5,128,256]{2,1,0:T(8,128)}, f32[5,128,256]{2,1,0:T(8,128)}, f32[128,128]{1,0:T(8,128)}, f32[128,128]{1,0:T(8,128)}) custom-call(s32[1,6144]{1,0:T(1,128)} %bitcast.2, f32[40,128,256]{2,1,0:T(8,128)} %temps_hbm.1, f32[5,128,256]{2,1,0:T(8,128)} %thick_hbm.1, f32[5,128,256]{2,1,0:T(8,128)} %snow_hbm.1, ...), custom_call_target="tpu_custom_call" | custom-call | tf_op jit(solution)/shard_map/thermo/pallas_call | solution.py:529
  12.2 1.3 %collective-permute-start = (f32[128,128]{1,0:T(8,128)}, f32[128,128]{1,0:T(8,128)S(1)}, u32[]{:S(2)}, u32[]{:S(2)}) collective-permute-start(f32[128,128]{1,0:T(8,128)} %get-tuple-element.16), channel_id=1, source_target_pairs={{0,8},{8,16},{16,24},{24,32},{32,40},{40,48},{48,56},{56,64},{64,7... | collective-permute-start | bytes 196616 | tf_op jit(solution)/shard_map/ppermute | solution.py:557
  13.4 4.8 %collective-permute-start.1 = (f32[128,128]{1,0:T(8,128)}, f32[128,128]{1,0:T(8,128)S(1)}, u32[]{:S(2)}, u32[]{:S(2)}) collective-permute-start(f32[128,128]{1,0:T(8,128)} %get-tuple-element.17), channel_id=1, source_target_pairs={{8,0},{16,8},{24,16},{32,24},{40,32},{48,40},{56,48},{64,56},{72,6... | collective-permute-start | bytes 196616 | tf_op jit(solution)/shard_map/ppermute | solution.py:558
  18.3 0.6 %pad_add_fusion.spot_ref = s32[2]{0:T(128)} fusion(s32[1]{0:T(128)} %constant.1.clone.1, s32[1]{0:T(128)} %bitcast.1), kind=kLoop, calls=%fused_computation | loop fusion | flops 2 | bytes 16 | tf_op jit(solution)/shard_map/stack | solution.py:560
  18.9 1.2 %collective-permute-done.west_low.west_high.west_ref = f32[128,128]{1,0:T(8,128)S(1)} collective-permute-done((f32[128,128]{1,0:T(8,128)}, f32[128,128]{1,0:T(8,128)S(1)}, u32[]{:S(2)}, u32[]{:S(2)}) %collective-permute-start) | collective-permute-done | bytes 65568 | tf_op jit(solution)/shard_map/ppermute | solution.py:557
  20.1 0.0 copy-start
  20.1 0.0 collective-permute-done.1.east_low.east_high.east_ref
  20.1 0.0 copy-start.1
  20.1 0.6 %copy-done = f32[128,128]{1,0:T(8,128)} copy-done((f32[128,128]{1,0:T(8,128)}, f32[128,128]{1,0:T(8,128)S(1)}, u32[]{:S(2)}) %copy-start) | copy-done | bytes 65560
  20.7 0.0 copy-done.1
  20.7 1.7 %edge_rows.1 = (f32[10,3,8,128]{3,2,1,0:T(8,128)}, f32[10,3,8,128]{3,2,1,0:T(8,128)}) custom-call(s32[2]{0:T(128)} %pad_add_fusion.spot_ref, f32[2,128,256]{2,1,0:T(8,128)} %vel_hbm.3, f32[3,128,256]{2,1,0:T(8,128)} %stress_hbm.3, f32[5,128,256]{2,1,0:T(8,128)} %get-tuple-element.15.forcing_low.forcing_high.forcing_hbm, f32[128,128]{1,0:T(8,128)} %copy-done, ...), custom_call_target="tpu_custom_call" | custom-call | tf_op jit(solution)/shard_map/edge_rows/pallas_call | solution.py:571
  22.4 1.5 %collective-permute-start.2 = (f32[10,3,8,128]{3,2,1,0:T(8,128)}, f32[10,3,8,128]{3,2,1,0:T(8,128)S(1)}, u32[]{:S(2)}, u32[]{:S(2)}) collective-permute-start(f32[10,3,8,128]{3,2,1,0:T(8,128)} %get-tuple-element.18), channel_id=1, source_target_pairs={{0,1},{1,0},{2,3},{3,2},{4,5},{5,4},{6,7},{7,6},{8,9},{9,8},{10,11... | collective-permute-start | bytes 368648 | tf_op jit(solution)/shard_map/ppermute | solution.py:592
  23.9 7.0 %collective-permute-start.3 = (f32[10,3,8,128]{3,2,1,0:T(8,128)}, f32[10,3,8,128]{3,2,1,0:T(8,128)S(1)}, u32[]{:S(2)}, u32[]{:S(2)}) collective-permute-start(f32[10,3,8,128]{3,2,1,0:T(8,128)} %get-tuple-element.19), channel_id=1, source_target_pairs={{1,2},{2,1},{3,4},{4,3},{5,6},{6,5},{7,127},{9,10},{10,9},{11,12},... | collective-permute-start | bytes 368648 | tf_op jit(solution)/shard_map/ppermute | solution.py:593
  30.9 0.0 collective-permute-done.2.even_ref
  30.9 0.0 copy-start.2
  31.0 2.4 %collective-permute-done.3.odd_ref = f32[10,3,8,128]{3,2,1,0:T(8,128)S(1)} collective-permute-done((f32[10,3,8,128]{3,2,1,0:T(8,128)}, f32[10,3,8,128]{3,2,1,0:T(8,128)S(1)}, u32[]{:S(2)}, u32[]{:S(2)}) %collective-permute-start.3) | collective-permute-done | bytes 122912 | tf_op jit(solution)/shard_map/ppermute | solution.py:593
  33.4 0.0 copy-done.2
  33.4 0.0 copy-start.3
  33.4 0.6 %copy-done.3 = f32[10,3,8,128]{3,2,1,0:T(8,128)} copy-done((f32[10,3,8,128]{3,2,1,0:T(8,128)}, f32[10,3,8,128]{3,2,1,0:T(8,128)S(1)}, u32[]{:S(2)}) %copy-start.3) | copy-done | bytes 122904
  34.1 7.3 %motion.1 = (f32[2,128,256]{2,1,0:T(8,128)}, f32[3,128,256]{2,1,0:T(8,128)}) custom-call(s32[2]{0:T(128)} %pad_add_fusion.spot_ref, f32[2,128,256]{2,1,0:T(8,128)} %vel_hbm.3, f32[3,128,256]{2,1,0:T(8,128)} %stress_hbm.3, f32[5,128,256]{2,1,0:T(8,128)} %get-tuple-element.15.forcing_low.forcing_high.forcing_hbm, f32[128,128]{1,0:T(8,128)} %copy-done, ...), custom_call_target="tpu_custom_call" | custom-call | tf_op jit(solution)/shard_map/motion/pallas_call | solution.py:595
Async XLA Ops:
  12.2 7.9 %collective-permute-start = (f32[128,128]{1,0:T(8,128)}, f32[128,128]{1,0:T(8,128)S(1)}, u32[]{:S(2)}, u32[]{:S(2)}) collective-permute-start(f32[128,128]{1,0:T(8,128)} %get-tuple-element.16), channel_id=1, source_target_pairs={{0,8},{8,16},{16,24},{24,32},{32,40},{40,48},{48,56},{56,64},{64,7... | collective-permute-start | bytes 196616 | tf_op jit(solution)/shard_map/ppermute | solution.py:557
  13.4 6.6 %collective-permute-start.1 = (f32[128,128]{1,0:T(8,128)}, f32[128,128]{1,0:T(8,128)S(1)}, u32[]{:S(2)}, u32[]{:S(2)}) collective-permute-start(f32[128,128]{1,0:T(8,128)} %get-tuple-element.17), channel_id=1, source_target_pairs={{8,0},{16,8},{24,16},{32,24},{40,32},{48,40},{56,48},{64,56},{72,6... | collective-permute-start | bytes 196616 | tf_op jit(solution)/shard_map/ppermute | solution.py:558
  20.1 0.6 %copy-start = (f32[128,128]{1,0:T(8,128)}, f32[128,128]{1,0:T(8,128)S(1)}, u32[]{:S(2)}) copy-start(f32[128,128]{1,0:T(8,128)S(1)} %collective-permute-done.west_low.west_high.west_ref) | copy-start | bytes 196612
  20.1 0.6 %copy-start.1 = (f32[128,128]{1,0:T(8,128)}, f32[128,128]{1,0:T(8,128)S(1)}, u32[]{:S(2)}) copy-start(f32[128,128]{1,0:T(8,128)S(1)} %collective-permute-done.1.east_low.east_high.east_ref) | copy-start | bytes 196612
  22.4 8.6 %collective-permute-start.2 = (f32[10,3,8,128]{3,2,1,0:T(8,128)}, f32[10,3,8,128]{3,2,1,0:T(8,128)S(1)}, u32[]{:S(2)}, u32[]{:S(2)}) collective-permute-start(f32[10,3,8,128]{3,2,1,0:T(8,128)} %get-tuple-element.18), channel_id=1, source_target_pairs={{0,1},{1,0},{2,3},{3,2},{4,5},{5,4},{6,7},{7,6},{8,9},{9,8},{10,11... | collective-permute-start | bytes 368648 | tf_op jit(solution)/shard_map/ppermute | solution.py:592
  23.9 9.5 %collective-permute-start.3 = (f32[10,3,8,128]{3,2,1,0:T(8,128)}, f32[10,3,8,128]{3,2,1,0:T(8,128)S(1)}, u32[]{:S(2)}, u32[]{:S(2)}) collective-permute-start(f32[10,3,8,128]{3,2,1,0:T(8,128)} %get-tuple-element.19), channel_id=1, source_target_pairs={{1,2},{2,1},{3,4},{4,3},{5,6},{6,5},{7,127},{9,10},{10,9},{11,12},... | collective-permute-start | bytes 368648 | tf_op jit(solution)/shard_map/ppermute | solution.py:593
  30.9 2.5 %copy-start.2 = (f32[10,3,8,128]{3,2,1,0:T(8,128)}, f32[10,3,8,128]{3,2,1,0:T(8,128)S(1)}, u32[]{:S(2)}) copy-start(f32[10,3,8,128]{3,2,1,0:T(8,128)S(1)} %collective-permute-done.2.even_ref) | copy-start | bytes 368644
  33.4 0.7 %copy-start.3 = (f32[10,3,8,128]{3,2,1,0:T(8,128)}, f32[10,3,8,128]{3,2,1,0:T(8,128)S(1)}, u32[]{:S(2)}) copy-start(f32[10,3,8,128]{3,2,1,0:T(8,128)S(1)} %collective-permute-done.3.odd_ref) | copy-start | bytes 368644

commit v4 on v3

--- a/solution.py
+++ b/solution.py
@@ -1,3 +1,5 @@
+import functools
+
 import jax
 import jax.numpy as jnp
 from jax import lax
@@ -12,7 +14,7 @@
 ROWS = 128
 COLS = 256
 DEEP = 8
-FIELDS = 10
+FIELDS = 11
 TALL = ROWS + 4 * DEEP
 BAND = 144
 LANES = 128
@@ -178,24 +180,31 @@
         result_ref[STACKED + cat] = thick + (growth - 0.0005 * heat)
 
 
-def spread_team(tiles, level, place_ref, source_ref, result_ref, fresh_ref):
+def field_of(i, moving, forcing):
+    return (moving, i) if i < 5 else (forcing, i - 5)
+
+
+def spread_team(tiles, level, place_ref, source_ref, result_ref, fresh_ref, planes, skip=0):
     for at in tiles:
         place = place_ref[at, :] - level * LANES
         inside = jnp.logical_and(place >= 0, place < LANES)
         spot = jnp.where(inside, place, 0)
-        for p in range(KEPT):
+        for p in planes:
             value = jnp.take_along_axis(result_ref[p], spot, axis=1)
-            fresh_ref[p, at, :] = jnp.where(inside, value, source_ref[p, at, :])
+            fresh_ref[p - skip, at, :] = jnp.where(inside, value, source_ref[p, at, :])
 
 
 def thermo_kernel(
     list_ref, temps_hbm, thick_hbm, snow_hbm, area_hbm, air_hbm, heat_hbm,
     vel_hbm, stress_hbm, wind_hbm, ocean_hbm, cells_hbm,
-    temps_out, thick_out, forcing_out, left_out, right_out,
+    thick_out, forcing_out, result_out, place_out, left_out, right_out,
     kept_ref, fresh_ref, snow_ref, area_ref, single_ref, moving_ref, drive_ref, cells_ref, forcing_ref,
     mask_ref, base_ref, count_ref, inverse_ref, place_ref, spot_ref,
-    gathered_a, gathered_b, result_a, result_b, in_sem, out_sem,
+    gathered_a, gathered_b, result_ref, in_sem, out_sem, result_sem, extra_sem,
 ):
+    band = lax.axis_index("by")
+    north = lax.axis_size("by") * ROWS
+
     def fetch(turn):
         half, inner = turn // (TURNS // 2), turn % (TURNS // 2)
         span = slice(half * LANES, half * LANES + LANES)
@@ -228,9 +237,8 @@
         there = slice(inner * HEIGHT, inner * HEIGHT + HEIGHT)
         rows = slice(turn * HEIGHT, turn * HEIGHT + HEIGHT)
         return [
-            pltpu.make_async_copy(fresh_ref.at[:STACKED, rows, :], temps_out.at[:, there, span], out_sem.at[turn, 0]),
-            pltpu.make_async_copy(fresh_ref.at[STACKED:, rows, :], thick_out.at[:, there, span], out_sem.at[turn, 1]),
-            pltpu.make_async_copy(forcing_ref.at[:, rows, :], forcing_out.at[:, there, span], out_sem.at[turn, 2]),
+            pltpu.make_async_copy(fresh_ref.at[:, rows, :], thick_out.at[:, there, span], out_sem.at[turn, 0]),
+            pltpu.make_async_copy(forcing_ref.at[:, rows, :], forcing_out.at[:, there, span], out_sem.at[turn, 1]),
         ]
 
     fetched = [fetch(turn) for turn in range(TURNS)]
@@ -238,26 +246,37 @@
         for copy in copies:
             copy.start()
     most = index_cells(list_ref, mask_ref, base_ref, count_ref, inverse_ref, place_ref, spot_ref)
+    sent = [pltpu.make_async_copy(place_ref, place_out, result_sem.at[TILES // TEAM])]
+    sent[0].start()
     lane = lax.broadcasted_iota(jnp.int32, (8, LANES), 1)
-    buffers = ((gathered_a, result_a), (gathered_b, result_b))
+    buffers = (gathered_a, gathered_b)
+    thick_planes = range(STACKED, KEPT)
 
     def tiles_of(team):
         return [pl.ds(pl.multiple_of((team * TEAM + u) * 8, 8), 8) for u in range(TEAM)]
 
-    def force(at):
+    def force(turn):
+        at = slice(turn * HEIGHT, turn * HEIGHT + HEIGHT)
         ice = mask_ref[at, :]
         load = jnp.zeros(ice.shape, jnp.float32)
         area_total = jnp.zeros(ice.shape, jnp.float32)
         for cat in range(CATS):
             area = area_ref[cat, at, :]
-            load = load + area * fresh_ref[STACKED + cat, at, :]
+            load = load + area * fresh_ref[cat, at, :]
             area_total = area_total + area
         load = ice * load
+        mass = 0.9 * load
+        row = lax.broadcasted_iota(jnp.int32, (HEIGHT, LANES), 0) + (turn % (TURNS // 2)) * HEIGHT + band * ROWS
+        latitude = row.astype(jnp.float32) + 0.5
+        turning = 1.4 * jnp.sin(0.5 * jnp.pi * (2.0 * latitude / north - 1.0)) * mass
+        diagonal = mass + 1.0
+        scale = cells_ref[at, :].astype(jnp.float32) / (diagonal * diagonal + turning * turning)
         forcing_ref[0, at, :] = drive_ref[0, at, :] + drive_ref[2, at, :]
         forcing_ref[1, at, :] = drive_ref[1, at, :] + drive_ref[3, at, :]
-        forcing_ref[2, at, :] = cells_ref[at, :].astype(jnp.float32)
+        forcing_ref[2, at, :] = diagonal * scale
         forcing_ref[3, at, :] = load * jnp.exp(-20.0 * (1.0 - area_total))
-        forcing_ref[4, at, :] = 0.9 * load
+        forcing_ref[4, at, :] = mass
+        forcing_ref[5, at, :] = turning * scale
 
     def extra(team):
         def one(level, carry):
@@ -269,25 +288,35 @@
                 spot = jnp.take_along_axis(inverse_ref[at, :], jnp.where(inside, rank, 0), axis=1)
                 picks.append((at, jnp.where(inside, spot, -1)))
             gather_team(picks, kept_ref, snow_ref, single_ref, gathered_a)
-            solve_team(gathered_a, result_a)
-            spread_team(tiles, level, place_ref, fresh_ref, result_a, fresh_ref)
+            solve_team(gathered_a, result_ref.at[TILES // TEAM])
+            for at in tiles:
+                place = place_ref[at, :] - level * LANES
+                inside = jnp.logical_and(place >= 0, place < LANES)
+                spot = jnp.where(inside, place, 0)
+                for p in thick_planes:
+                    value = jnp.take_along_axis(result_ref[TILES // TEAM, p], spot, axis=1)
+                    fresh_ref[p - STACKED, at, :] = jnp.where(inside, value, fresh_ref[p - STACKED, at, :])
+            copy = pltpu.make_async_copy(result_ref.at[TILES // TEAM, :STACKED], result_out.at[level, team], extra_sem)
+            copy.start()
+            copy.wait()
             return carry
 
         return one
 
-    sent = []
     for turn in range(TURNS):
         for copy in fetched[turn]:
             copy.wait()
         teams = [turn * PAIR + k for k in range(PAIR)]
         for k, team in enumerate(teams):
-            gather_team([(at, spot_ref[at, :]) for at in tiles_of(team)], kept_ref, snow_ref, single_ref, buffers[k % 2][0])
+            gather_team([(at, spot_ref[at, :]) for at in tiles_of(team)], kept_ref, snow_ref, single_ref, buffers[k % 2])
         for k, team in enumerate(teams):
-            solve_team(*buffers[k % 2])
+            solve_team(buffers[k % 2], result_ref.at[team])
         for k, team in enumerate(teams):
-            spread_team(tiles_of(team), 0, place_ref, kept_ref, buffers[k % 2][1], fresh_ref)
-
-        force(slice(turn * HEIGHT, turn * HEIGHT + HEIGHT))
+            spread_team(tiles_of(team), 0, place_ref, kept_ref, result_ref.at[team], fresh_ref, thick_planes, STACKED)
+            copy = pltpu.make_async_copy(result_ref.at[team, :STACKED], result_out.at[0, team], result_sem.at[team])
+            copy.start()
+            sent.append(copy)
+        force(turn)
         for copy in send(turn):
             copy.start()
             sent.append(copy)
@@ -302,7 +331,7 @@
 
         lax.fori_loop(0, TILES // TEAM, again, 0)
         for turn in range(TURNS):
-            force(slice(turn * HEIGHT, turn * HEIGHT + HEIGHT))
+            force(turn)
         for copy in sent:
             copy.start()
 
@@ -312,7 +341,8 @@
             at = pl.ds(pl.multiple_of(tile * 8 + half * ROWS, 8), 8)
             packed = jnp.zeros((8, LANES), jnp.float32)
             for i in range(FIELDS):
-                x = moving_ref[i, at, :] if i < 5 else forcing_ref[i - 5, at, :]
+                ref, k = field_of(i, moving_ref, forcing_ref)
+                x = ref[k, at, :]
                 turn = (8 * i + push) % LANES
                 if turn:
                     x = pltpu.roll(x, turn, axis=1)
@@ -325,6 +355,65 @@
         copy.wait()
 
 
+def temps_kernel(half, temps_hbm, result_hbm, place_hbm, *rest):
+    temps_out, kept_ref, fresh_ref, place_ref, result_ref, in_sem, out_sem, extra_sem = rest[-8:]
+    teams = TILES // TEAM // 2
+    height = TEAM * 8
+    span = slice(half * LANES, half * LANES + LANES)
+    rows = slice(half * ROWS, half * ROWS + ROWS)
+    whole = pltpu.make_async_copy(place_hbm.at[rows, :], place_ref, extra_sem)
+    whole.start()
+    fetched = []
+    for k in range(teams):
+        here = slice(k * height, k * height + height)
+        fetched.append([
+            pltpu.make_async_copy(temps_hbm.at[:, here, span], kept_ref.at[:, here, :], in_sem.at[k, 0]),
+            pltpu.make_async_copy(result_hbm.at[0, half * teams + k], result_ref.at[k], in_sem.at[k, 1]),
+        ])
+    for copies in fetched:
+        for copy in copies:
+            copy.start()
+    whole.wait()
+    sent = []
+    for k in range(teams):
+        for copy in fetched[k]:
+            copy.wait()
+        here = slice(k * height, k * height + height)
+        tiles = [slice(k * height + 8 * u, k * height + 8 * u + 8) for u in range(TEAM)]
+        spread_team(tiles, 0, place_ref, kept_ref, result_ref.at[k], fresh_ref, range(STACKED))
+        copy = pltpu.make_async_copy(fresh_ref.at[:, here, :], temps_out.at[:, here, span], out_sem.at[k])
+        copy.start()
+        sent.append(copy)
+
+    @pl.when(jnp.max(place_ref[...]) >= LANES)
+    def _():
+        for copy in sent:
+            copy.wait()
+
+        def again(step, carry):
+            team = lax.div(step, TEAM - 1)
+            level = lax.rem(step, TEAM - 1) + 1
+            copy = pltpu.make_async_copy(result_hbm.at[level, half * teams + team], result_ref.at[0], extra_sem)
+            copy.start()
+            copy.wait()
+            for u in range(TEAM):
+                at = pl.ds(pl.multiple_of(team * height + 8 * u, 8), 8)
+                place = place_ref[at, :] - level * LANES
+                inside = jnp.logical_and(place >= 0, place < LANES)
+                spot = jnp.where(inside, place, 0)
+                for p in range(STACKED):
+                    value = jnp.take_along_axis(result_ref[0, p], spot, axis=1)
+                    fresh_ref[p, at, :] = jnp.where(inside, value, fresh_ref[p, at, :])
+            return carry
+
+        lax.fori_loop(0, teams * (TEAM - 1), again, 0)
+        for copy in sent:
+            copy.start()
+
+    for copy in sent:
+        copy.wait()
+
+
 def halo_tile(west, east, field, rows):
     lane = lax.broadcasted_iota(jnp.int32, (rows, LANES), 1)
     east_side = pltpu.roll(east, (LANES - 8 * field) % LANES, axis=1) if field else east
@@ -334,10 +423,10 @@
 
 
 def rows_kernel(
-    spot_ref, vel_low, stress_low, forcing_low, west_low, east_low,
+    vel_low, stress_low, forcing_low, west_low, east_low,
     vel_high, stress_high, forcing_high, west_high, east_high, even_out, odd_out,
 ):
-    even = lax.rem(spot_ref[0], 2) == 0
+    even = lax.rem(lax.axis_index("by"), 2) == 0
 
     def fill(to_low, to_high):
         for out, vel_ref, stress_ref, forcing_ref, west_ref, east_ref in (
@@ -366,12 +455,17 @@
 
 
 def motion_kernel(
-    spot_ref, vel_hbm, stress_hbm, forcing_hbm, west_ref, east_ref, even_ref, odd_ref,
-    vel_out, stress_out, state_ref, in_sem, out_sem,
+    vel_hbm, stress_hbm, forcing_hbm, west_hbm, east_hbm, even_hbm, odd_hbm,
+    vel_out, stress_out, state_ref, west_ref, east_ref, even_ref, odd_ref, in_sem, halo_sem, out_sem,
 ):
-    spot = spot_ref[0]
+    spot = lax.axis_index("by")
     even = lax.rem(spot, 2) == 0
-    top = spot == spot_ref[1] - 1
+    top = spot == lax.axis_size("by") - 1
+    halos = []
+    for source, target in ((west_hbm, west_ref), (east_hbm, east_ref), (even_hbm, even_ref), (odd_hbm, odd_ref)):
+        copy = pltpu.make_async_copy(source, target, halo_sem.at[len(halos)])
+        copy.start()
+        halos.append(copy)
     low = slice(DEEP, 2 * DEEP)
     mid = slice(2 * DEEP, 2 * DEEP + ROWS)
     high = slice(2 * DEEP + ROWS, 3 * DEEP + ROWS)
@@ -381,11 +475,13 @@
         for number, (source, target) in enumerate((
             (vel_hbm, state_ref.at[0:2, tile, mid, :]),
             (stress_hbm, state_ref.at[2:5, tile, mid, :]),
-            (forcing_hbm, state_ref.at[5:10, tile, mid, :]),
+            (forcing_hbm, state_ref.at[5:11, tile, mid, :]),
         )):
             copy = pltpu.make_async_copy(source.at[:, :, span], target, in_sem.at[tile, number])
             copy.start()
             copies.append(copy)
+    for copy in halos:
+        copy.wait()
     blank = jnp.zeros((DEEP, LANES), jnp.float32)
     for i in range(FIELDS):
         for tile in range(3):
@@ -420,25 +516,6 @@
     lane = lax.broadcasted_iota(jnp.int32, (BAND, LANES), 1)
     is_first = lane == 0
     is_final = lane == LANES - 1
-
-    def prepare(band, carry):
-        start = pl.multiple_of(DEEP + band * BAND, 8)
-        at = pl.ds(start, BAND)
-        row = lax.broadcasted_iota(jnp.int32, (BAND, LANES), 0) + (start - 2 * DEEP) + spot * ROWS
-        whole = spot_ref[1] * ROWS
-        row = jnp.where(row >= whole, 2 * whole - 1 - row, row)
-        latitude = row.astype(jnp.float32) + 0.5
-        turn = 1.4 * jnp.sin(0.5 * jnp.pi * (2.0 * latitude / whole.astype(jnp.float32) - 1.0))
-        for tile in range(3):
-            mass = state_ref[9, tile, at, :]
-            diagonal = mass + 1.0
-            turning = turn * mass
-            scale = state_ref[7, tile, at, :] / (diagonal * diagonal + turning * turning)
-            state_ref[7, tile, at, :] = diagonal * scale
-            state_ref[10, tile, at, :] = turning * scale
-        return carry
-
-    lax.fori_loop(0, bands, prepare, 0)
 
     def shift_x(parts):
         ahead = [pltpu.roll(x, LANES - 1, axis=1) for x in parts]
@@ -496,17 +573,22 @@
         lax.fori_loop(0, bands, momentum, 0)
         return carry
 
-    lax.fori_loop(0, SUB, subcycle, 0)
+    lax.fori_loop(0, SUB - 1, subcycle, 0)
+    lax.fori_loop(0, bands, stresses, 0)
     sent = []
-    for tile in range(2):
-        span = slice(tile * LANES, tile * LANES + LANES)
-        for number, (source, target) in enumerate((
-            (state_ref.at[0:2, tile, mid, :], vel_out),
-            (state_ref.at[2:5, tile, mid, :], stress_out),
-        )):
-            copy = pltpu.make_async_copy(source, target.at[:, :, span], out_sem.at[tile, number])
+
+    def send(number, fields, target):
+        for tile in range(2):
+            span = slice(tile * LANES, tile * LANES + LANES)
+            copy = pltpu.make_async_copy(
+                state_ref.at[fields, tile, mid, :], target.at[:, :, span], out_sem.at[tile, number]
+            )
             copy.start()
             sent.append(copy)
+
+    send(0, slice(2, 5), stress_out)
+    lax.fori_loop(0, bands, momentum, 0)
+    send(1, slice(0, 2), vel_out)
     for copy in sent:
         copy.wait()
 
@@ -517,7 +599,6 @@
 ):
     f32 = jnp.float32
     i32 = jnp.int32
-    smem = pl.BlockSpec(memory_space=pltpu.SMEM)
     vmem = pl.BlockSpec(memory_space=pltpu.VMEM)
     here = pl.BlockSpec(memory_space=pl.ANY)
     listed = ice_cols.reshape(1, -1)
@@ -526,38 +607,61 @@
         return pltpu.VMEM((n, FLAT, LANES), kind)
 
     one = pltpu.VMEM((FLAT, LANES), i32)
-    temps_new, thick_new, forcing, left, right = pl.pallas_call(
+    teams = TILES // TEAM
+    thick_new, forcing, result, place, left, right = pl.pallas_call(
         thermo_kernel,
         name="thermo",
         in_specs=[vmem] + [here] * 11,
-        out_specs=[here, here, here, vmem, vmem],
+        out_specs=[here, here, here, here, vmem, vmem],
         out_shape=[
-            jax.ShapeDtypeStruct((STACKED, ROWS, COLS), f32),
             jax.ShapeDtypeStruct((CATS, ROWS, COLS), f32),
-            jax.ShapeDtypeStruct((5, ROWS, COLS), f32),
+            jax.ShapeDtypeStruct((6, ROWS, COLS), f32),
+            jax.ShapeDtypeStruct((TEAM, teams, STACKED, 8, LANES), f32),
+            jax.ShapeDtypeStruct((FLAT, LANES), i32),
             jax.ShapeDtypeStruct((ROWS, LANES), f32),
             jax.ShapeDtypeStruct((ROWS, LANES), f32),
         ],
         scratch_shapes=[
-            flat(KEPT), flat(KEPT), flat(CATS), flat(CATS), flat(2), flat(5), flat(4), one, flat(5),
+            flat(KEPT), flat(CATS), flat(CATS), flat(CATS), flat(2), flat(5), flat(4), one, flat(6),
             pltpu.VMEM((FLAT, LANES), f32), one, one, one, one, one,
             pltpu.VMEM((KEPT + CATS + 2, 8, LANES), f32),
             pltpu.VMEM((KEPT + CATS + 2, 8, LANES), f32),
-            pltpu.VMEM((KEPT, 8, LANES), f32),
-            pltpu.VMEM((KEPT, 8, LANES), f32),
+            pltpu.VMEM((teams + 1, KEPT, 8, LANES), f32),
             pltpu.SemaphoreType.DMA((TURNS, 11)),
-            pltpu.SemaphoreType.DMA((TURNS, 3)),
+            pltpu.SemaphoreType.DMA((TURNS, 2)),
+            pltpu.SemaphoreType.DMA((teams + 1,)),
+            pltpu.SemaphoreType.DMA,
         ],
     )(
         listed, layer_temps, ice_thick, snow_thick, ice_area, air_temp, ocean_heat,
         velocity, stress, wind_stress, ocean_current, ocean_mask,
     )
+
+    def renew(half, *before):
+        return pl.pallas_call(
+            functools.partial(temps_kernel, half),
+            name="temps_west" if half == 0 else "temps_east",
+            in_specs=[here] * (3 + len(before)),
+            out_specs=here,
+            out_shape=jax.ShapeDtypeStruct((STACKED, ROWS, COLS), f32),
+            input_output_aliases={3: 0} if before else {},
+            cost_estimate=pl.CostEstimate(flops=20_000_000, transcendentals=0, bytes_accessed=6_000_000),
+            scratch_shapes=[
+                pltpu.VMEM((STACKED, ROWS, LANES), f32),
+                pltpu.VMEM((STACKED, ROWS, LANES), f32),
+                pltpu.VMEM((ROWS, LANES), i32),
+                pltpu.VMEM((teams // 2, STACKED, 8, LANES), f32),
+                pltpu.SemaphoreType.DMA((teams // 2, 2)),
+                pltpu.SemaphoreType.DMA((teams // 2,)),
+                pltpu.SemaphoreType.DMA,
+            ],
+        )(layer_temps, result, place, *before)
+
     n_bx = lax.axis_size("bx")
     n_by = lax.axis_size("by")
     west = lax.ppermute(right, "bx", [(q, (q + 1) % n_bx) for q in range(n_bx)])
     east = lax.ppermute(left, "bx", [((q + 1) % n_bx, q) for q in range(n_bx)])
-
-    spot = jnp.stack([lax.axis_index("by"), jnp.int32(n_by)]).astype(i32)
+    temps_part = renew(0)
     band = jax.ShapeDtypeStruct((FIELDS, 3, DEEP, LANES), f32)
 
     def slab(n, block):
@@ -572,12 +676,11 @@
         rows_kernel,
         name="edge_rows",
         grid=(1,),
-        in_specs=[smem]
-        + [slab(2, 0), slab(3, 0), slab(5, 0), edge(0), edge(0)]
-        + [slab(2, final), slab(3, final), slab(5, final), edge(final), edge(final)],
+        in_specs=[slab(2, 0), slab(3, 0), slab(6, 0), edge(0), edge(0)]
+        + [slab(2, final), slab(3, final), slab(6, final), edge(final), edge(final)],
         out_specs=[halo, halo],
         out_shape=[band, band],
-    )(spot, velocity, stress, forcing, west, east, velocity, stress, forcing, west, east)
+    )(velocity, stress, forcing, west, east, velocity, stress, forcing, west, east)
 
     def at(p, q):
         return q * n_by + p
@@ -589,24 +692,29 @@
         for p in range(1, n_by - 1, 2):
             odd_pairs += [(at(p, q), at(p + 1, q)), (at(p + 1, q), at(p, q))]
         odd_pairs.append((at(n_by - 1, q), at(n_by - 1, n_bx - 1 - q)))
+    even_rows, odd_rows, temps_part = lax.optimization_barrier((even_rows, odd_rows, temps_part))
+    odd_halo = lax.ppermute(odd_rows, ("bx", "by"), odd_pairs)
     even_halo = lax.ppermute(even_rows, ("bx", "by"), even_pairs)
-    odd_halo = lax.ppermute(odd_rows, ("bx", "by"), odd_pairs)
-
+    temps_new = renew(1, temps_part)
+    edge_shape = pltpu.VMEM((ROWS, LANES), f32)
+    band_shape = pltpu.VMEM((FIELDS, 3, DEEP, LANES), f32)
     velocity_new, stress_new = pl.pallas_call(
         motion_kernel,
         name="motion",
-        in_specs=[smem] + [here] * 3 + [vmem] * 4,
+        in_specs=[here] * 7,
         out_specs=[here, here],
         out_shape=[
             jax.ShapeDtypeStruct((2, ROWS, COLS), f32),
             jax.ShapeDtypeStruct((3, ROWS, COLS), f32),
         ],
         scratch_shapes=[
-            pltpu.VMEM((FIELDS + 1, 3, TALL, LANES), f32),
+            pltpu.VMEM((FIELDS, 3, TALL, LANES), f32),
+            edge_shape, edge_shape, band_shape, band_shape,
             pltpu.SemaphoreType.DMA((2, 3)),
+            pltpu.SemaphoreType.DMA((4,)),
             pltpu.SemaphoreType.DMA((2, 2)),
         ],
-    )(spot, velocity, stress, forcing, west, east, even_halo, odd_halo)
+    )(velocity, stress, forcing, west, east, even_halo, odd_halo)
     return temps_new, thick_new, velocity_new, stress_new
 
 

time: 41.6 us -> 40.9 us (0.983)
  Pallas kernels: 20.5 us -> 24.5 us
  waiting for transfers between devices: 3.62 us -> 0.01 us
  starting transfers between devices: 14.6 us -> 13.3 us
  other arithmetic: 0.61 us -> 0 us
  local copies, waits for them, and re-layouts: 1.3 us -> 1.91 us
    pallas_call x2 -> x4, Pallas kernels: 8.95 us -> 14 us  [the longest x2 6.27 us: renew(): pl.pallas_call(functools.partial(temps_kernel, half), name='temps_west' i...]
    ppermute x1, waiting for transfers between devices: 2.44 us -> 0.01 us  [per_device(): odd_halo = lax.ppermute(odd_rows, ('bx', 'by'), odd_pairs)]
    ppermute x1, waiting for transfers between devices: 1.17 us -> 0.01 us  [per_device(): west = lax.ppermute(right, 'bx', [(q, (q + 1) % n_bx) for q in range(n_bx)])]
    pallas_call x1, Pallas kernels: 11.5 us -> 10.5 us  [per_device(): pl.pallas_call(thermo_kernel, name='thermo', in_specs=[vmem] + [here] * 1...]
    ppermute x1, starting transfers between devices: 7.01 us -> 6.23 us  [per_device(): odd_halo = lax.ppermute(odd_rows, ('bx', 'by'), odd_pairs)]
    another operation x1 -> x0, other arithmetic: 0.61 us -> none  [per_device(): spot = jnp.stack([lax.axis_index('by'), jnp.int32(n_by)]).astype(i32)]
    unnamed x8, local copies, waits for them, and re-layouts: 1.3 us -> 1.91 us
    ppermute x1, starting transfers between devices: 1.54 us -> 0.96 us  [per_device(): even_halo = lax.ppermute(even_rows, ('bx', 'by'), even_pairs)]
  transfers between devices with their start and end apart: 4 -> 4, of which waited for: 2 -> 0; matrix products, arithmetic and copies ran while one was open for 1% -> 0% of each run, Pallas kernels for 0% -> 15%
where the time goes in v4:
time: 40.9 us; the launch traced here: 40.6 us
  Pallas kernels  24.5 us (60%)
  starting transfers between devices  13.3 us (33%)
  local copies, waits for them, and re-layouts  1.91 us (5%)
  between operations  0.89 us (2%)
    pallas_call x1, Pallas kernels, per_device(): pl.pallas_call(thermo_kernel, name='thermo', in_specs=[vmem] + [here] * 1...  10.5 us
    pallas_call x2, Pallas kernels, renew(): pl.pallas_call(functools.partial(temps_kernel, half), name='temps_west' i...  6.27 us
    ppermute x1, starting transfers between devices, per_device(): odd_halo = lax.ppermute(odd_rows, ('bx', 'by'), odd_pairs)  6.23 us
    pallas_call x1, Pallas kernels, per_device(): pl.pallas_call(motion_kernel, name='motion', in_specs=[here] * 7, out_spe...  6.04 us
    ppermute x1, starting transfers between devices, per_device(): east = lax.ppermute(left, 'bx', [((q + 1) % n_bx, q) for q in range(n_bx)])  4.82 us
    unnamed x8, local copies, waits for them, and re-layouts  1.91 us
    pallas_call x1, Pallas kernels, per_device(): pl.pallas_call(rows_kernel, name='edge_rows', grid=(1,), in_specs=[slab(2...  1.7 us
    ppermute x1, starting transfers between devices, per_device(): west = lax.ppermute(right, 'bx', [(q, (q + 1) % n_bx) for q in range(n_bx)])  1.28 us
  transfers between devices with their start and end apart: 4, of which 0 were waited for; matrix products, arithmetic and copies ran while one was open for 0% of the time, Pallas kernels for 15%

profile of v4, /device:TPU:25, one launch (start us, length us, event | category | flops | bytes accessed | tf_op | source)
XLA Modules:
  0.0 40.6 jit_solution(8084711400385333704)
XLA Ops:
  0.6 10.5 %thermo.1 = (f32[5,128,256]{2,1,0:T(8,128)}, f32[6,128,256]{2,1,0:T(8,128)}, f32[4,8,40,8,128]{4,3,2,1,0:T(8,128)}, s32[256,128]{1,0:T(8,128)}, f32[128,128]{1,0:T(8,128)}, /*index=5*/f32[128,128]{1,0:T(8,128)}) custom-call(s32[1,6144]{1,0:T(1,128)} %bitcast.1, f32[40,128,256]{2,1,0:T(8,128)} %temps_hbm.5, f32[5,128,256]{2,1,0:T(8,128)} %thick_hbm.1, ...), custom_call_target="tpu_custom_call" | custom-call | tf_op jit(solution)/shard_map/thermo/pallas_call | solution.py:611
  11.2 1.3 %collective-permute-start = (f32[128,128]{1,0:T(8,128)}, f32[128,128]{1,0:T(8,128)S(1)}, u32[]{:S(2)}, u32[]{:S(2)}) collective-permute-start(f32[128,128]{1,0:T(8,128)} %get-tuple-element.20), channel_id=1, source_target_pairs={{0,8},{8,16},{16,24},{24,32},{32,40},{40,48},{48,56},{56,64},{64,7... | collective-permute-start | bytes 196616 | tf_op jit(solution)/shard_map/ppermute | solution.py:662
  12.4 4.8 %collective-permute-start.1 = (f32[128,128]{1,0:T(8,128)}, f32[128,128]{1,0:T(8,128)S(1)}, u32[]{:S(2)}, u32[]{:S(2)}) collective-permute-start(f32[128,128]{1,0:T(8,128)} %get-tuple-element.21), channel_id=1, source_target_pairs={{8,0},{16,8},{24,16},{32,24},{40,32},{48,40},{56,48},{64,56},{72,6... | collective-permute-start | bytes 196616 | tf_op jit(solution)/shard_map/ppermute | solution.py:663
  17.3 3.1 %temps_west.1.rest_0_ = f32[40,128,256]{2,1,0:T(8,128)} custom-call(f32[40,128,256]{2,1,0:T(8,128)} %temps_hbm.5, f32[4,8,40,8,128]{4,3,2,1,0:T(8,128)} %get-tuple-element.17.result_hbm, s32[256,128]{1,0:T(8,128)} %get-tuple-element.18.place_hbm), custom_call_target="tpu_custom_call" | custom-call | flops 20000000 | bytes 6000000 | tf_op jit(solution)/shard_map/temps_west/pallas_call | solution.py:641
  20.4 0.0 collective-permute-done.west_low.west_high.west_hbm
  20.4 0.0 copy-start
  20.4 0.0 collective-permute-done.1.east_low.east_high.east_hbm
  20.4 0.0 copy-start.1
  20.4 0.6 %copy-done = f32[128,128]{1,0:T(8,128)} copy-done((f32[128,128]{1,0:T(8,128)}, f32[128,128]{1,0:T(8,128)S(1)}, u32[]{:S(2)}) %copy-start) | copy-done | bytes 65560
  21.0 0.0 copy-done.1
  21.1 1.7 %edge_rows.1 = (f32[11,3,8,128]{3,2,1,0:T(8,128)}, f32[11,3,8,128]{3,2,1,0:T(8,128)}) custom-call(f32[2,128,256]{2,1,0:T(8,128)} %vel_hbm.3, f32[3,128,256]{2,1,0:T(8,128)} %stress_hbm.3, f32[6,128,256]{2,1,0:T(8,128)} %get-tuple-element.19.forcing_low.forcing_high.forcing_hbm, f32[128,128]{1,0:T(8,128)} %copy-done, f32[128,128]{1,0:T(8,128)} %copy-done.1, ...), custom_call_target="tpu_custom_call" | custom-call | tf_op jit(solution)/shard_map/edge_rows/pallas_call | solution.py:675
  22.8 1.0 %collective-permute-start.2 = (f32[11,3,8,128]{3,2,1,0:T(8,128)}, f32[11,3,8,128]{3,2,1,0:T(8,128)S(1)}, u32[]{:S(2)}, u32[]{:S(2)}) collective-permute-start(f32[11,3,8,128]{3,2,1,0:T(8,128)} %get-tuple-element.26), channel_id=1, source_target_pairs={{0,1},{1,0},{2,3},{3,2},{4,5},{5,4},{6,7},{7,6},{8,9},{9,8},{10,11... | collective-permute-start | bytes 405512 | tf_op jit(solution)/shard_map/ppermute | solution.py:697
  23.7 6.2 %collective-permute-start.3 = (f32[11,3,8,128]{3,2,1,0:T(8,128)}, f32[11,3,8,128]{3,2,1,0:T(8,128)S(1)}, u32[]{:S(2)}, u32[]{:S(2)}) collective-permute-start(f32[11,3,8,128]{3,2,1,0:T(8,128)} %get-tuple-element.27), channel_id=1, source_target_pairs={{1,2},{2,1},{3,4},{4,3},{5,6},{6,5},{7,127},{9,10},{10,9},{11,12},... | collective-permute-start | bytes 405512 | tf_op jit(solution)/shard_map/ppermute | solution.py:696
  30.0 3.1 %temps_east.1 = f32[40,128,256]{2,1,0:T(8,128)} custom-call(f32[40,128,256]{2,1,0:T(8,128)} %temps_hbm.5, f32[4,8,40,8,128]{4,3,2,1,0:T(8,128)} %get-tuple-element.17.result_hbm, s32[256,128]{1,0:T(8,128)} %get-tuple-element.18.place_hbm, f32[40,128,256]{2,1,0:T(8,128)} %temps_west.1.rest_0_), custom_call_target="tpu_custom_call", output_to_operand_aliasing={{}: (3, {})} | custom-call | flops 20000000 | bytes 6000000 | tf_op jit(solution)/shard_map/temps_east/pallas_call | solution.py:641
  33.1 0.0 collective-permute-done.2.even_hbm
  33.1 0.0 copy-start.2
  33.1 0.0 collective-permute-done.3.odd_hbm
  33.1 0.6 %copy-done.2 = f32[11,3,8,128]{3,2,1,0:T(8,128)} copy-done((f32[11,3,8,128]{3,2,1,0:T(8,128)}, f32[11,3,8,128]{3,2,1,0:T(8,128)S(1)}, u32[]{:S(2)}) %copy-start.2) | copy-done | bytes 135192
  33.8 0.0 copy-start.3
  33.8 0.7 %copy-done.3 = f32[11,3,8,128]{3,2,1,0:T(8,128)} copy-done((f32[11,3,8,128]{3,2,1,0:T(8,128)}, f32[11,3,8,128]{3,2,1,0:T(8,128)S(1)}, u32[]{:S(2)}) %copy-start.3) | copy-done | bytes 135192
  34.4 6.0 %motion.1 = (f32[2,128,256]{2,1,0:T(8,128)}, f32[3,128,256]{2,1,0:T(8,128)}) custom-call(f32[2,128,256]{2,1,0:T(8,128)} %vel_hbm.3, f32[3,128,256]{2,1,0:T(8,128)} %stress_hbm.3, f32[6,128,256]{2,1,0:T(8,128)} %get-tuple-element.19.forcing_low.forcing_high.forcing_hbm, f32[128,128]{1,0:T(8,128)} %copy-done, f32[128,128]{1,0:T(8,128)} %copy-done.1, ...), custom_call_target="tpu_custom_call" | custom-call | tf_op jit(solution)/shard_map/motion/pallas_call | solution.py:701
Async XLA Ops:
  11.2 9.2 %collective-permute-start = (f32[128,128]{1,0:T(8,128)}, f32[128,128]{1,0:T(8,128)S(1)}, u32[]{:S(2)}, u32[]{:S(2)}) collective-permute-start(f32[128,128]{1,0:T(8,128)} %get-tuple-element.20), channel_id=1, source_target_pairs={{0,8},{8,16},{16,24},{24,32},{32,40},{40,48},{48,56},{56,64},{64,7... | collective-permute-start | bytes 196616 | tf_op jit(solution)/shard_map/ppermute | solution.py:662
  12.4 8.0 %collective-permute-start.1 = (f32[128,128]{1,0:T(8,128)}, f32[128,128]{1,0:T(8,128)S(1)}, u32[]{:S(2)}, u32[]{:S(2)}) collective-permute-start(f32[128,128]{1,0:T(8,128)} %get-tuple-element.21), channel_id=1, source_target_pairs={{8,0},{16,8},{24,16},{32,24},{40,32},{48,40},{56,48},{64,56},{72,6... | collective-permute-start | bytes 196616 | tf_op jit(solution)/shard_map/ppermute | solution.py:663
  20.4 0.6 %copy-start = (f32[128,128]{1,0:T(8,128)}, f32[128,128]{1,0:T(8,128)S(1)}, u32[]{:S(2)}) copy-start(f32[128,128]{1,0:T(8,128)S(1)} %collective-permute-done.west_low.west_high.west_hbm) | copy-start | bytes 196612
  20.4 0.6 %copy-start.1 = (f32[128,128]{1,0:T(8,128)}, f32[128,128]{1,0:T(8,128)S(1)}, u32[]{:S(2)}) copy-start(f32[128,128]{1,0:T(8,128)S(1)} %collective-permute-done.1.east_low.east_high.east_hbm) | copy-start | bytes 196612
  22.8 10.3 %collective-permute-start.2 = (f32[11,3,8,128]{3,2,1,0:T(8,128)}, f32[11,3,8,128]{3,2,1,0:T(8,128)S(1)}, u32[]{:S(2)}, u32[]{:S(2)}) collective-permute-start(f32[11,3,8,128]{3,2,1,0:T(8,128)} %get-tuple-element.26), channel_id=1, source_target_pairs={{0,1},{1,0},{2,3},{3,2},{4,5},{5,4},{6,7},{7,6},{8,9},{9,8},{10,11... | collective-permute-start | bytes 405512 | tf_op jit(solution)/shard_map/ppermute | solution.py:697
  23.7 9.4 %collective-permute-start.3 = (f32[11,3,8,128]{3,2,1,0:T(8,128)}, f32[11,3,8,128]{3,2,1,0:T(8,128)S(1)}, u32[]{:S(2)}, u32[]{:S(2)}) collective-permute-start(f32[11,3,8,128]{3,2,1,0:T(8,128)} %get-tuple-element.27), channel_id=1, source_target_pairs={{1,2},{2,1},{3,4},{4,3},{5,6},{6,5},{7,127},{9,10},{10,9},{11,12},... | collective-permute-start | bytes 405512 | tf_op jit(solution)/shard_map/ppermute | solution.py:696
  33.1 0.6 %copy-start.2 = (f32[11,3,8,128]{3,2,1,0:T(8,128)}, f32[11,3,8,128]{3,2,1,0:T(8,128)S(1)}, u32[]{:S(2)}) copy-start(f32[11,3,8,128]{3,2,1,0:T(8,128)S(1)} %collective-permute-done.2.even_hbm) | copy-start | bytes 405508
  33.8 0.7 %copy-start.3 = (f32[11,3,8,128]{3,2,1,0:T(8,128)}, f32[11,3,8,128]{3,2,1,0:T(8,128)S(1)}, u32[]{:S(2)}) copy-start(f32[11,3,8,128]{3,2,1,0:T(8,128)S(1)} %collective-permute-done.3.odd_hbm) | copy-start | bytes 405508

commit v5 on v4

--- a/solution.py
+++ b/solution.py
@@ -25,7 +25,7 @@
 TEAM = 4
 PAIR = 2
 TURNS = TILES // (TEAM * PAIR)
-HEIGHT = FLAT // TURNS
+HEIGHT = ROWS // TURNS
 BLOCK = 13
 
 FREEZING = -1.8
@@ -99,7 +99,11 @@
     zero = jnp.bfloat16(0.0)
     for start in range(0, list_ref.shape[1], step):
         cells = list_ref[:, start : start + step]
-        row = lax.shift_right_arithmetic(cells, 8) + (lax.bitwise_and(cells, 128))
+        row = (
+            lax.bitwise_and(lax.shift_right_arithmetic(cells, 7), 0xF0)
+            + lax.bitwise_and(lax.shift_right_arithmetic(cells, 4), 8)
+            + lax.bitwise_and(lax.shift_right_arithmetic(cells, 8), 7)
+        )
         row = jnp.where(cells >= 0, row, -1).astype(jnp.float32).astype(jnp.bfloat16)
         lane = lax.bitwise_and(cells, 127).astype(jnp.float32).astype(jnp.bfloat16)
         total = total + lax.dot_general(
@@ -158,11 +162,11 @@
     for start in range(0, len(planes), BLOCK):
         block = planes[start : start + BLOCK]
         values = [None] * len(block)
-        for at, spot in picks:
+        for (rows, lanes), spot in picks:
             inside = spot >= 0
             spot = jnp.maximum(spot, 0)
             for k, (ref, p) in enumerate(block):
-                value = jnp.take_along_axis(ref[p, at, :], spot, axis=1)
+                value = jnp.take_along_axis(ref[p, rows, lanes], spot, axis=1)
                 values[k] = value if values[k] is None else jnp.where(inside, value, values[k])
         for k, value in enumerate(values):
             gathered_ref[start + k] = value
@@ -180,35 +184,44 @@
         result_ref[STACKED + cat] = thick + (growth - 0.0005 * heat)
 
 
-def field_of(i, moving, forcing):
-    return (moving, i) if i < 5 else (forcing, i - 5)
+def tiles_of(team):
+    tiles = []
+    for u in range(TEAM):
+        row = (team * (TEAM // 2) + u // 2) * 8
+        flat = (team * TEAM + u) * 8
+        if not isinstance(team, int):
+            row, flat = pl.multiple_of(row, 8), pl.multiple_of(flat, 8)
+        lanes = slice((u % 2) * LANES, (u % 2) * LANES + LANES)
+        tiles.append(((pl.ds(row, 8), lanes), pl.ds(flat, 8)))
+    return tiles
 
 
 def spread_team(tiles, level, place_ref, source_ref, result_ref, fresh_ref, planes, skip=0):
-    for at in tiles:
-        place = place_ref[at, :] - level * LANES
+    for (rows, lanes), flat in tiles:
+        place = place_ref[flat, :] - level * LANES
         inside = jnp.logical_and(place >= 0, place < LANES)
         spot = jnp.where(inside, place, 0)
         for p in planes:
             value = jnp.take_along_axis(result_ref[p], spot, axis=1)
-            fresh_ref[p - skip, at, :] = jnp.where(inside, value, source_ref[p, at, :])
+            before = source_ref[p, rows, lanes] if source_ref is not None else fresh_ref[p - skip, rows, lanes]
+            fresh_ref[p - skip, rows, lanes] = jnp.where(inside, value, before)
 
 
 def thermo_kernel(
-    list_ref, temps_hbm, thick_hbm, snow_hbm, area_hbm, air_hbm, heat_hbm,
+    list_hbm, temps_hbm, thick_hbm, snow_hbm, area_hbm, air_hbm, heat_hbm,
     vel_hbm, stress_hbm, wind_hbm, ocean_hbm, cells_hbm,
-    thick_out, forcing_out, result_out, place_out, left_out, right_out,
-    kept_ref, fresh_ref, snow_ref, area_ref, single_ref, moving_ref, drive_ref, cells_ref, forcing_ref,
+    thick_out, state_out, result_out, place_out, left_out, right_out,
+    list_ref, kept_ref, fresh_ref, snow_ref, area_ref, single_ref, drive_ref, cells_ref, state_ref,
     mask_ref, base_ref, count_ref, inverse_ref, place_ref, spot_ref,
-    gathered_a, gathered_b, result_ref, in_sem, out_sem, result_sem, extra_sem,
+    gathered_a, gathered_b, result_ref, edge_ref, in_sem, out_sem, move_sem, result_sem, extra_sem,
 ):
     band = lax.axis_index("by")
     north = lax.axis_size("by") * ROWS
+    teams = TILES // TEAM
+    listing = pltpu.make_async_copy(list_hbm, list_ref, extra_sem)
+    listing.start()
 
     def fetch(turn):
-        half, inner = turn // (TURNS // 2), turn % (TURNS // 2)
-        span = slice(half * LANES, half * LANES + LANES)
-        there = slice(inner * HEIGHT, inner * HEIGHT + HEIGHT)
         rows = slice(turn * HEIGHT, turn * HEIGHT + HEIGHT)
         copies = []
         for source, target in (
@@ -221,82 +234,79 @@
             (wind_hbm, drive_ref.at[0:2]),
             (ocean_hbm, drive_ref.at[2:4]),
             (cells_hbm, cells_ref),
-            (vel_hbm, moving_ref.at[0:2]),
-            (stress_hbm, moving_ref.at[2:5]),
         ):
             sem = in_sem.at[turn, len(copies)]
             if len(source.shape) == 3:
-                copies.append(pltpu.make_async_copy(source.at[:, there, span], target.at[:, rows, :], sem))
+                copies.append(pltpu.make_async_copy(source.at[:, rows, :], target.at[:, rows, :], sem))
             else:
-                copies.append(pltpu.make_async_copy(source.at[there, span], target.at[rows, :], sem))
+                copies.append(pltpu.make_async_copy(source.at[rows, :], target.at[rows, :], sem))
         return copies
 
     def send(turn):
-        half, inner = turn // (TURNS // 2), turn % (TURNS // 2)
-        span = slice(half * LANES, half * LANES + LANES)
-        there = slice(inner * HEIGHT, inner * HEIGHT + HEIGHT)
         rows = slice(turn * HEIGHT, turn * HEIGHT + HEIGHT)
         return [
-            pltpu.make_async_copy(fresh_ref.at[:, rows, :], thick_out.at[:, there, span], out_sem.at[turn, 0]),
-            pltpu.make_async_copy(forcing_ref.at[:, rows, :], forcing_out.at[:, there, span], out_sem.at[turn, 1]),
+            pltpu.make_async_copy(fresh_ref.at[:, rows, :], thick_out.at[:, rows, :], out_sem.at[turn, 0]),
+            pltpu.make_async_copy(state_ref.at[:, :, rows, :], state_out.at[:, :, rows, :], out_sem.at[turn, 1]),
         ]
 
     fetched = [fetch(turn) for turn in range(TURNS)]
-    for copies in fetched:
+    moved = []
+    for half in range(2):
+        span = slice(half * LANES, half * LANES + LANES)
+        moved.append(pltpu.make_async_copy(vel_hbm.at[:, :, span], state_ref.at[0:2, half], move_sem.at[half, 0]))
+        moved.append(pltpu.make_async_copy(stress_hbm.at[:, :, span], state_ref.at[2:5, half], move_sem.at[half, 1]))
+    for copies in fetched + [moved]:
         for copy in copies:
             copy.start()
+    listing.wait()
     most = index_cells(list_ref, mask_ref, base_ref, count_ref, inverse_ref, place_ref, spot_ref)
-    sent = [pltpu.make_async_copy(place_ref, place_out, result_sem.at[TILES // TEAM])]
+    sent = [pltpu.make_async_copy(place_ref, place_out, result_sem.at[teams])]
     sent[0].start()
     lane = lax.broadcasted_iota(jnp.int32, (8, LANES), 1)
     buffers = (gathered_a, gathered_b)
     thick_planes = range(STACKED, KEPT)
 
-    def tiles_of(team):
-        return [pl.ds(pl.multiple_of((team * TEAM + u) * 8, 8), 8) for u in range(TEAM)]
-
     def force(turn):
-        at = slice(turn * HEIGHT, turn * HEIGHT + HEIGHT)
-        ice = mask_ref[at, :]
-        load = jnp.zeros(ice.shape, jnp.float32)
-        area_total = jnp.zeros(ice.shape, jnp.float32)
-        for cat in range(CATS):
-            area = area_ref[cat, at, :]
-            load = load + area * fresh_ref[cat, at, :]
-            area_total = area_total + area
-        load = ice * load
-        mass = 0.9 * load
-        row = lax.broadcasted_iota(jnp.int32, (HEIGHT, LANES), 0) + (turn % (TURNS // 2)) * HEIGHT + band * ROWS
-        latitude = row.astype(jnp.float32) + 0.5
-        turning = 1.4 * jnp.sin(0.5 * jnp.pi * (2.0 * latitude / north - 1.0)) * mass
-        diagonal = mass + 1.0
-        scale = cells_ref[at, :].astype(jnp.float32) / (diagonal * diagonal + turning * turning)
-        forcing_ref[0, at, :] = drive_ref[0, at, :] + drive_ref[2, at, :]
-        forcing_ref[1, at, :] = drive_ref[1, at, :] + drive_ref[3, at, :]
-        forcing_ref[2, at, :] = diagonal * scale
-        forcing_ref[3, at, :] = load * jnp.exp(-20.0 * (1.0 - area_total))
-        forcing_ref[4, at, :] = mass
-        forcing_ref[5, at, :] = turning * scale
+        for inner in range(HEIGHT // 8):
+            start = turn * HEIGHT + inner * 8
+            rows = slice(start, start + 8)
+            row = lax.broadcasted_iota(jnp.int32, (8, LANES), 0) + start + band * ROWS
+            latitude = row.astype(jnp.float32) + 0.5
+            coriolis = 1.4 * jnp.sin(0.5 * jnp.pi * (2.0 * latitude / north - 1.0))
+            for half in range(2):
+                lanes = slice(half * LANES, half * LANES + LANES)
+                ice = mask_ref[2 * start + 8 * half : 2 * start + 8 * half + 8, :]
+                load = jnp.zeros(ice.shape, jnp.float32)
+                area_total = jnp.zeros(ice.shape, jnp.float32)
+                for cat in range(CATS):
+                    area = area_ref[cat, rows, lanes]
+                    load = load + area * fresh_ref[cat, rows, lanes]
+                    area_total = area_total + area
+                load = ice * load
+                mass = 0.9 * load
+                turning = coriolis * mass
+                diagonal = mass + 1.0
+                scale = cells_ref[rows, lanes].astype(jnp.float32) / (diagonal * diagonal + turning * turning)
+                state_ref[5, half, rows, :] = drive_ref[0, rows, lanes] + drive_ref[2, rows, lanes]
+                state_ref[6, half, rows, :] = drive_ref[1, rows, lanes] + drive_ref[3, rows, lanes]
+                state_ref[7, half, rows, :] = diagonal * scale
+                state_ref[8, half, rows, :] = load * jnp.exp(-20.0 * (1.0 - area_total))
+                state_ref[9, half, rows, :] = mass
+                state_ref[10, half, rows, :] = turning * scale
 
     def extra(team):
         def one(level, carry):
             tiles = tiles_of(team)
             picks = []
-            for at in tiles:
-                rank = lane + level * LANES - base_ref[at, :]
-                inside = jnp.logical_and(rank >= 0, rank < count_ref[at, :])
-                spot = jnp.take_along_axis(inverse_ref[at, :], jnp.where(inside, rank, 0), axis=1)
+            for at, flat in tiles:
+                rank = lane + level * LANES - base_ref[flat, :]
+                inside = jnp.logical_and(rank >= 0, rank < count_ref[flat, :])
+                spot = jnp.take_along_axis(inverse_ref[flat, :], jnp.where(inside, rank, 0), axis=1)
                 picks.append((at, jnp.where(inside, spot, -1)))
             gather_team(picks, kept_ref, snow_ref, single_ref, gathered_a)
-            solve_team(gathered_a, result_ref.at[TILES // TEAM])
-            for at in tiles:
-                place = place_ref[at, :] - level * LANES
-                inside = jnp.logical_and(place >= 0, place < LANES)
-                spot = jnp.where(inside, place, 0)
-                for p in thick_planes:
-                    value = jnp.take_along_axis(result_ref[TILES // TEAM, p], spot, axis=1)
-                    fresh_ref[p - STACKED, at, :] = jnp.where(inside, value, fresh_ref[p - STACKED, at, :])
-            copy = pltpu.make_async_copy(result_ref.at[TILES // TEAM, :STACKED], result_out.at[level, team], extra_sem)
+            solve_team(gathered_a, result_ref.at[teams])
+            spread_team(tiles, level, place_ref, None, result_ref.at[teams], fresh_ref, thick_planes, STACKED)
+            copy = pltpu.make_async_copy(result_ref.at[teams, :STACKED], result_out.at[level, team], extra_sem)
             copy.start()
             copy.wait()
             return carry
@@ -306,12 +316,16 @@
     for turn in range(TURNS):
         for copy in fetched[turn]:
             copy.wait()
-        teams = [turn * PAIR + k for k in range(PAIR)]
-        for k, team in enumerate(teams):
-            gather_team([(at, spot_ref[at, :]) for at in tiles_of(team)], kept_ref, snow_ref, single_ref, buffers[k % 2])
-        for k, team in enumerate(teams):
+        if turn == 0:
+            for copy in moved:
+                copy.wait()
+        mine = [turn * PAIR + k for k in range(PAIR)]
+        for k, team in enumerate(mine):
+            picks = [(at, spot_ref[flat, :]) for at, flat in tiles_of(team)]
+            gather_team(picks, kept_ref, snow_ref, single_ref, buffers[k % 2])
+        for k, team in enumerate(mine):
             solve_team(buffers[k % 2], result_ref.at[team])
-        for k, team in enumerate(teams):
+        for k, team in enumerate(mine):
             spread_team(tiles_of(team), 0, place_ref, kept_ref, result_ref.at[team], fresh_ref, thick_planes, STACKED)
             copy = pltpu.make_async_copy(result_ref.at[team, :STACKED], result_out.at[0, team], result_sem.at[team])
             copy.start()
@@ -329,45 +343,44 @@
         def again(team, carry):
             return lax.fori_loop(1, TEAM, extra(team), carry)
 
-        lax.fori_loop(0, TILES // TEAM, again, 0)
+        lax.fori_loop(0, teams, again, 0)
         for turn in range(TURNS):
             force(turn)
         for copy in sent:
             copy.start()
 
-    def pack(tile, carry):
-        group = lax.shift_right_logical(lane, 3)
-        for out_ref, half, push in ((left_out, 0, 0), (right_out, 1, 8)):
-            at = pl.ds(pl.multiple_of(tile * 8 + half * ROWS, 8), 8)
+    group = lax.shift_right_logical(lane, 3)
+    edges = []
+    for half, push, target in ((1, 8, right_out), (0, 0, left_out)):
+        for tile in range(ROWS // 8):
             packed = jnp.zeros((8, LANES), jnp.float32)
             for i in range(FIELDS):
-                ref, k = field_of(i, moving_ref, forcing_ref)
-                x = ref[k, at, :]
+                x = state_ref[i, half, 8 * tile : 8 * tile + 8, :]
                 turn = (8 * i + push) % LANES
                 if turn:
                     x = pltpu.roll(x, turn, axis=1)
                 packed = jnp.where(group == i, x, packed)
-            out_ref[pl.ds(pl.multiple_of(tile * 8, 8), 8), :] = packed
-        return carry
-
-    lax.fori_loop(0, ROWS // 8, pack, 0, unroll=True)
-    for copy in sent:
+            edge_ref[half, 8 * tile : 8 * tile + 8, :] = packed
+        copy = pltpu.make_async_copy(edge_ref.at[half], target, move_sem.at[half, 2])
+        copy.start()
+        edges.append(copy)
+    for copy in sent + edges:
         copy.wait()
 
 
 def temps_kernel(half, temps_hbm, result_hbm, place_hbm, *rest):
     temps_out, kept_ref, fresh_ref, place_ref, result_ref, in_sem, out_sem, extra_sem = rest[-8:]
     teams = TILES // TEAM // 2
-    height = TEAM * 8
-    span = slice(half * LANES, half * LANES + LANES)
-    rows = slice(half * ROWS, half * ROWS + ROWS)
-    whole = pltpu.make_async_copy(place_hbm.at[rows, :], place_ref, extra_sem)
+    height = TEAM * 4
+    skip = half * (ROWS // 2)
+    whole = pltpu.make_async_copy(place_hbm.at[half * ROWS : half * ROWS + ROWS, :], place_ref, extra_sem)
     whole.start()
     fetched = []
     for k in range(teams):
         here = slice(k * height, k * height + height)
+        there = slice(skip + k * height, skip + k * height + height)
         fetched.append([
-            pltpu.make_async_copy(temps_hbm.at[:, here, span], kept_ref.at[:, here, :], in_sem.at[k, 0]),
+            pltpu.make_async_copy(temps_hbm.at[:, there, :], kept_ref.at[:, here, :], in_sem.at[k, 0]),
             pltpu.make_async_copy(result_hbm.at[0, half * teams + k], result_ref.at[k], in_sem.at[k, 1]),
         ])
     for copies in fetched:
@@ -379,9 +392,9 @@
         for copy in fetched[k]:
             copy.wait()
         here = slice(k * height, k * height + height)
-        tiles = [slice(k * height + 8 * u, k * height + 8 * u + 8) for u in range(TEAM)]
-        spread_team(tiles, 0, place_ref, kept_ref, result_ref.at[k], fresh_ref, range(STACKED))
-        copy = pltpu.make_async_copy(fresh_ref.at[:, here, :], temps_out.at[:, here, span], out_sem.at[k])
+        there = slice(skip + k * height, skip + k * height + height)
+        spread_team(tiles_of(k), 0, place_ref, kept_ref, result_ref.at[k], fresh_ref, range(STACKED))
+        copy = pltpu.make_async_copy(fresh_ref.at[:, here, :], temps_out.at[:, there, :], out_sem.at[k])
         copy.start()
         sent.append(copy)
 
@@ -396,14 +409,7 @@
             copy = pltpu.make_async_copy(result_hbm.at[level, half * teams + team], result_ref.at[0], extra_sem)
             copy.start()
             copy.wait()
-            for u in range(TEAM):
-                at = pl.ds(pl.multiple_of(team * height + 8 * u, 8), 8)
-                place = place_ref[at, :] - level * LANES
-                inside = jnp.logical_and(place >= 0, place < LANES)
-                spot = jnp.where(inside, place, 0)
-                for p in range(STACKED):
-                    value = jnp.take_along_axis(result_ref[0, p], spot, axis=1)
-                    fresh_ref[p, at, :] = jnp.where(inside, value, fresh_ref[p, at, :])
+            spread_team(tiles_of(team), level, place_ref, None, result_ref.at[0], fresh_ref, range(STACKED))
             return carry
 
         lax.fori_loop(0, teams * (TEAM - 1), again, 0)
@@ -422,21 +428,17 @@
     return jnp.where(lane < DEEP, east_side, jnp.where(lane >= LANES - DEEP, west_side, zero))
 
 
-def rows_kernel(
-    vel_low, stress_low, forcing_low, west_low, east_low,
-    vel_high, stress_high, forcing_high, west_high, east_high, even_out, odd_out,
-):
+def rows_kernel(state_low, west_low, east_low, state_high, west_high, east_high, even_out, odd_out):
     even = lax.rem(lax.axis_index("by"), 2) == 0
 
     def fill(to_low, to_high):
-        for out, vel_ref, stress_ref, forcing_ref, west_ref, east_ref in (
-            (to_low, vel_low, stress_low, forcing_low, west_low, east_low),
-            (to_high, vel_high, stress_high, forcing_high, west_high, east_high),
+        for out, state_ref, west_ref, east_ref in (
+            (to_low, state_low, west_low, east_low),
+            (to_high, state_high, west_high, east_high),
         ):
             for i in range(FIELDS):
-                ref, at = (vel_ref, i) if i < 2 else (stress_ref, i - 2) if i < 5 else (forcing_ref, i - 5)
-                out[i, 0] = ref[at, :, :LANES]
-                out[i, 1] = ref[at, :, LANES:]
+                out[i, 0] = state_ref[i, 0]
+                out[i, 1] = state_ref[i, 1]
                 out[i, 2] = halo_tile(west_ref[...], east_ref[...], i, DEEP)
 
     @pl.when(even)
@@ -455,7 +457,7 @@
 
 
 def motion_kernel(
-    vel_hbm, stress_hbm, forcing_hbm, west_hbm, east_hbm, even_hbm, odd_hbm,
+    state_hbm, west_hbm, east_hbm, even_hbm, odd_hbm,
     vel_out, stress_out, state_ref, west_ref, east_ref, even_ref, odd_ref, in_sem, halo_sem, out_sem,
 ):
     spot = lax.axis_index("by")
@@ -471,15 +473,9 @@
     high = slice(2 * DEEP + ROWS, 3 * DEEP + ROWS)
     copies = []
     for tile in range(2):
-        span = slice(tile * LANES, tile * LANES + LANES)
-        for number, (source, target) in enumerate((
-            (vel_hbm, state_ref.at[0:2, tile, mid, :]),
-            (stress_hbm, state_ref.at[2:5, tile, mid, :]),
-            (forcing_hbm, state_ref.at[5:11, tile, mid, :]),
-        )):
-            copy = pltpu.make_async_copy(source.at[:, :, span], target, in_sem.at[tile, number])
-            copy.start()
-            copies.append(copy)
+        copy = pltpu.make_async_copy(state_hbm.at[:, tile], state_ref.at[:, tile, mid, :], in_sem.at[tile])
+        copy.start()
+        copies.append(copy)
     for copy in halos:
         copy.wait()
     blank = jnp.zeros((DEEP, LANES), jnp.float32)
@@ -599,36 +595,39 @@
 ):
     f32 = jnp.float32
     i32 = jnp.int32
-    vmem = pl.BlockSpec(memory_space=pltpu.VMEM)
     here = pl.BlockSpec(memory_space=pl.ANY)
     listed = ice_cols.reshape(1, -1)
 
-    def flat(n, kind=f32):
-        return pltpu.VMEM((n, FLAT, LANES), kind)
+    def planes(n):
+        return pltpu.VMEM((n, ROWS, COLS), f32)
 
     one = pltpu.VMEM((FLAT, LANES), i32)
     teams = TILES // TEAM
-    thick_new, forcing, result, place, left, right = pl.pallas_call(
+    thick_new, state, result, place, left, right = pl.pallas_call(
         thermo_kernel,
         name="thermo",
-        in_specs=[vmem] + [here] * 11,
-        out_specs=[here, here, here, here, vmem, vmem],
+        in_specs=[here] * 12,
+        out_specs=[here] * 6,
         out_shape=[
             jax.ShapeDtypeStruct((CATS, ROWS, COLS), f32),
-            jax.ShapeDtypeStruct((6, ROWS, COLS), f32),
+            jax.ShapeDtypeStruct((FIELDS, 2, ROWS, LANES), f32),
             jax.ShapeDtypeStruct((TEAM, teams, STACKED, 8, LANES), f32),
             jax.ShapeDtypeStruct((FLAT, LANES), i32),
             jax.ShapeDtypeStruct((ROWS, LANES), f32),
             jax.ShapeDtypeStruct((ROWS, LANES), f32),
         ],
         scratch_shapes=[
-            flat(KEPT), flat(CATS), flat(CATS), flat(CATS), flat(2), flat(5), flat(4), one, flat(6),
+            pltpu.VMEM(listed.shape, i32),
+            planes(KEPT), planes(CATS), planes(CATS), planes(CATS), planes(2), planes(4),
+            pltpu.VMEM((ROWS, COLS), i32), pltpu.VMEM((FIELDS, 2, ROWS, LANES), f32),
             pltpu.VMEM((FLAT, LANES), f32), one, one, one, one, one,
             pltpu.VMEM((KEPT + CATS + 2, 8, LANES), f32),
             pltpu.VMEM((KEPT + CATS + 2, 8, LANES), f32),
             pltpu.VMEM((teams + 1, KEPT, 8, LANES), f32),
-            pltpu.SemaphoreType.DMA((TURNS, 11)),
+            pltpu.VMEM((2, ROWS, LANES), f32),
+            pltpu.SemaphoreType.DMA((TURNS, 9)),
             pltpu.SemaphoreType.DMA((TURNS, 2)),
+            pltpu.SemaphoreType.DMA((2, 3)),
             pltpu.SemaphoreType.DMA((teams + 1,)),
             pltpu.SemaphoreType.DMA,
         ],
@@ -640,15 +639,15 @@
     def renew(half, *before):
         return pl.pallas_call(
             functools.partial(temps_kernel, half),
-            name="temps_west" if half == 0 else "temps_east",
+            name="temps_low" if half == 0 else "temps_high",
             in_specs=[here] * (3 + len(before)),
             out_specs=here,
             out_shape=jax.ShapeDtypeStruct((STACKED, ROWS, COLS), f32),
             input_output_aliases={3: 0} if before else {},
             cost_estimate=pl.CostEstimate(flops=20_000_000, transcendentals=0, bytes_accessed=6_000_000),
             scratch_shapes=[
-                pltpu.VMEM((STACKED, ROWS, LANES), f32),
-                pltpu.VMEM((STACKED, ROWS, LANES), f32),
+                pltpu.VMEM((STACKED, ROWS // 2, COLS), f32),
+                pltpu.VMEM((STACKED, ROWS // 2, COLS), f32),
                 pltpu.VMEM((ROWS, LANES), i32),
                 pltpu.VMEM((teams // 2, STACKED, 8, LANES), f32),
                 pltpu.SemaphoreType.DMA((teams // 2, 2)),
@@ -664,8 +663,8 @@
     temps_part = renew(0)
     band = jax.ShapeDtypeStruct((FIELDS, 3, DEEP, LANES), f32)
 
-    def slab(n, block):
-        return pl.BlockSpec((n, DEEP, COLS), lambda i: (0, block, 0))
+    def slab(block):
+        return pl.BlockSpec((FIELDS, 2, DEEP, LANES), lambda i: (0, 0, block, 0))
 
     def edge(block):
         return pl.BlockSpec((DEEP, LANES), lambda i: (block, 0))
@@ -676,11 +675,10 @@
         rows_kernel,
         name="edge_rows",
         grid=(1,),
-        in_specs=[slab(2, 0), slab(3, 0), slab(6, 0), edge(0), edge(0)]
-        + [slab(2, final), slab(3, final), slab(6, final), edge(final), edge(final)],
+        in_specs=[slab(0), edge(0), edge(0), slab(final), edge(final), edge(final)],
         out_specs=[halo, halo],
         out_shape=[band, band],
-    )(velocity, stress, forcing, west, east, velocity, stress, forcing, west, east)
+    )(state, west, east, state, west, east)
 
     def at(p, q):
         return q * n_by + p
@@ -701,7 +699,7 @@
     velocity_new, stress_new = pl.pallas_call(
         motion_kernel,
         name="motion",
-        in_specs=[here] * 7,
+        in_specs=[here] * 5,
         out_specs=[here, here],
         out_shape=[
             jax.ShapeDtypeStruct((2, ROWS, COLS), f32),
@@ -710,11 +708,11 @@
         scratch_shapes=[
             pltpu.VMEM((FIELDS, 3, TALL, LANES), f32),
             edge_shape, edge_shape, band_shape, band_shape,
-            pltpu.SemaphoreType.DMA((2, 3)),
+            pltpu.SemaphoreType.DMA((2,)),
             pltpu.SemaphoreType.DMA((4,)),
             pltpu.SemaphoreType.DMA((2, 2)),
         ],
-    )(velocity, stress, forcing, west, east, even_halo, odd_halo)
+    )(state, west, east, even_halo, odd_halo)
     return temps_new, thick_new, velocity_new, stress_new
 
 

time: 40.9 us -> 43.5 us (1.064)
  Pallas kernels: 24.5 us -> 28 us
  starting transfers between devices: 13.3 us -> 12.6 us
    pallas_call x5, Pallas kernels: 24.5 us -> 28 us  [the longest x1 12.4 us: per_device(): pl.pallas_call(thermo_kernel, name='thermo', in_specs=[here] * 12, out_sp...]
    ppermute x1, starting transfers between devices: 6.23 us -> 5.52 us  [per_device(): odd_halo = lax.ppermute(odd_rows, ('bx', 'by'), odd_pairs)]
  transfers between devices with their start and end apart: 4 -> 4, of which waited for: 0 -> 0; matrix products, arithmetic and copies ran while one was open for 0% -> 0% of each run, Pallas kernels for 15% -> 18%
where the time goes in v5:
time: 43.5 us; the launch traced here: 43.3 us
  Pallas kernels  28 us (64%)
  starting transfers between devices  12.6 us (29%)
  local copies, waits for them, and re-layouts  1.89 us (4%)
  between operations  0.73 us (2%)
    pallas_call x1, Pallas kernels, per_device(): pl.pallas_call(thermo_kernel, name='thermo', in_specs=[here] * 12, out_sp...  12.4 us
    pallas_call x2, Pallas kernels, renew(): pl.pallas_call(functools.partial(temps_kernel, half), name='temps_low' if...  7.7 us
    pallas_call x1, Pallas kernels, per_device(): pl.pallas_call(motion_kernel, name='motion', in_specs=[here] * 5, out_spe...  6.22 us
    ppermute x1, starting transfers between devices, per_device(): odd_halo = lax.ppermute(odd_rows, ('bx', 'by'), odd_pairs)  5.52 us
    ppermute x1, starting transfers between devices, per_device(): east = lax.ppermute(left, 'bx', [((q + 1) % n_bx, q) for q in range(n_bx)])  4.82 us
    unnamed x8, local copies, waits for them, and re-layouts  1.89 us
    pallas_call x1, Pallas kernels, per_device(): pl.pallas_call(rows_kernel, name='edge_rows', grid=(1,), in_specs=[slab(0...  1.76 us
    ppermute x1, starting transfers between devices, per_device(): west = lax.ppermute(right, 'bx', [(q, (q + 1) % n_bx) for q in range(n_bx)])  1.28 us
  transfers between devices with their start and end apart: 4, of which 0 were waited for; matrix products, arithmetic and copies ran while one was open for 0% of the time, Pallas kernels for 18%

profile of v5, /device:TPU:25, one launch (start us, length us, event | category | flops | bytes accessed | tf_op | source)
XLA Modules:
  0.0 43.3 jit_solution(15227360905192783265)
XLA Ops:
  0.6 12.4 %thermo.1 = (f32[5,128,256]{2,1,0:T(8,128)}, f32[11,2,128,128]{3,2,1,0:T(8,128)}, f32[4,8,40,8,128]{4,3,2,1,0:T(8,128)}, s32[256,128]{1,0:T(8,128)}, f32[128,128]{1,0:T(8,128)}, /*index=5*/f32[128,128]{1,0:T(8,128)}) custom-call(s32[1,6144]{1,0:T(1,128)} %bitcast.1, f32[40,128,256]{2,1,0:T(8,128)} %temps_hbm.5, f32[5,128,256]{2,1,0:T(8,128)} %thick_hbm.1, ...), custom_call_target="tpu_custom_call" | custom-call | tf_op jit(solution)/shard_map/thermo/pallas_call | solution.py:606
  13.0 1.3 %collective-permute-start = (f32[128,128]{1,0:T(8,128)}, f32[128,128]{1,0:T(8,128)S(1)}, u32[]{:S(2)}, u32[]{:S(2)}) collective-permute-start(f32[128,128]{1,0:T(8,128)} %get-tuple-element.20), channel_id=1, source_target_pairs={{0,8},{8,16},{16,24},{24,32},{32,40},{40,48},{48,56},{56,64},{64,7... | collective-permute-start | bytes 196616 | tf_op jit(solution)/shard_map/ppermute | solution.py:661
  14.3 4.8 %collective-permute-start.1 = (f32[128,128]{1,0:T(8,128)}, f32[128,128]{1,0:T(8,128)S(1)}, u32[]{:S(2)}, u32[]{:S(2)}) collective-permute-start(f32[128,128]{1,0:T(8,128)} %get-tuple-element.21), channel_id=1, source_target_pairs={{8,0},{16,8},{24,16},{32,24},{40,32},{48,40},{56,48},{64,56},{72,6... | collective-permute-start | bytes 196616 | tf_op jit(solution)/shard_map/ppermute | solution.py:662
  19.1 3.8 %temps_low.1.rest_0_ = f32[40,128,256]{2,1,0:T(8,128)} custom-call(f32[40,128,256]{2,1,0:T(8,128)} %temps_hbm.5, f32[4,8,40,8,128]{4,3,2,1,0:T(8,128)} %get-tuple-element.17.result_hbm, s32[256,128]{1,0:T(8,128)} %get-tuple-element.18.place_hbm), custom_call_target="tpu_custom_call" | custom-call | flops 20000000 | bytes 6000000 | tf_op jit(solution)/shard_map/temps_low/pallas_call | solution.py:640
  23.0 0.0 collective-permute-done.west_low.west_high.west_hbm
  23.0 0.0 copy-start
  23.0 0.0 collective-permute-done.1.east_low.east_high.east_hbm
  23.0 0.0 copy-start.1
  23.0 0.6 %copy-done = f32[128,128]{1,0:T(8,128)} copy-done((f32[128,128]{1,0:T(8,128)}, f32[128,128]{1,0:T(8,128)S(1)}, u32[]{:S(2)}) %copy-start) | copy-done | bytes 65560
  23.6 0.0 copy-done.1
  23.6 1.8 %edge_rows.1 = (f32[11,3,8,128]{3,2,1,0:T(8,128)}, f32[11,3,8,128]{3,2,1,0:T(8,128)}) custom-call(f32[11,2,128,128]{3,2,1,0:T(8,128)} %get-tuple-element.19.state_low.state_high.state_hbm, f32[128,128]{1,0:T(8,128)} %copy-done, f32[128,128]{1,0:T(8,128)} %copy-done.1, f32[11,2,128,128]{3,2,1,0:T(8,128)} %get-tuple-element.19.state_low.state_high.state_hbm, ...), custom_call_target="tpu_custom_call" | custom-call | tf_op jit(solution)/shard_map/edge_rows/pallas_call | solution.py:674
  25.4 1.0 %collective-permute-start.2 = (f32[11,3,8,128]{3,2,1,0:T(8,128)}, f32[11,3,8,128]{3,2,1,0:T(8,128)S(1)}, u32[]{:S(2)}, u32[]{:S(2)}) collective-permute-start(f32[11,3,8,128]{3,2,1,0:T(8,128)} %get-tuple-element.26), channel_id=1, source_target_pairs={{0,1},{1,0},{2,3},{3,2},{4,5},{5,4},{6,7},{7,6},{8,9},{9,8},{10,11... | collective-permute-start | bytes 405512 | tf_op jit(solution)/shard_map/ppermute | solution.py:695
  26.3 5.5 %collective-permute-start.3 = (f32[11,3,8,128]{3,2,1,0:T(8,128)}, f32[11,3,8,128]{3,2,1,0:T(8,128)S(1)}, u32[]{:S(2)}, u32[]{:S(2)}) collective-permute-start(f32[11,3,8,128]{3,2,1,0:T(8,128)} %get-tuple-element.27), channel_id=1, source_target_pairs={{1,2},{2,1},{3,4},{4,3},{5,6},{6,5},{7,127},{9,10},{10,9},{11,12},... | collective-permute-start | bytes 405512 | tf_op jit(solution)/shard_map/ppermute | solution.py:694
  31.9 3.9 %temps_high.1 = f32[40,128,256]{2,1,0:T(8,128)} custom-call(f32[40,128,256]{2,1,0:T(8,128)} %temps_hbm.5, f32[4,8,40,8,128]{4,3,2,1,0:T(8,128)} %get-tuple-element.17.result_hbm, s32[256,128]{1,0:T(8,128)} %get-tuple-element.18.place_hbm, f32[40,128,256]{2,1,0:T(8,128)} %temps_low.1.rest_0_), custom_call_target="tpu_custom_call", output_to_operand_aliasing={{}: (3, {})} | custom-call | flops 20000000 | bytes 6000000 | tf_op jit(solution)/shard_map/temps_high/pallas_call | solution.py:640
  35.7 0.0 collective-permute-done.2.even_hbm
  35.7 0.0 copy-start.2
  35.8 0.0 collective-permute-done.3.odd_hbm
  35.8 0.6 %copy-done.2 = f32[11,3,8,128]{3,2,1,0:T(8,128)} copy-done((f32[11,3,8,128]{3,2,1,0:T(8,128)}, f32[11,3,8,128]{3,2,1,0:T(8,128)S(1)}, u32[]{:S(2)}) %copy-start.2) | copy-done | bytes 135192
  36.4 0.0 copy-start.3
  36.4 0.7 %copy-done.3 = f32[11,3,8,128]{3,2,1,0:T(8,128)} copy-done((f32[11,3,8,128]{3,2,1,0:T(8,128)}, f32[11,3,8,128]{3,2,1,0:T(8,128)S(1)}, u32[]{:S(2)}) %copy-start.3) | copy-done | bytes 135192
  37.0 6.2 %motion.1 = (f32[2,128,256]{2,1,0:T(8,128)}, f32[3,128,256]{2,1,0:T(8,128)}) custom-call(f32[11,2,128,128]{3,2,1,0:T(8,128)} %get-tuple-element.19.state_low.state_high.state_hbm, f32[128,128]{1,0:T(8,128)} %copy-done, f32[128,128]{1,0:T(8,128)} %copy-done.1, f32[11,3,8,128]{3,2,1,0:T(8,128)} %copy-done.2, f32[11,3,8,128]{3,2,1,0:T(8,128)} %copy-done.3), custom_call_target="tpu_custom_call" | custom-call | tf_op jit(solution)/shard_map/motion/pallas_call | solution.py:699
Async XLA Ops:
  13.0 10.0 %collective-permute-start = (f32[128,128]{1,0:T(8,128)}, f32[128,128]{1,0:T(8,128)S(1)}, u32[]{:S(2)}, u32[]{:S(2)}) collective-permute-start(f32[128,128]{1,0:T(8,128)} %get-tuple-element.20), channel_id=1, source_target_pairs={{0,8},{8,16},{16,24},{24,32},{32,40},{40,48},{48,56},{56,64},{64,7... | collective-permute-start | bytes 196616 | tf_op jit(solution)/shard_map/ppermute | solution.py:661
  14.3 8.7 %collective-permute-start.1 = (f32[128,128]{1,0:T(8,128)}, f32[128,128]{1,0:T(8,128)S(1)}, u32[]{:S(2)}, u32[]{:S(2)}) collective-permute-start(f32[128,128]{1,0:T(8,128)} %get-tuple-element.21), channel_id=1, source_target_pairs={{8,0},{16,8},{24,16},{32,24},{40,32},{48,40},{56,48},{64,56},{72,6... | collective-permute-start | bytes 196616 | tf_op jit(solution)/shard_map/ppermute | solution.py:662
  23.0 0.6 %copy-start = (f32[128,128]{1,0:T(8,128)}, f32[128,128]{1,0:T(8,128)S(1)}, u32[]{:S(2)}) copy-start(f32[128,128]{1,0:T(8,128)S(1)} %collective-permute-done.west_low.west_high.west_hbm) | copy-start | bytes 196612
  23.0 0.6 %copy-start.1 = (f32[128,128]{1,0:T(8,128)}, f32[128,128]{1,0:T(8,128)S(1)}, u32[]{:S(2)}) copy-start(f32[128,128]{1,0:T(8,128)S(1)} %collective-permute-done.1.east_low.east_high.east_hbm) | copy-start | bytes 196612
  25.4 10.3 %collective-permute-start.2 = (f32[11,3,8,128]{3,2,1,0:T(8,128)}, f32[11,3,8,128]{3,2,1,0:T(8,128)S(1)}, u32[]{:S(2)}, u32[]{:S(2)}) collective-permute-start(f32[11,3,8,128]{3,2,1,0:T(8,128)} %get-tuple-element.26), channel_id=1, source_target_pairs={{0,1},{1,0},{2,3},{3,2},{4,5},{5,4},{6,7},{7,6},{8,9},{9,8},{10,11... | collective-permute-start | bytes 405512 | tf_op jit(solution)/shard_map/ppermute | solution.py:695
  26.3 9.4 %collective-permute-start.3 = (f32[11,3,8,128]{3,2,1,0:T(8,128)}, f32[11,3,8,128]{3,2,1,0:T(8,128)S(1)}, u32[]{:S(2)}, u32[]{:S(2)}) collective-permute-start(f32[11,3,8,128]{3,2,1,0:T(8,128)} %get-tuple-element.27), channel_id=1, source_target_pairs={{1,2},{2,1},{3,4},{4,3},{5,6},{6,5},{7,127},{9,10},{10,9},{11,12},... | collective-permute-start | bytes 405512 | tf_op jit(solution)/shard_map/ppermute | solution.py:694
  35.7 0.6 %copy-start.2 = (f32[11,3,8,128]{3,2,1,0:T(8,128)}, f32[11,3,8,128]{3,2,1,0:T(8,128)S(1)}, u32[]{:S(2)}) copy-start(f32[11,3,8,128]{3,2,1,0:T(8,128)S(1)} %collective-permute-done.2.even_hbm) | copy-start | bytes 405508
  36.4 0.7 %copy-start.3 = (f32[11,3,8,128]{3,2,1,0:T(8,128)}, f32[11,3,8,128]{3,2,1,0:T(8,128)S(1)}, u32[]{:S(2)}) copy-start(f32[11,3,8,128]{3,2,1,0:T(8,128)S(1)} %collective-permute-done.3.odd_hbm) | copy-start | bytes 405508

commit v6 on v4

--- a/solution.py
+++ b/solution.py
@@ -195,13 +195,15 @@
 
 
 def thermo_kernel(
-    list_ref, temps_hbm, thick_hbm, snow_hbm, area_hbm, air_hbm, heat_hbm,
+    list_hbm, temps_hbm, thick_hbm, snow_hbm, area_hbm, air_hbm, heat_hbm,
     vel_hbm, stress_hbm, wind_hbm, ocean_hbm, cells_hbm,
     thick_out, forcing_out, result_out, place_out, left_out, right_out,
-    kept_ref, fresh_ref, snow_ref, area_ref, single_ref, moving_ref, drive_ref, cells_ref, forcing_ref,
+    list_ref, kept_ref, fresh_ref, snow_ref, area_ref, single_ref, moving_ref, drive_ref, cells_ref, forcing_ref,
     mask_ref, base_ref, count_ref, inverse_ref, place_ref, spot_ref,
-    gathered_a, gathered_b, result_ref, in_sem, out_sem, result_sem, extra_sem,
+    gathered_a, gathered_b, result_ref, edge_ref, turn_ref, in_sem, out_sem, result_sem, edge_sem, extra_sem,
 ):
+    listing = pltpu.make_async_copy(list_hbm, list_ref, extra_sem)
+    listing.start()
     band = lax.axis_index("by")
     north = lax.axis_size("by") * ROWS
 
@@ -245,6 +247,10 @@
     for copies in fetched:
         for copy in copies:
             copy.start()
+    row = lax.broadcasted_iota(jnp.int32, (ROWS, LANES), 0) + band * ROWS
+    latitude = row.astype(jnp.float32) + 0.5
+    turn_ref[...] = 1.4 * jnp.sin(0.5 * jnp.pi * (2.0 * latitude / north - 1.0))
+    listing.wait()
     most = index_cells(list_ref, mask_ref, base_ref, count_ref, inverse_ref, place_ref, spot_ref)
     sent = [pltpu.make_async_copy(place_ref, place_out, result_sem.at[TILES // TEAM])]
     sent[0].start()
@@ -266,9 +272,8 @@
             area_total = area_total + area
         load = ice * load
         mass = 0.9 * load
-        row = lax.broadcasted_iota(jnp.int32, (HEIGHT, LANES), 0) + (turn % (TURNS // 2)) * HEIGHT + band * ROWS
-        latitude = row.astype(jnp.float32) + 0.5
-        turning = 1.4 * jnp.sin(0.5 * jnp.pi * (2.0 * latitude / north - 1.0)) * mass
+        inner = (turn % (TURNS // 2)) * HEIGHT
+        turning = turn_ref[inner : inner + HEIGHT, :] * mass
         diagonal = mass + 1.0
         scale = cells_ref[at, :].astype(jnp.float32) / (diagonal * diagonal + turning * turning)
         forcing_ref[0, at, :] = drive_ref[0, at, :] + drive_ref[2, at, :]
@@ -335,10 +340,11 @@
         for copy in sent:
             copy.start()
 
-    def pack(tile, carry):
-        group = lax.shift_right_logical(lane, 3)
-        for out_ref, half, push in ((left_out, 0, 0), (right_out, 1, 8)):
-            at = pl.ds(pl.multiple_of(tile * 8 + half * ROWS, 8), 8)
+    group = lax.shift_right_logical(lane, 3)
+    edges = []
+    for half, push, target in ((1, 8, right_out), (0, 0, left_out)):
+        for tile in range(ROWS // 8):
+            at = slice(8 * tile + half * ROWS, 8 * tile + half * ROWS + 8)
             packed = jnp.zeros((8, LANES), jnp.float32)
             for i in range(FIELDS):
                 ref, k = field_of(i, moving_ref, forcing_ref)
@@ -347,11 +353,11 @@
                 if turn:
                     x = pltpu.roll(x, turn, axis=1)
                 packed = jnp.where(group == i, x, packed)
-            out_ref[pl.ds(pl.multiple_of(tile * 8, 8), 8), :] = packed
-        return carry
-
-    lax.fori_loop(0, ROWS // 8, pack, 0, unroll=True)
-    for copy in sent:
+            edge_ref[half, 8 * tile : 8 * tile + 8, :] = packed
+        copy = pltpu.make_async_copy(edge_ref.at[half], target, edge_sem.at[half])
+        copy.start()
+        edges.append(copy)
+    for copy in sent + edges:
         copy.wait()
 
 
@@ -599,7 +605,6 @@
 ):
     f32 = jnp.float32
     i32 = jnp.int32
-    vmem = pl.BlockSpec(memory_space=pltpu.VMEM)
     here = pl.BlockSpec(memory_space=pl.ANY)
     listed = ice_cols.reshape(1, -1)
 
@@ -611,8 +616,8 @@
     thick_new, forcing, result, place, left, right = pl.pallas_call(
         thermo_kernel,
         name="thermo",
-        in_specs=[vmem] + [here] * 11,
-        out_specs=[here, here, here, here, vmem, vmem],
+        in_specs=[here] * 12,
+        out_specs=[here] * 6,
         out_shape=[
             jax.ShapeDtypeStruct((CATS, ROWS, COLS), f32),
             jax.ShapeDtypeStruct((6, ROWS, COLS), f32),
@@ -622,14 +627,18 @@
             jax.ShapeDtypeStruct((ROWS, LANES), f32),
         ],
         scratch_shapes=[
+            pltpu.VMEM(listed.shape, i32),
             flat(KEPT), flat(CATS), flat(CATS), flat(CATS), flat(2), flat(5), flat(4), one, flat(6),
             pltpu.VMEM((FLAT, LANES), f32), one, one, one, one, one,
             pltpu.VMEM((KEPT + CATS + 2, 8, LANES), f32),
             pltpu.VMEM((KEPT + CATS + 2, 8, LANES), f32),
             pltpu.VMEM((teams + 1, KEPT, 8, LANES), f32),
+            pltpu.VMEM((2, ROWS, LANES), f32),
+            pltpu.VMEM((ROWS, LANES), f32),
             pltpu.SemaphoreType.DMA((TURNS, 11)),
             pltpu.SemaphoreType.DMA((TURNS, 2)),
             pltpu.SemaphoreType.DMA((teams + 1,)),
+            pltpu.SemaphoreType.DMA((2,)),
             pltpu.SemaphoreType.DMA,
         ],
     )(

time: 40.9 us -> 40.3 us (0.985)
  Pallas kernels: 24.5 us -> 24 us
    pallas_call x1, Pallas kernels: 10.5 us -> 9.97 us  [per_device(): pl.pallas_call(thermo_kernel, name='thermo', in_specs=[here] * 12, out_sp...]
  transfers between devices with their start and end apart: 4 -> 4, of which waited for: 0 -> 0; matrix products, arithmetic and copies ran while one was open for 0% -> 0% of each run, Pallas kernels for 15% -> 16%
where the time goes in v6:
time: 40.3 us; the launch traced here: 40.1 us
  Pallas kernels  24 us (60%)
  starting transfers between devices  13.3 us (33%)
  local copies, waits for them, and re-layouts  1.91 us (5%)
  between operations  0.89 us (2%)
    pallas_call x1, Pallas kernels, per_device(): pl.pallas_call(thermo_kernel, name='thermo', in_specs=[here] * 12, out_sp...  9.97 us
    pallas_call x2, Pallas kernels, renew(): pl.pallas_call(functools.partial(temps_kernel, half), name='temps_west' i...  6.27 us
    ppermute x1, starting transfers between devices, per_device(): odd_halo = lax.ppermute(odd_rows, ('bx', 'by'), odd_pairs)  6.23 us
    pallas_call x1, Pallas kernels, per_device(): pl.pallas_call(motion_kernel, name='motion', in_specs=[here] * 7, out_spe...  6.04 us
    ppermute x1, starting transfers between devices, per_device(): east = lax.ppermute(left, 'bx', [((q + 1) % n_bx, q) for q in range(n_bx)])  4.82 us
    unnamed x8, local copies, waits for them, and re-layouts  1.91 us
    pallas_call x1, Pallas kernels, per_device(): pl.pallas_call(rows_kernel, name='edge_rows', grid=(1,), in_specs=[slab(2...  1.7 us
    ppermute x1, starting transfers between devices, per_device(): west = lax.ppermute(right, 'bx', [(q, (q + 1) % n_bx) for q in range(n_bx)])  1.28 us
  transfers between devices with their start and end apart: 4, of which 0 were waited for; matrix products, arithmetic and copies ran while one was open for 0% of the time, Pallas kernels for 16%

profile of v6, /device:TPU:25, one launch (start us, length us, event | category | flops | bytes accessed | tf_op | source)
XLA Modules:
  0.0 40.1 jit_solution(17284279239726815958)
XLA Ops:
  0.6 10.0 %thermo.1 = (f32[5,128,256]{2,1,0:T(8,128)}, f32[6,128,256]{2,1,0:T(8,128)}, f32[4,8,40,8,128]{4,3,2,1,0:T(8,128)}, s32[256,128]{1,0:T(8,128)}, f32[128,128]{1,0:T(8,128)}, /*index=5*/f32[128,128]{1,0:T(8,128)}) custom-call(s32[1,6144]{1,0:T(1,128)} %bitcast.1, f32[40,128,256]{2,1,0:T(8,128)} %temps_hbm.5, f32[5,128,256]{2,1,0:T(8,128)} %thick_hbm.1, ...), custom_call_target="tpu_custom_call" | custom-call | tf_op jit(solution)/shard_map/thermo/pallas_call | solution.py:616
  10.6 1.3 %collective-permute-start = (f32[128,128]{1,0:T(8,128)}, f32[128,128]{1,0:T(8,128)S(1)}, u32[]{:S(2)}, u32[]{:S(2)}) collective-permute-start(f32[128,128]{1,0:T(8,128)} %get-tuple-element.20), channel_id=1, source_target_pairs={{0,8},{8,16},{16,24},{24,32},{32,40},{40,48},{48,56},{56,64},{64,7... | collective-permute-start | bytes 196616 | tf_op jit(solution)/shard_map/ppermute | solution.py:671
  11.9 4.8 %collective-permute-start.1 = (f32[128,128]{1,0:T(8,128)}, f32[128,128]{1,0:T(8,128)S(1)}, u32[]{:S(2)}, u32[]{:S(2)}) collective-permute-start(f32[128,128]{1,0:T(8,128)} %get-tuple-element.21), channel_id=1, source_target_pairs={{8,0},{16,8},{24,16},{32,24},{40,32},{48,40},{56,48},{64,56},{72,6... | collective-permute-start | bytes 196616 | tf_op jit(solution)/shard_map/ppermute | solution.py:672
  16.7 3.1 %temps_west.1.rest_0_ = f32[40,128,256]{2,1,0:T(8,128)} custom-call(f32[40,128,256]{2,1,0:T(8,128)} %temps_hbm.5, f32[4,8,40,8,128]{4,3,2,1,0:T(8,128)} %get-tuple-element.17.result_hbm, s32[256,128]{1,0:T(8,128)} %get-tuple-element.18.place_hbm), custom_call_target="tpu_custom_call" | custom-call | flops 20000000 | bytes 6000000 | tf_op jit(solution)/shard_map/temps_west/pallas_call | solution.py:650
  19.9 0.0 collective-permute-done.west_low.west_high.west_hbm
  19.9 0.0 copy-start
  19.9 0.0 collective-permute-done.1.east_low.east_high.east_hbm
  19.9 0.0 copy-start.1
  19.9 0.6 %copy-done = f32[128,128]{1,0:T(8,128)} copy-done((f32[128,128]{1,0:T(8,128)}, f32[128,128]{1,0:T(8,128)S(1)}, u32[]{:S(2)}) %copy-start) | copy-done | bytes 65560
  20.5 0.0 copy-done.1
  20.5 1.7 %edge_rows.1 = (f32[11,3,8,128]{3,2,1,0:T(8,128)}, f32[11,3,8,128]{3,2,1,0:T(8,128)}) custom-call(f32[2,128,256]{2,1,0:T(8,128)} %vel_hbm.3, f32[3,128,256]{2,1,0:T(8,128)} %stress_hbm.3, f32[6,128,256]{2,1,0:T(8,128)} %get-tuple-element.19.forcing_low.forcing_high.forcing_hbm, f32[128,128]{1,0:T(8,128)} %copy-done, f32[128,128]{1,0:T(8,128)} %copy-done.1, ...), custom_call_target="tpu_custom_call" | custom-call | tf_op jit(solution)/shard_map/edge_rows/pallas_call | solution.py:684
  22.2 1.0 %collective-permute-start.2 = (f32[11,3,8,128]{3,2,1,0:T(8,128)}, f32[11,3,8,128]{3,2,1,0:T(8,128)S(1)}, u32[]{:S(2)}, u32[]{:S(2)}) collective-permute-start(f32[11,3,8,128]{3,2,1,0:T(8,128)} %get-tuple-element.26), channel_id=1, source_target_pairs={{0,1},{1,0},{2,3},{3,2},{4,5},{5,4},{6,7},{7,6},{8,9},{9,8},{10,11... | collective-permute-start | bytes 405512 | tf_op jit(solution)/shard_map/ppermute | solution.py:706
  23.2 6.2 %collective-permute-start.3 = (f32[11,3,8,128]{3,2,1,0:T(8,128)}, f32[11,3,8,128]{3,2,1,0:T(8,128)S(1)}, u32[]{:S(2)}, u32[]{:S(2)}) collective-permute-start(f32[11,3,8,128]{3,2,1,0:T(8,128)} %get-tuple-element.27), channel_id=1, source_target_pairs={{1,2},{2,1},{3,4},{4,3},{5,6},{6,5},{7,127},{9,10},{10,9},{11,12},... | collective-permute-start | bytes 405512 | tf_op jit(solution)/shard_map/ppermute | solution.py:705
  29.4 3.1 %temps_east.1 = f32[40,128,256]{2,1,0:T(8,128)} custom-call(f32[40,128,256]{2,1,0:T(8,128)} %temps_hbm.5, f32[4,8,40,8,128]{4,3,2,1,0:T(8,128)} %get-tuple-element.17.result_hbm, s32[256,128]{1,0:T(8,128)} %get-tuple-element.18.place_hbm, f32[40,128,256]{2,1,0:T(8,128)} %temps_west.1.rest_0_), custom_call_target="tpu_custom_call", output_to_operand_aliasing={{}: (3, {})} | custom-call | flops 20000000 | bytes 6000000 | tf_op jit(solution)/shard_map/temps_east/pallas_call | solution.py:650
  32.6 0.0 collective-permute-done.2.even_hbm
  32.6 0.0 copy-start.2
  32.6 0.0 collective-permute-done.3.odd_hbm
  32.6 0.6 %copy-done.2 = f32[11,3,8,128]{3,2,1,0:T(8,128)} copy-done((f32[11,3,8,128]{3,2,1,0:T(8,128)}, f32[11,3,8,128]{3,2,1,0:T(8,128)S(1)}, u32[]{:S(2)}) %copy-start.2) | copy-done | bytes 135192
  33.2 0.0 copy-start.3
  33.2 0.7 %copy-done.3 = f32[11,3,8,128]{3,2,1,0:T(8,128)} copy-done((f32[11,3,8,128]{3,2,1,0:T(8,128)}, f32[11,3,8,128]{3,2,1,0:T(8,128)S(1)}, u32[]{:S(2)}) %copy-start.3) | copy-done | bytes 135192
  33.9 6.0 %motion.1 = (f32[2,128,256]{2,1,0:T(8,128)}, f32[3,128,256]{2,1,0:T(8,128)}) custom-call(f32[2,128,256]{2,1,0:T(8,128)} %vel_hbm.3, f32[3,128,256]{2,1,0:T(8,128)} %stress_hbm.3, f32[6,128,256]{2,1,0:T(8,128)} %get-tuple-element.19.forcing_low.forcing_high.forcing_hbm, f32[128,128]{1,0:T(8,128)} %copy-done, f32[128,128]{1,0:T(8,128)} %copy-done.1, ...), custom_call_target="tpu_custom_call" | custom-call | tf_op jit(solution)/shard_map/motion/pallas_call | solution.py:710
Async XLA Ops:
  10.6 9.2 %collective-permute-start = (f32[128,128]{1,0:T(8,128)}, f32[128,128]{1,0:T(8,128)S(1)}, u32[]{:S(2)}, u32[]{:S(2)}) collective-permute-start(f32[128,128]{1,0:T(8,128)} %get-tuple-element.20), channel_id=1, source_target_pairs={{0,8},{8,16},{16,24},{24,32},{32,40},{40,48},{48,56},{56,64},{64,7... | collective-permute-start | bytes 196616 | tf_op jit(solution)/shard_map/ppermute | solution.py:671
  11.9 8.0 %collective-permute-start.1 = (f32[128,128]{1,0:T(8,128)}, f32[128,128]{1,0:T(8,128)S(1)}, u32[]{:S(2)}, u32[]{:S(2)}) collective-permute-start(f32[128,128]{1,0:T(8,128)} %get-tuple-element.21), channel_id=1, source_target_pairs={{8,0},{16,8},{24,16},{32,24},{40,32},{48,40},{56,48},{64,56},{72,6... | collective-permute-start | bytes 196616 | tf_op jit(solution)/shard_map/ppermute | solution.py:672
  19.9 0.6 %copy-start = (f32[128,128]{1,0:T(8,128)}, f32[128,128]{1,0:T(8,128)S(1)}, u32[]{:S(2)}) copy-start(f32[128,128]{1,0:T(8,128)S(1)} %collective-permute-done.west_low.west_high.west_hbm) | copy-start | bytes 196612
  19.9 0.6 %copy-start.1 = (f32[128,128]{1,0:T(8,128)}, f32[128,128]{1,0:T(8,128)S(1)}, u32[]{:S(2)}) copy-start(f32[128,128]{1,0:T(8,128)S(1)} %collective-permute-done.1.east_low.east_high.east_hbm) | copy-start | bytes 196612
  22.2 10.3 %collective-permute-start.2 = (f32[11,3,8,128]{3,2,1,0:T(8,128)}, f32[11,3,8,128]{3,2,1,0:T(8,128)S(1)}, u32[]{:S(2)}, u32[]{:S(2)}) collective-permute-start(f32[11,3,8,128]{3,2,1,0:T(8,128)} %get-tuple-element.26), channel_id=1, source_target_pairs={{0,1},{1,0},{2,3},{3,2},{4,5},{5,4},{6,7},{7,6},{8,9},{9,8},{10,11... | collective-permute-start | bytes 405512 | tf_op jit(solution)/shard_map/ppermute | solution.py:706
  23.2 9.4 %collective-permute-start.3 = (f32[11,3,8,128]{3,2,1,0:T(8,128)}, f32[11,3,8,128]{3,2,1,0:T(8,128)S(1)}, u32[]{:S(2)}, u32[]{:S(2)}) collective-permute-start(f32[11,3,8,128]{3,2,1,0:T(8,128)} %get-tuple-element.27), channel_id=1, source_target_pairs={{1,2},{2,1},{3,4},{4,3},{5,6},{6,5},{7,127},{9,10},{10,9},{11,12},... | collective-permute-start | bytes 405512 | tf_op jit(solution)/shard_map/ppermute | solution.py:705
  32.6 0.6 %copy-start.2 = (f32[11,3,8,128]{3,2,1,0:T(8,128)}, f32[11,3,8,128]{3,2,1,0:T(8,128)S(1)}, u32[]{:S(2)}) copy-start(f32[11,3,8,128]{3,2,1,0:T(8,128)S(1)} %collective-permute-done.2.even_hbm) | copy-start | bytes 405508
  33.2 0.7 %copy-start.3 = (f32[11,3,8,128]{3,2,1,0:T(8,128)}, f32[11,3,8,128]{3,2,1,0:T(8,128)S(1)}, u32[]{:S(2)}) copy-start(f32[11,3,8,128]{3,2,1,0:T(8,128)S(1)} %collective-permute-done.3.odd_hbm) | copy-start | bytes 405508
